TPU v7x, 32 devices: a whole 2x2x4 slice. The times are simulated.
32 devices in a mesh: dp: 8 (over z, core), tensor: 4 (over y, x).
Axes of the slice: x: 2, y: 2, z: 4, core: 2. Of those that a mesh axis runs over, the one named last changes fastest.
Arguments:
- tokens: bfloat16 [8192, 2048], P('dp'), may hold values from -6 to 6
- lengths: int32 [8], P('dp'), may hold values from 256 to 1024, as said below
- norm1_gain: bfloat16 [2048], replicated, may hold values from 0.5 to 1.5
- norm1_shift: bfloat16 [2048], replicated, may hold values from -4 to 4
- query_weight: bfloat16 [2048, 2048], P(None, 'tensor'), may hold values from -0.1875 to 0.1875
- query_bias: bfloat16 [2048], P('tensor'), may hold values from -6 to 6
- keyval_weight: bfloat16 [2048, 256], replicated, may hold values from -0.1875 to 0.1875
- value_bias: bfloat16 [128], replicated, may hold values from -6 to 6
- proj_weight: bfloat16 [2048, 2048], P('tensor'), may hold values from -0.5 to 0.5
- proj_bias: bfloat16 [2048], replicated, may hold values from -4 to 4
- norm2_gain: bfloat16 [2048], replicated, may hold values from 0.5 to 1.5
- norm2_shift: bfloat16 [2048], replicated, may hold values from -4 to 4
- up_weight: bfloat16 [2048, 8192], P(None, 'tensor'), may hold values from -0.125 to 0.125
- up_bias: bfloat16 [8192], P('tensor'), may hold values from -6 to 6
- down_weight: bfloat16 [8192, 2048], P('tensor'), may hold values from -0.0625 to 0.0625
- down_bias: bfloat16 [2048], replicated, may hold values from -4 to 4
- cotangent: bfloat16 [8192, 2048], P('dp'), may hold values from -6 to 6
Outputs:
- result: bfloat16 [8192, 2048], P('dp')
- grad_tokens: bfloat16 [8192, 2048], P('dp')
- grad_gain1: float32 [2048], replicated
- grad_shift1: float32 [2048], replicated
- grad_query: float32 [2048, 2048], P(None, 'tensor')
- grad_qbias: float32 [2048], P('tensor')
- grad_keyval: float32 [2048, 256], replicated
- grad_vbias: float32 [128], replicated
- grad_proj: float32 [2048, 2048], P('tensor')
- grad_pbias: float32 [2048], replicated
- grad_gain2: float32 [2048], replicated
- grad_shift2: float32 [2048], replicated
- grad_up: float32 [2048, 8192], P(None, 'tensor')
- grad_upbias: float32 [8192], P('tensor')
- grad_down: float32 [8192, 2048], P('tensor')
- grad_dnbias: float32 [2048], replicated
Inputs may be any that keep to these rules, and one draw needn't show every extreme that they name: `lengths`: valid tokens at the start of each slot; some slot is full (1024) and some holds 256.
All inputs are finite; a program needn't handle non-finite values.
Results may differ from a plain program's by a relative error of at most 0.023.
Values may be sent and summed in bfloat16 or wider, within the bound.
A program may use at most 256 MiB of HBM per device.

v0:
```python
import jax
import jax.numpy as jnp
from jax import lax
from jax.sharding import PartitionSpec as P


def layer_norm(values, gain, shift):
    center = values - jnp.mean(values, axis=-1, keepdims=True)
    scaled = center * lax.rsqrt(jnp.mean(center * center, axis=-1, keepdims=True) + 1e-05)
    return scaled * gain + shift


def gelu_tanh(values):
    return (
        0.5
        * values
        * (1.0 + jnp.tanh(0.7978845608028654 * (values + 0.044715 * values * values * values)))
    )


def contract_rows(left, right):
    return lax.dot_general(
        left, right, (((0,), (0,)), ((), ())), preferred_element_type=jnp.float32
    )


def contract_cols(left, right):
    return lax.dot_general(
        left, right, (((1,), (1,)), ((), ())), preferred_element_type=jnp.float32
    )


def block_scores(query_block, key_rows, offset, length):
    scale = query_block.shape[2] ** (-0.5)
    scores = (
        jnp.einsum("qhd,kd->hqk", query_block, key_rows, preferred_element_type=jnp.float32) * scale
    )
    rows_pos = offset + jnp.arange(query_block.shape[0], dtype=jnp.int32)
    keys_pos = jnp.arange(key_rows.shape[0], dtype=jnp.int32)
    allowed = (keys_pos[None, :] <= rows_pos[:, None]) & (keys_pos[None, :] < length)
    return jnp.where(allowed[None], scores, -1e30)


def attend_forward(queries, key_rows, value_rows, length, block_rows):
    pieces = []
    log_totals = []
    for offset in range(0, queries.shape[0], block_rows):
        query_block = queries[offset : offset + block_rows]
        scores = block_scores(query_block, key_rows, offset, length)
        highest = jnp.max(scores, axis=-1, keepdims=True)
        exponent = jnp.exp(scores - highest)
        normaliser = jnp.sum(exponent, axis=-1, keepdims=True)
        probability = (exponent / normaliser).astype(jnp.bfloat16)
        log_totals.append(highest + jnp.log(normaliser))
        pieces.append(
            jnp.einsum("hqk,kd->qhd", probability, value_rows, preferred_element_type=jnp.float32)
        )
    return (jnp.concatenate(pieces, axis=0), log_totals)


def attend_backward(queries, key_rows, value_rows, length, block_rows, log_totals, grad_heads):
    scale = queries.shape[2] ** (-0.5)
    query_grads = []
    key_grads = jnp.zeros(key_rows.shape, jnp.float32)
    value_grads = jnp.zeros(value_rows.shape, jnp.float32)
    for counter, offset in enumerate(range(0, queries.shape[0], block_rows)):
        query_block = queries[offset : offset + block_rows]
        grad_block = grad_heads[offset : offset + block_rows]
        scores = block_scores(query_block, key_rows, offset, length)
        probability = jnp.exp(scores - log_totals[counter])
        grad_probs = jnp.einsum(
            "qhd,kd->hqk", grad_block, value_rows, preferred_element_type=jnp.float32
        )
        inner = jnp.sum(probability * grad_probs, axis=-1, keepdims=True)
        grad_scores = (probability * (grad_probs - inner)).astype(jnp.bfloat16)
        query_grads.append(
            (
                jnp.einsum("hqk,kd->qhd", grad_scores, key_rows, preferred_element_type=jnp.float32)
                * scale
            ).astype(jnp.bfloat16)
        )
        key_grads = (
            key_grads
            + jnp.einsum(
                "hqk,qhd->kd", grad_scores, query_block, preferred_element_type=jnp.float32
            )
            * scale
        )
        value_grads = value_grads + jnp.einsum(
            "hqk,qhd->kd",
            probability.astype(jnp.bfloat16),
            grad_block,
            preferred_element_type=jnp.float32,
        )
    return (jnp.concatenate(query_grads, axis=0), key_grads, value_grads)


def local(
    tokens,
    lengths,
    norm1_gain,
    norm1_shift,
    query_weight,
    query_bias,
    keyval_weight,
    value_bias,
    proj_weight,
    proj_bias,
    norm2_gain,
    norm2_shift,
    up_weight,
    up_bias,
    down_weight,
    down_bias,
    cotangent,
):
    total_rows = tokens.shape[0]
    slot_count = lengths.shape[0]
    slot_len = total_rows // slot_count
    head_dim = keyval_weight.shape[1] // 2
    heads_here = query_weight.shape[1] // head_dim
    block_rows = min(512, slot_len)
    tokens_wide = tokens.astype(jnp.float32)
    gain1 = norm1_gain.astype(jnp.float32)
    shift1 = norm1_shift.astype(jnp.float32)
    gain2 = norm2_gain.astype(jnp.float32)
    shift2 = norm2_shift.astype(jnp.float32)
    normed1, undo_norm1 = jax.vjp(layer_norm, tokens_wide, gain1, shift1)
    hidden1 = normed1.astype(jnp.bfloat16)
    queries = (
        jnp.dot(hidden1, query_weight, preferred_element_type=jnp.float32)
        + query_bias.astype(jnp.float32)
    ).astype(jnp.bfloat16)
    keyval = jnp.dot(hidden1, keyval_weight, preferred_element_type=jnp.float32)
    key_rows = keyval[:, :head_dim].astype(jnp.bfloat16)
    value_rows = (keyval[:, head_dim:] + value_bias.astype(jnp.float32)).astype(jnp.bfloat16)
    number = 0
    slot_queries = queries.reshape(slot_len, heads_here, head_dim)
    attended, log_totals = attend_forward(
        slot_queries, key_rows, value_rows, lengths[number], block_rows
    )
    saved_totals = [log_totals]
    heads_out = attended.reshape(total_rows, heads_here * head_dim).astype(jnp.bfloat16)
    attn_terms = jnp.dot(heads_out, proj_weight, preferred_element_type=jnp.float32)
    middle = (
        tokens_wide
        + lax.psum(attn_terms.astype(jnp.bfloat16), "tensor").astype(jnp.float32)
        + proj_bias.astype(jnp.float32)
    )
    normed2, undo_norm2 = jax.vjp(layer_norm, middle, gain2, shift2)
    hidden2 = normed2.astype(jnp.bfloat16)
    pre_act = jnp.dot(hidden2, up_weight, preferred_element_type=jnp.float32) + up_bias.astype(
        jnp.float32
    )
    activated = gelu_tanh(pre_act).astype(jnp.bfloat16)
    mlp_terms = jnp.dot(activated, down_weight, preferred_element_type=jnp.float32)
    result = (
        middle
        + lax.psum(mlp_terms.astype(jnp.bfloat16), "tensor").astype(jnp.float32)
        + down_bias.astype(jnp.float32)
    ).astype(jnp.bfloat16)
    positions = jnp.arange(slot_len, dtype=jnp.int32)
    valid = (positions[None, :] < lengths[:, None]).astype(jnp.float32).reshape(total_rows, 1)
    grad_result = cotangent.astype(jnp.float32) * valid
    grad_dnbias = jnp.sum(grad_result, axis=0)
    result_low = grad_result.astype(jnp.bfloat16)
    grad_down = contract_rows(activated, result_low)
    grad_act = contract_cols(result_low, down_weight).astype(jnp.bfloat16)
    gelu_pull = jax.vjp(gelu_tanh, pre_act)[1]
    grad_pre = gelu_pull(grad_act.astype(jnp.float32))[0].astype(jnp.bfloat16)
    grad_upbias = jnp.sum(grad_pre.astype(jnp.float32), axis=0)
    grad_up = contract_rows(hidden2, grad_pre)
    back_terms2 = contract_cols(grad_pre, up_weight)
    mid_from_norm, grad_gain2, grad_shift2 = undo_norm2(
        lax.psum(back_terms2.astype(jnp.bfloat16), "tensor").astype(jnp.float32)
    )
    grad_middle = grad_result + mid_from_norm
    middle_low = grad_middle.astype(jnp.bfloat16)
    grad_pbias = jnp.sum(grad_middle, axis=0)
    grad_proj = contract_rows(heads_out, middle_low)
    grad_heads = contract_cols(middle_low, proj_weight).astype(jnp.bfloat16)
    number = 0
    slot_queries = queries.reshape(slot_len, heads_here, head_dim)
    slot_grads = grad_heads.reshape(slot_len, heads_here, head_dim)
    query_part, key_part, value_part = attend_backward(
        slot_queries,
        key_rows,
        value_rows,
        lengths[number],
        block_rows,
        saved_totals[number],
        slot_grads,
    )
    grad_queries = query_part.reshape(total_rows, heads_here * head_dim)
    grad_kv_rows = jnp.concatenate([key_part, value_part], axis=1).astype(jnp.bfloat16)
    grad_qbias = jnp.sum(grad_queries.astype(jnp.float32), axis=0)
    grad_query = contract_rows(hidden1, grad_queries)
    grad_keyval = contract_rows(hidden1, grad_kv_rows)
    grad_vbias = jnp.sum(grad_kv_rows[:, head_dim:].astype(jnp.float32), axis=0)
    back_terms1 = contract_cols(grad_queries, query_weight) + contract_cols(
        grad_kv_rows, keyval_weight
    )
    tokens_from_norm, grad_gain1, grad_shift1 = undo_norm1(
        lax.psum(back_terms1.astype(jnp.bfloat16), "tensor").astype(jnp.float32)
    )
    grad_tokens = (grad_middle + tokens_from_norm).astype(jnp.bfloat16)
    grad_keyval, grad_vbias = lax.psum((grad_keyval, grad_vbias), ("dp", "tensor"))
    (
        grad_query,
        grad_qbias,
        grad_proj,
        grad_pbias,
        grad_gain1,
        grad_shift1,
        grad_gain2,
        grad_shift2,
        grad_up,
        grad_upbias,
        grad_down,
        grad_dnbias,
    ) = (
        lax.psum(grad_query.astype(jnp.bfloat16), "dp").astype(jnp.float32),
        lax.psum(grad_qbias.astype(jnp.bfloat16), "dp").astype(jnp.float32),
        lax.psum(grad_proj.astype(jnp.bfloat16), "dp").astype(jnp.float32),
        lax.psum(grad_pbias.astype(jnp.bfloat16), "dp").astype(jnp.float32),
        lax.psum(grad_gain1.astype(jnp.bfloat16), "dp").astype(jnp.float32),
        lax.psum(grad_shift1.astype(jnp.bfloat16), "dp").astype(jnp.float32),
        lax.psum(grad_gain2.astype(jnp.bfloat16), "dp").astype(jnp.float32),
        lax.psum(grad_shift2.astype(jnp.bfloat16), "dp").astype(jnp.float32),
        lax.psum(grad_up.astype(jnp.bfloat16), "dp").astype(jnp.float32),
        lax.psum(grad_upbias.astype(jnp.bfloat16), "dp").astype(jnp.float32),
        lax.psum(grad_down.astype(jnp.bfloat16), "dp").astype(jnp.float32),
        lax.psum(grad_dnbias.astype(jnp.bfloat16), "dp").astype(jnp.float32),
    )
    return (
        result,
        grad_tokens,
        grad_gain1,
        grad_shift1,
        grad_query,
        grad_qbias,
        grad_keyval,
        grad_vbias,
        grad_proj,
        grad_pbias,
        grad_gain2,
        grad_shift2,
        grad_up,
        grad_upbias,
        grad_down,
        grad_dnbias,
    )


def solution(mesh):
    in_specs = (
        P("dp", None),
        P("dp"),
        P(),
        P(),
        P(None, "tensor"),
        P("tensor"),
        P(),
        P(),
        P("tensor", None),
        P(),
        P(),
        P(),
        P(None, "tensor"),
        P("tensor"),
        P("tensor", None),
        P(),
        P("dp", None),
    )
    out_specs = (
        P("dp", None),
        P("dp", None),
        P(),
        P(),
        P(None, "tensor"),
        P("tensor"),
        P(),
        P(),
        P("tensor", None),
        P(),
        P(),
        P(),
        P(None, "tensor"),
        P("tensor"),
        P("tensor", None),
        P(),
    )
    return jax.shard_map(local, mesh=mesh, in_specs=in_specs, out_specs=out_specs, check_vma=False)
```

profile of v0, /device:TPU:0, one launch (start us, length us, event | category | flops | bytes accessed | tf_op | source)
XLA Modules:
  0.0 1095.1 jit_solution(10420720279538975203)
XLA Ops:
  10.0 3.0 convert_reduce_fusion
  12.9 3.4 fusion.20
  17.6 2.0 fusion.9
  19.6 2.5 add_convert_fusion.4
  26.9 1.7 fusion.71
  31.8 2.1 fusion.70
  35.0 4.4 convolution_convert_fusion.4
  39.6 106.3 %all-reduce.9.cloned.1.call-done = bf16[1024,2048]{1,0:T(8,128)(2,1)} async-done(((bf16[1024,2048]{1,0:T(8,128)(2,1)}), bf16[1024,2048]{1,0:T(8,128)(2,1)}) %all-reduce.9.cloned.1.call-update) | async-done | bytes 4194320 | tf_op jit(solution)/shard_map/psum | solution.py:147
  146.0 5.0 fusion.38
  151.9 2.4 multiply_reduce_fusion
  154.3 13.9 %fusion.91 = f32[1024,2048]{1,0:T(8,128)} fusion(bf16[2048,2048]{1,0:T(8,128)(2,1)} %param.29, f32[2048]{0:T(1024)S(1)} %convert_element_type.225, f32[2048]{0:T(1024)S(1)} %convert_element_type.224, f32[1024]{0:T(1024)S(1)} %fusion.86, bf16[1024,2048]{1,0:T(8,128)(2,1)S(1)} %copy-done.7, bf16[1024,2048]{1,0:T(8,128)(2,1)S(1)} %copy-done.3, ...), kind=kOutput, calls=%fused_computation.145 | convolution fusion | flops 8608808960 | bytes 25198592 | tf_op jit(solution)/shard_map/dot_general | solution.py:152
  168.2 19.2 %fusion.101 = (bf16[2048]{0:T(1024)(128)(2,1)}, bf16[1024,2048]{1,0:T(8,128)(2,1)S(1)}) fusion(bf16[2048,2048]{1,0:T(8,128)(2,1)} %param.31, bf16[1024,2048]{1,0:T(8,128)(2,1)S(1)} %copy-done.15, f32[1024]{0:T(1024)S(1)} %fusion.87, f32[1024,2048]{1,0:T(8,128)} %fusion.91, f32[2048]{0:T(1024)S(1)} %convert_element_type.227), kind=kOutput, calls=%fused_computation.153 | convolution fusion | flops 8654944256 | bytes 25182208 | tf_op jit(solution)/shard_map/dot_general | solution.py:28
  187.4 2.0 copy-done.45
  189.4 12.7 %convolution_convert_fusion.2 = bf16[1024,2048]{1,0:T(8,128)(2,1)} fusion(bf16[1024,2048]{1,0:T(8,128)(2,1)S(1)} %get-tuple-element.58, bf16[2048,2048]{1,0:T(8,128)(2,1)} %param.29), kind=kOutput, calls=%fused_computation.83 | convolution fusion | flops 8592031744 | bytes 16777216 | tf_op jit(solution)/shard_map/dot_general | solution.py:28
  202.3 15.9 %convolution_convert_fusion.3 = bf16[1024,2048]{1,0:T(8,128)(2,1)} fusion(bf16[2048,2048]{1,0:T(8,128)(2,1)} %param.31, f32[1024,2048]{1,0:T(8,128)} %fusion.91, f32[2048]{0:T(1024)S(1)} %convert_element_type.227), kind=kOutput, calls=%fused_computation.84 | convolution fusion | flops 8613003264 | bytes 20979712 | tf_op jit(solution)/shard_map/dot_general | solution.py:156
  218.2 87.8 %all-reduce.11.cloned.1.call-done = bf16[1024,2048]{1,0:T(8,128)(2,1)} async-done(((bf16[1024,2048]{1,0:T(8,128)(2,1)}), bf16[1024,2048]{1,0:T(8,128)(2,1)}) %all-reduce.11.cloned.1.call-update) | async-done | bytes 4194320 | tf_op jit(solution)/shard_map/psum | solution.py:175
  306.0 7.0 fusion.10
  314.3 5.5 fusion.16
  319.8 5.9 fusion.94
  325.8 2.4 fusion.55
  329.3 2.4 fusion.25
  331.7 2.5 fusion.27
  334.1 3.3 convolution_bitcast_fusion
  340.5 1.9 fusion.28
  342.5 1.6 convert_reduce_fusion.1
  344.1 2.4 fusion.30
  349.1 2.4 fusion.107
  351.5 3.4 add_convert_fusion.1
  355.0 15.7 %convolution_convert_fusion.1 = bf16[2048,2048]{1,0:T(8,128)(2,1)} fusion(bf16[1024,2048]{1,0:T(8,128)(2,1)} %copy-done.45, f32[2048]{0:T(1024)S(1)} %convert_element_type.225, f32[2048]{0:T(1024)S(1)} %convert_element_type.224, f32[1024]{0:T(1024)S(1)} %fusion.86, bf16[1024,2048]{1,0:T(8,128)(2,1)} %all-reduce.9.cloned.1.call-done, ...), kind=kOutput, calls=%fused_computation.69 | convolution fusion | flops 8613003264 | bytes 21004288 | tf_op jit(solution)/shard_map/dot_general | solution.py:22
  370.7 19.9 %convolution_convert_fusion = bf16[2048,2048]{1,0:T(8,128)(2,1)} fusion(bf16[1024,2048]{1,0:T(8,128)(2,1)S(1)} %copy-done.17, f32[1024]{0:T(1024)S(1)} %fusion.87, f32[1024,2048]{1,0:T(8,128)} %fusion.91, f32[2048]{0:T(1024)S(1)} %convert_element_type.227), kind=kOutput, calls=%fused_computation.68 | convolution fusion | flops 8621391872 | bytes 20983808 | tf_op jit(solution)/shard_map/dot_general | solution.py:22
  390.7 3.8 convolution_convert_fusion.6
  394.5 3.7 convolution_convert_fusion.5
  398.9 40.0 %psum.135 = f32[128]{0:T(128)} all-reduce(f32[128]{0:T(128)S(1)} %get-tuple-element.59), channel_id=1, replica_groups=mesh['dp'=8,'tensor'=4] {'dp','tensor'}, use_global_device_ids=true, to_apply=%region_28.29 | all-reduce | flops 128 | bytes 1024 | tf_op jit(solution)/shard_map/psum | solution.py:207
  438.9 4.9 fusion.82
  443.9 2.8 reduce_sum.266
  446.7 81.6 %all-reduce.17.cloned.1.call-done = (bf16[1024,2048]{1,0:T(8,128)(2,1)}, bf16[1024,2048]{1,0:T(8,128)(2,1)}) async-done(((bf16[1024,2048]{1,0:T(8,128)(2,1)}, bf16[1024,2048]{1,0:T(8,128)(2,1)}), (bf16[1024,2048]{1,0:T(8,128)(2,1)}, bf16[1024,2048]{1,0:T(8,128)(2,1)})) %all-reduce.17.cloned.1.call-update) | async-done | bytes 8388624 | tf_op jit(solution)/shard_map/psum | solution.py:159
  528.3 4.5 fusion.21
  532.8 2.8 reduce_sum.258
  535.7 6.3 fusion.17
  542.0 30.6 %all-reduce = (bf16[2048]{0:T(1024)(128)(2,1)S(1)}, bf16[2048]{0:T(1024)(128)(2,1)S(1)}, bf16[512]{0:T(512)(128)(2,1)S(1)}, bf16[2048]{0:T(1024)(128)(2,1)S(1)},...) all-reduce(bf16[2048]{0:T(1024)(128)(2,1)S(1)} %get-tuple-element.1, ...), channel_id=1, replica_groups=mesh['dp'=8,'tensor'=4] {'dp'}, use_global_device_ids=true, to_apply=%region_19.20 | all-reduce | flops 14848 | bytes 59392 | tf_op jit(solution)/shard_map/psum | solution.py:226
  577.3 13.3 %add_convert_fusion = (bf16[1024,2048]{1,0:T(8,128)(2,1)}, bf16[1024,2048]{1,0:T(8,128)(2,1)}) fusion(f32[1024,2048]{1,0:T(8,128)} %copy-done.10, bf16[1024,2048]{1,0:T(8,128)(2,1)} %param.17, bf16[1024,2048]{1,0:T(8,128)(2,1)} %get-tuple-element.33, f32[1024]{0:T(1024)S(1)} %negate_multiply_fusion, f32[1024]{0:T(1024)S(1)} %multiply_multiply_fusion.2, ...), kind=kLoop, calls=%fused_computation.52 | loop fusion | flops 37748736 | bytes 33595392 | tf_op jit(solution)/shard_map/convert_element_type | solution.py:206
  590.7 354.6 %all-reduce.15.cloned.1.call-done = (bf16[2048,512]{1,0:T(8,128)(2,1)}, bf16[512,2048]{1,0:T(8,128)(2,1)}, bf16[2048,2048]{1,0:T(8,128)(2,1)}, bf16[2048,2048]{1,0:T(8,128)(2,1)}) async-done(((bf16[2048,512]{1,0:T(8,128)(2,1)}, bf16[512,2048]{1,0:T(8,128)(2,1)}, bf16[2048,2048]{1,0:T(8,128)(2,1)}, bf16[2048,2048]{1,0:T(8,128)(2,1)}), (bf16[2048,512]{1,0:T(8,128)(2,1)}, bf16[512,2048]{1,0:T(8,128)(2,1)}, ...) | async-done | bytes 20971536 | tf_op jit(solution)/shard_map/psum | solution.py:222
  945.3 4.2 convert_element_type.258
  949.5 4.1 convert_element_type.262
  953.6 11.9 %convert_element_type.269 = f32[2048,2048]{1,0:T(8,128)} convert(bf16[2048,2048]{1,0:T(8,128)(2,1)} %get-tuple-element.30) | non-fusion elementwise | flops 4194304 | bytes 25165824 | tf_op jit(solution)/shard_map/convert_element_type | solution.py:230
  965.6 11.9 %convert_element_type.272 = f32[2048,2048]{1,0:T(8,128)} convert(bf16[2048,2048]{1,0:T(8,128)(2,1)} %get-tuple-element.31) | non-fusion elementwise | flops 4194304 | bytes 25165824 | tf_op jit(solution)/shard_map/convert_element_type | solution.py:232
  977.5 107.8 %all-reduce.13.cloned.1.call-done = f32[2048,256]{1,0:T(8,128)} async-done(((f32[2048,256]{1,0:T(8,128)}), f32[2048,256]{1,0:T(8,128)}) %all-reduce.13.cloned.1.call-update) | async-done | bytes 2097168 | tf_op jit(solution)/shard_map/psum | solution.py:207
  1085.3 3.0 copy.85
  (162 shorter events, 26.6 us)
Async XLA Ops:
  7.2 27.9 %copy-start = (bf16[512,2048]{1,0:T(8,128)(2,1)S(1)}, bf16[512,2048]{1,0:T(8,128)(2,1)}, u32[]{:S(2)}) copy-start(bf16[512,2048]{1,0:T(8,128)(2,1)} %param.25) | copy-start | bytes 6291460
  7.2 9.8 copy-start.35
  7.2 9.8 copy-start.36
  7.2 138.7 %all-reduce.9.cloned.1.call-start = ((), (), s32[]{:S(2)}) async-start(), calls=%async_computation | async-start | bytes 8388608 | tf_op jit(solution)/shard_map/psum | solution.py:147
  7.3 10.3 copy-start.2
  10.0 9.6 copy-start.43
  12.9 4.1 copy-start.29
  19.6 2.6 copy-start.18
  19.6 2.6 copy-start.22
  22.2 3.5 copy-start.20
  22.2 6.8 copy-start.13
  23.5 5.5 copy-start.11
  25.7 3.3 copy-start.5
  30.6 3.3 copy-start.6
  34.0 5.5 copy-start.37
  34.1 5.5 copy-start.38
  34.1 5.5 copy-start.39
  34.1 5.5 copy-start.40
  39.5 266.5 %all-reduce.11.cloned.1.call-start = ((), (), s32[]{:S(2)}) async-start(), calls=%async_computation.1 | async-start | bytes 8388608 | tf_op jit(solution)/shard_map/psum | solution.py:175
  146.0 5.0 copy-start.3
  146.0 5.9 copy-start.7
  154.3 13.9 %copy-start.15 = (bf16[1024,2048]{1,0:T(8,128)(2,1)S(1)}, bf16[1024,2048]{1,0:T(8,128)(2,1)}, u32[]{:S(2)}) copy-start(bf16[1024,2048]{1,0:T(8,128)(2,1)} %param.33) | copy-start | bytes 12582916
  202.2 326.1 %all-reduce.17.cloned.1.call-start = ((), (), s32[]{:S(2)}) async-start(), calls=%async_computation.4 | async-start | bytes 16777216 | tf_op jit(solution)/shard_map/psum | solution.py:159
  306.0 7.1 copy-start.4
  306.0 7.1 copy-start.8
  306.0 8.3 copy-start.9
  313.0 6.8 copy-start.16
  314.3 14.9 %slice-start = ((s8[8388608]{0:T(1024)(128)(4,1)}), s8[4194304]{0:T(1024)(128)(4,1)S(1)}, s32[]{:S(2)}) async-start(s8[8388608]{0:T(1024)(128)(4,1)} %bitcast.107), calls=%async_computation.5 | async-start | bytes 8388608
  319.8 9.4 slice-start.1
  325.7 3.4 copy-start.10
  329.3 9.7 slice-start.2
  331.6 5.8 copy-start.12
  331.6 7.3 slice-start.3
  344.1 3.3 copy-start.14
  344.1 3.3 copy-start.26
  354.9 590.4 %all-reduce.15.cloned.1.call-start = ((), (), s32[]{:S(2)}) async-start(), calls=%async_computation.3 | async-start | bytes 41943040 | tf_op jit(solution)/shard_map/psum | solution.py:222
  354.9 15.8 %copy-start.17 = (bf16[1024,2048]{1,0:T(8,128)(2,1)S(1)}, bf16[1024,2048]{1,0:T(8,128)(2,1)}, u32[]{:S(2)}) copy-start(bf16[1024,2048]{1,0:T(8,128)(2,1)} %param.33) | copy-start | bytes 12582916
  355.0 39.5 %slice-start.4 = ((s8[8388608]{0:T(1024)(128)(4,1)}), s8[4194304]{0:T(1024)(128)(4,1)S(1)}, s32[]{:S(2)}) async-start(s8[8388608]{0:T(1024)(128)(4,1)} %bitcast.111), calls=%async_computation.9 | async-start | bytes 8388608
  370.7 19.9 %copy-start.19 = (bf16[1024,2048]{1,0:T(8,128)(2,1)S(1)}, bf16[1024,2048]{1,0:T(8,128)(2,1)}, u32[]{:S(2)}) copy-start(bf16[1024,2048]{1,0:T(8,128)(2,1)} %copy-done.18) | copy-start | bytes 12582916
  370.7 23.8 %slice-start.5 = ((s8[8388608]{0:T(1024)(128)(4,1)}), s8[4194304]{0:T(1024)(128)(4,1)S(1)}, s32[]{:S(2)}) async-start(s8[8388608]{0:T(1024)(128)(4,1)} %bitcast.111), calls=%async_computation.10 | async-start | bytes 8388608
  390.7 3.8 copy-start.25
  398.2 130.1 %copy-start.28 = (f32[2048]{0:T(1024)S(1)}, f32[2048]{0:T(1024)}, u32[]{:S(2)}) copy-start(f32[2048]{0:T(1024)} %copy-done.27) | copy-start | bytes 24580
  398.2 130.1 %copy-start.30 = (f32[1024]{0:T(1024)S(1)}, f32[1024]{0:T(1024)}, u32[]{:S(2)}) copy-start(f32[1024]{0:T(1024)} %copy-done.29) | copy-start | bytes 12292
  398.2 687.0 %all-reduce.13.cloned.1.call-start = ((), (), s32[]{:S(2)}) async-start(), calls=%async_computation.2 | async-start | bytes 4194304 | tf_op jit(solution)/shard_map/psum | solution.py:207
  443.8 91.8 %copy-start.34 = (f32[1024]{0:T(1024)S(1)}, f32[1024]{0:T(1024)}, u32[]{:S(2)}) copy-start(f32[1024]{0:T(1024)} %copy-done.33) | copy-start | bytes 12292
  443.9 91.8 %copy-start.32 = (f32[1024]{0:T(1024)S(1)}, f32[1024]{0:T(1024)}, u32[]{:S(2)}) copy-start(f32[1024]{0:T(1024)} %copy-done.31) | copy-start | bytes 12292
  532.8 9.2 copy-start.42
  965.6 122.8 %copy-start.1 = (bf16[512,2048]{1,0:T(8,128)(2,1)S(1)}, bf16[512,2048]{1,0:T(8,128)(2,1)}, u32[]{:S(2)}) copy-start(bf16[512,2048]{1,0:T(8,128)(2,1)} %param.25) | copy-start | bytes 6291460
  (9 other events, 12.9 us)
Sparse Core Ops, SparseCore 0:
  39.6 106.3 all-reduce.8
  202.3 103.6 all-reduce.10
  355.0 173.2 all-reduce.16
  532.3 413.0 all-reduce.14
  950.5 134.7 all-reduce.12
where the time goes:
time: 1100 us
  waiting for transfers between devices  738 us (67%)
  matrix products  148 us (13%)
  other arithmetic  111 us (10%)
  blocking collectives  70.6 us (6%)
  between operations  15.7 us (1%)
  local copies, waits for them, and re-layouts  11.6 us (1%)
    psum x1, waiting for transfers between devices, local(): lax.psum(grad_query.astype(jnp.bfloat16), 'dp').astype(jnp.float32)  355 us
    psum x1, waiting for transfers between devices, local(): lax.psum((grad_keyval, grad_vbias), ('dp', 'tensor'))  108 us
    psum x1, waiting for transfers between devices, local(): lax.psum(attn_terms.astype(jnp.bfloat16), 'tensor').astype(jnp.float32)  106 us
    psum x1, waiting for transfers between devices, local(): lax.psum(back_terms2.astype(jnp.bfloat16), 'tensor').astype(jnp.float32)  87.8 us
    psum x1, waiting for transfers between devices, local(): lax.psum(mlp_terms.astype(jnp.bfloat16), 'tensor').astype(jnp.float32)  81.6 us
    dot_general x5, matrix products, contract_rows(): lax.dot_general(left, right, (((0,), (0,)), ((), ())), preferred_element_...  48 us
    dot_general x5, matrix products, contract_cols(): lax.dot_general(left, right, (((1,), (1,)), ((), ())), preferred_element_...  40.2 us
    psum x1, blocking collectives, local(): lax.psum((grad_keyval, grad_vbias), ('dp', 'tensor'))  40 us
  transfers between devices with their start and end apart: 5, of which 5 were waited for; matrix products, arithmetic and copies ran while one was open for 12% of the time, Pallas kernels for 0%

commit v1 on v0

v1 whole, which is shorter than its diff:
```python
import functools

import jax
import jax.numpy as jnp
from jax import lax
from jax.experimental import pallas as pl
from jax.experimental.pallas import tpu as pltpu
from jax.sharding import PartitionSpec as P

STRIP = 16
SUBS = 2
EPS = 1e-05


def suffixes(count):
    if count == 0:
        return [()]
    rest = [()]
    for _ in range(count - 1):
        rest = [(bit,) + more for bit in (1, 0) for more in rest]
    return [(bit,) + more for bit in (1, 0) for more in rest]


def as_number(path):
    total = 0
    for bit in path:
        total = 2 * total + bit
    return total


class Tree:
    def __init__(self, axis, size, number, rows):
        self.axis, self.size = axis, size
        self.depth = size.bit_length() - 1
        self.number = number
        self.half = rows // 2
        self.unit = self.half // size
        order = list(range(self.depth))
        self.order = order if number == 0 else order[::-1]
        me = lax.axis_index(axis)
        self.mine = [(me // (1 << bit)) % 2 for bit in self.order]
        self.partners = [me + (1 - 2 * own) * (1 << bit) for own, bit in zip(self.mine, self.order)]

    def offset(self, path, skip=0):
        start = 0
        for level in range(skip, self.depth):
            side = (self.mine[level] + path[level]) % 2
            start = start + side * (self.half >> (level + 1))
        return start

    def rows(self, path, sub, sub_rows):
        start = self.number * self.half + self.offset(path) + sub * sub_rows
        return pl.ds(pl.multiple_of(start, sub_rows), sub_rows)

    def own_rows(self, path, sub, sub_rows):
        start = self.offset(path, 1) + sub * sub_rows
        return pl.multiple_of(start, sub_rows)

    def slot(self, level, path):
        base = sum(1 << (self.depth - 1 - lower) for lower in range(level))
        return base + as_number(path)


def stream(axis, size, shape, part, out, own, slots, outbuf, local_sem, send_sem, recv_sem, finish, loads=()):
    rows, width = shape
    trees = [Tree(axis, size, number, rows) for number in (0, 1)]
    unit = trees[0].unit
    depth = trees[0].depth
    sub_rows = unit // SUBS
    sends = []

    def remote(tree, src, dst, kind, index, sub, level):
        place = ((tree.number * 2 + kind) * (size - 1) + index) * SUBS + sub
        copy = pltpu.make_async_remote_copy(
            src_ref=src,
            dst_ref=dst,
            send_sem=send_sem.at[place],
            recv_sem=recv_sem.at[place],
            device_id={axis: tree.partners[level]},
            device_id_type=pl.DeviceIdType.MESH,
        )
        return copy

    def reduce_copy(tree, level, path, sub):
        slot = tree.slot(level, path)
        if level == 0:
            src = part.at[tree.rows((1,) + path, sub, sub_rows), :]
        else:
            src = slots.at[tree.number, tree.slot(level - 1, (1,) + path), pl.ds(sub * sub_rows, sub_rows), :]
        dst = slots.at[tree.number, slot, pl.ds(sub * sub_rows, sub_rows), :]
        return remote(tree, src, dst, 0, slot, sub, level)

    def gather_copy(tree, level, path, sub):
        there = path[:level] + (1,) + path[level + 1 :]
        where = tree.rows(path, sub, sub_rows)
        if any(path):
            src = out.at[where, :]
        else:
            src = outbuf.at[tree.number, pl.ds(sub * sub_rows, sub_rows), :]
        return remote(tree, src, out.at[where, :], 1, as_number(there) - 1, sub, level)

    copies = []
    for tree in trees:
        start = tree.number * tree.half + tree.mine[0] * (tree.half // 2)
        copies.append(
            pltpu.make_async_copy(
                part.at[pl.ds(pl.multiple_of(start, tree.half // 2), tree.half // 2), :],
                own.at[tree.number],
                local_sem.at[tree.number],
            )
        )
    for copy in copies:
        copy.start()
    for path in suffixes(depth - 1):
        for sub in range(SUBS):
            for tree in trees:
                copy = reduce_copy(tree, 0, path, sub)
                copy.start()
                sends.append(copy)
    for copy in copies:
        copy.wait()
    yield
    zero = (0,) * depth
    stored = []
    for level in range(depth):
        last = level == depth - 1
        if last:
            for load in loads:
                load.wait()
        for path in suffixes(depth - 1 - level):
            for sub in range(SUBS):
                for tree in trees:
                    reduce_copy(tree, level, path, sub).wait_recv()
                    slot = tree.slot(level, path)
                    first = tree.own_rows((0,) + path if level == 0 else zero, sub, sub_rows)

                    def strip(step, tree=tree, slot=slot, first=first, path=path, sub=sub, level=level, last=last):
                        line = sub * sub_rows + step * STRIP
                        here = pl.ds(pl.multiple_of(line, STRIP), STRIP)
                        if level == 0:
                            mine = own[tree.number, pl.ds(pl.multiple_of(first + step * STRIP, STRIP), STRIP), :]
                        else:
                            mine = slots[tree.number, tree.slot(level - 1, (0,) + path), here, :]
                        total = mine.astype(jnp.float32) + slots[tree.number, slot, here, :].astype(jnp.float32)
                        if last:
                            outbuf[tree.number, here, :] = finish(
                                total, tree.number, here, pl.ds(pl.multiple_of(tree.number * unit + line, STRIP), STRIP)
                            )
                        else:
                            slots[tree.number, slot, here, :] = total.astype(slots.dtype)

                    pl.loop(0, sub_rows // STRIP)(strip)
                    if last:
                        keep = pltpu.make_async_copy(
                            outbuf.at[tree.number, pl.ds(sub * sub_rows, sub_rows), :],
                            out.at[tree.rows(zero, sub, sub_rows), :],
                            local_sem.at[2 + tree.number * SUBS + sub],
                        )
                        keep.start()
                        stored.append(keep)
                        for back in reversed(range(depth)):
                            copy = gather_copy(tree, back, zero, sub)
                            copy.start()
                            sends.append(copy)
                    elif path[0] == 1:
                        copy = reduce_copy(tree, level + 1, path[1:], sub)
                        copy.start()
                        sends.append(copy)
            if not last:
                yield
        yield
    for level in reversed(range(depth)):
        for path in suffixes(depth - 1 - level):
            full = (0,) * level + (1,) + path
            sender = (0,) * (level + 1) + path
            for sub in range(SUBS):
                for tree in trees:
                    gather_copy(tree, level, sender, sub).wait_recv()
                    for back in reversed(range(level)):
                        copy = gather_copy(tree, back, full, sub)
                        copy.start()
                        sends.append(copy)
        yield
    for copy in sends:
        copy.wait_send()
    for copy in stored:
        copy.wait()


def greet(axis, size):
    barrier = pltpu.get_barrier_semaphore()
    me = lax.axis_index(axis)
    for step in range(1, size):
        pl.semaphore_signal(
            barrier, inc=1, device_id={axis: (me + step) % size}, device_id_type=pl.DeviceIdType.MESH
        )
    pl.semaphore_wait(barrier, size - 1)


def run_together(streams):
    waiting = list(streams)
    while waiting:
        left = []
        for one in waiting:
            try:
                next(one)
                left.append(one)
            except StopIteration:
                pass
        waiting = left


def stream_scratch(size, rows, width):
    half = rows // 2
    unit = half // size
    count = 2 * 2 * (size - 1) * SUBS
    return [
        pltpu.VMEM((2, half // 2, width), jnp.bfloat16),
        pltpu.VMEM((2, size - 1, unit, width), jnp.bfloat16),
        pltpu.VMEM((2, unit, width), jnp.bfloat16),
        pltpu.SemaphoreType.DMA((2 + 2 * SUBS,)),
        pltpu.SemaphoreType.DMA((count,)),
        pltpu.SemaphoreType.DMA((count,)),
    ]


def load_rows(axis, size, rows, source, target, sems):
    copies = []
    for number in (0, 1):
        tree = Tree(axis, size, number, rows)
        unit = tree.unit
        copies.append(
            pltpu.make_async_copy(
                source.at[tree.rows((0,) * tree.depth, 0, unit), :], target.at[number], sems.at[number]
            )
        )
    for copy in copies:
        copy.start()
    return copies


def moments(values):
    center = values - jnp.mean(values, axis=-1, keepdims=True)
    scale = lax.rsqrt(jnp.mean(center * center, axis=-1, keepdims=True) + EPS)
    return center * scale, scale


def norm_back(grad, gain, scaled, scale):
    inner = grad * gain
    return scale * (
        inner
        - jnp.mean(inner, axis=-1, keepdims=True)
        - scaled * jnp.mean(inner * scaled, axis=-1, keepdims=True)
    )


def fold(values):
    return values[:8] + values[8:]


HBM = pl.BlockSpec(memory_space=pl.ANY)
VMEM = pl.BlockSpec(memory_space=pltpu.VMEM)


def middle_kernel(size, rows, width, part, tokens, pbias, gain, shift, hidden, mid, own, slots, outbuf, local_sem, send_sem, recv_sem, tok, load_sem):
    greet("tensor", size)
    loads = load_rows("tensor", size, rows, tokens, tok, load_sem)

    def finish(total, number, here, line):
        value = tok[number, here, :].astype(jnp.float32) + total + pbias[...]
        mid[line, :] = value
        scaled, _ = moments(value)
        return (scaled * gain[...] + shift[...]).astype(jnp.bfloat16)

    run_together(
        [stream("tensor", size, (rows, width), part, hidden, own, slots, outbuf, local_sem, send_sem, recv_sem, finish, loads)]
    )


def reduce_middle(size, part, tokens, pbias, gain, shift):
    rows, width = part.shape
    unit = rows // 2 // size
    return pl.pallas_call(
        functools.partial(middle_kernel, size, rows, width),
        out_shape=(
            jax.ShapeDtypeStruct((rows, width), jnp.bfloat16),
            jax.ShapeDtypeStruct((2 * unit, width), jnp.float32),
        ),
        in_specs=[HBM, HBM, VMEM, VMEM, VMEM],
        out_specs=(HBM, VMEM),
        scratch_shapes=stream_scratch(size, rows, width)
        + [pltpu.VMEM((2, unit, width), jnp.bfloat16), pltpu.SemaphoreType.DMA((2,))],
        compiler_params=pltpu.CompilerParams(collective_id=1, has_side_effects=True),
        name="reduce_middle",
    )(part, tokens, pbias, gain, shift)


def back_kernel(size, rows, width, part, d_out, mid, gain, low, dmid, sums, own, slots, outbuf, local_sem, send_sem, recv_sem, dout, load_sem):
    greet("tensor", size)
    loads = load_rows("tensor", size, rows, d_out, dout, load_sem)
    sums[...] = jnp.zeros_like(sums)

    def finish(total, number, here, line):
        scaled, scale = moments(mid[line, :])
        direct = dout[number, here, :].astype(jnp.float32)
        value = direct + norm_back(total, gain[...], scaled, scale)
        dmid[line, :] = value
        sums[0] += fold(total * scaled)
        sums[1] += fold(total)
        sums[2] += fold(value)
        sums[3] += fold(direct)
        return value.astype(jnp.bfloat16)

    run_together(
        [stream("tensor", size, (rows, width), part, low, own, slots, outbuf, local_sem, send_sem, recv_sem, finish, loads)]
    )


def reduce_back(size, part, d_out, mid, gain):
    rows, width = part.shape
    unit = rows // 2 // size
    return pl.pallas_call(
        functools.partial(back_kernel, size, rows, width),
        out_shape=(
            jax.ShapeDtypeStruct((rows, width), jnp.bfloat16),
            jax.ShapeDtypeStruct((2 * unit, width), jnp.float32),
            jax.ShapeDtypeStruct((4, 8, width), jnp.float32),
        ),
        in_specs=[HBM, HBM, VMEM, VMEM],
        out_specs=(HBM, VMEM, VMEM),
        scratch_shapes=stream_scratch(size, rows, width)
        + [pltpu.VMEM((2, unit, width), jnp.bfloat16), pltpu.SemaphoreType.DMA((2,))],
        compiler_params=pltpu.CompilerParams(collective_id=2, has_side_effects=True),
        name="reduce_back",
    )(part, d_out, mid, gain)


def last_kernel(size, rows, width, kv_rows, mlp, part, kv, tokens, mid, dmid, dbias, gain, result, grad, kv_out, sums, *scratch):
    greet("tensor", size)
    first, second, third = scratch[:6], scratch[6:12], scratch[12:18]
    tok, load_sem = scratch[18:]
    loads = load_rows("tensor", size, rows, tokens, tok, load_sem)
    sums[...] = jnp.zeros_like(sums)

    def finish_result(total, number, here, line):
        return (mid[line, :] + total + dbias[...]).astype(jnp.bfloat16)

    def finish_grad(total, number, here, line):
        scaled, scale = moments(tok[number, here, :].astype(jnp.float32))
        sums[0] += fold(total * scaled)
        sums[1] += fold(total)
        return (dmid[line, :] + norm_back(total, gain[...], scaled, scale)).astype(jnp.bfloat16)

    def finish_kv(total, number, here, line):
        return total.astype(jnp.bfloat16)

    run_together(
        [
            stream("tensor", size, (rows, width), mlp, result, *first, finish_result),
            stream("tensor", size, (rows, width), part, grad, *second, finish_grad, loads),
            stream("tensor", size, (kv_rows, width), kv, kv_out, *third, finish_kv),
        ]
    )


def reduce_last(size, mlp, part, kv, tokens, mid, dmid, dbias, gain):
    rows, width = part.shape
    unit = rows // 2 // size
    kv_rows = kv.shape[0]
    return pl.pallas_call(
        functools.partial(last_kernel, size, rows, width, kv_rows),
        out_shape=(
            jax.ShapeDtypeStruct((rows, width), jnp.bfloat16),
            jax.ShapeDtypeStruct((rows, width), jnp.bfloat16),
            jax.ShapeDtypeStruct((kv_rows, width), jnp.bfloat16),
            jax.ShapeDtypeStruct((2, 8, width), jnp.float32),
        ),
        in_specs=[HBM, HBM, HBM, HBM, VMEM, VMEM, VMEM, VMEM],
        out_specs=(HBM, HBM, HBM, VMEM),
        scratch_shapes=stream_scratch(size, rows, width) * 2
        + stream_scratch(size, kv_rows, width)
        + [pltpu.VMEM((2, unit, width), jnp.bfloat16), pltpu.SemaphoreType.DMA((2,))],
        compiler_params=pltpu.CompilerParams(collective_id=3, has_side_effects=True),
        name="reduce_last",
    )(mlp, part, kv, tokens, mid, dmid, dbias, gain)


def layer_norm(values, gain, shift):
    center = values - jnp.mean(values, axis=-1, keepdims=True)
    scaled = center * lax.rsqrt(jnp.mean(center * center, axis=-1, keepdims=True) + 1e-05)
    return scaled * gain + shift


def gelu_tanh(values):
    return (
        0.5
        * values
        * (1.0 + jnp.tanh(0.7978845608028654 * (values + 0.044715 * values * values * values)))
    )


def contract_rows(left, right):
    return lax.dot_general(
        left, right, (((0,), (0,)), ((), ())), preferred_element_type=jnp.float32
    )


def contract_cols(left, right):
    return lax.dot_general(
        left, right, (((1,), (1,)), ((), ())), preferred_element_type=jnp.float32
    )


def block_scores(query_block, key_rows, offset, length):
    scale = query_block.shape[2] ** (-0.5)
    scores = (
        jnp.einsum("qhd,kd->hqk", query_block, key_rows, preferred_element_type=jnp.float32) * scale
    )
    rows_pos = offset + jnp.arange(query_block.shape[0], dtype=jnp.int32)
    keys_pos = jnp.arange(key_rows.shape[0], dtype=jnp.int32)
    allowed = (keys_pos[None, :] <= rows_pos[:, None]) & (keys_pos[None, :] < length)
    return jnp.where(allowed[None], scores, -1e30)


def attend_forward(queries, key_rows, value_rows, length, block_rows):
    pieces = []
    log_totals = []
    for offset in range(0, queries.shape[0], block_rows):
        query_block = queries[offset : offset + block_rows]
        scores = block_scores(query_block, key_rows, offset, length)
        highest = jnp.max(scores, axis=-1, keepdims=True)
        exponent = jnp.exp(scores - highest)
        normaliser = jnp.sum(exponent, axis=-1, keepdims=True)
        probability = (exponent / normaliser).astype(jnp.bfloat16)
        log_totals.append(highest + jnp.log(normaliser))
        pieces.append(
            jnp.einsum("hqk,kd->qhd", probability, value_rows, preferred_element_type=jnp.float32)
        )
    return (jnp.concatenate(pieces, axis=0), log_totals)


def attend_backward(queries, key_rows, value_rows, length, block_rows, log_totals, grad_heads):
    scale = queries.shape[2] ** (-0.5)
    query_grads = []
    key_grads = jnp.zeros(key_rows.shape, jnp.float32)
    value_grads = jnp.zeros(value_rows.shape, jnp.float32)
    for counter, offset in enumerate(range(0, queries.shape[0], block_rows)):
        query_block = queries[offset : offset + block_rows]
        grad_block = grad_heads[offset : offset + block_rows]
        scores = block_scores(query_block, key_rows, offset, length)
        probability = jnp.exp(scores - log_totals[counter])
        grad_probs = jnp.einsum(
            "qhd,kd->hqk", grad_block, value_rows, preferred_element_type=jnp.float32
        )
        inner = jnp.sum(probability * grad_probs, axis=-1, keepdims=True)
        grad_scores = (probability * (grad_probs - inner)).astype(jnp.bfloat16)
        query_grads.append(
            (
                jnp.einsum("hqk,kd->qhd", grad_scores, key_rows, preferred_element_type=jnp.float32)
                * scale
            ).astype(jnp.bfloat16)
        )
        key_grads = (
            key_grads
            + jnp.einsum(
                "hqk,qhd->kd", grad_scores, query_block, preferred_element_type=jnp.float32
            )
            * scale
        )
        value_grads = value_grads + jnp.einsum(
            "hqk,qhd->kd",
            probability.astype(jnp.bfloat16),
            grad_block,
            preferred_element_type=jnp.float32,
        )
    return (jnp.concatenate(query_grads, axis=0), key_grads, value_grads)


def local(
    size,
    tokens,
    lengths,
    norm1_gain,
    norm1_shift,
    query_weight,
    query_bias,
    keyval_weight,
    value_bias,
    proj_weight,
    proj_bias,
    norm2_gain,
    norm2_shift,
    up_weight,
    up_bias,
    down_weight,
    down_bias,
    cotangent,
):
    wide = jnp.float32
    slot_len, width = tokens.shape
    head_dim = keyval_weight.shape[1] // 2
    heads_here = query_weight.shape[1] // head_dim
    block_rows = min(512, slot_len)
    length = lengths[0]

    def row(vector):
        return vector.astype(wide).reshape(1, -1)

    hidden1 = layer_norm(tokens.astype(wide), norm1_gain.astype(wide), norm1_shift.astype(wide)).astype(jnp.bfloat16)
    queries = (
        jnp.dot(hidden1, query_weight, preferred_element_type=wide) + query_bias.astype(wide)
    ).astype(jnp.bfloat16)
    keyval = jnp.dot(hidden1, keyval_weight, preferred_element_type=wide)
    key_rows = keyval[:, :head_dim].astype(jnp.bfloat16)
    value_rows = (keyval[:, head_dim:] + value_bias.astype(wide)).astype(jnp.bfloat16)
    slot_queries = queries.reshape(slot_len, heads_here, head_dim)
    attended, log_totals = attend_forward(slot_queries, key_rows, value_rows, length, block_rows)
    heads_out = attended.reshape(slot_len, heads_here * head_dim).astype(jnp.bfloat16)
    attn_terms = jnp.dot(heads_out, proj_weight, preferred_element_type=wide).astype(jnp.bfloat16)
    hidden2, mid = reduce_middle(size, attn_terms, tokens, row(proj_bias), row(norm2_gain), row(norm2_shift))

    pre_act = jnp.dot(hidden2, up_weight, preferred_element_type=wide) + up_bias.astype(wide)
    activated = gelu_tanh(pre_act).astype(jnp.bfloat16)
    valid = (jnp.arange(slot_len, dtype=jnp.int32) < length)[:, None]
    d_out = jnp.where(valid, cotangent, jnp.zeros_like(cotangent))
    grad_down = contract_rows(activated, d_out).astype(jnp.bfloat16)
    grad_down = lax.psum(grad_down, "dp")
    grad_act = contract_cols(d_out, down_weight).astype(jnp.bfloat16)
    gelu_pull = jax.vjp(gelu_tanh, pre_act)[1]
    grad_pre = gelu_pull(grad_act.astype(wide))[0].astype(jnp.bfloat16)
    back2 = contract_cols(grad_pre, up_weight).astype(jnp.bfloat16)
    middle_low, dmid, sums2 = reduce_back(size, back2, d_out, mid, row(norm2_gain))
    grad_up = contract_rows(hidden2, grad_pre).astype(jnp.bfloat16)
    grad_up, grad_down = lax.optimization_barrier((grad_up, grad_down))
    grad_up = lax.psum(grad_up, "dp")
    grad_upbias = jnp.sum(grad_pre.astype(wide), axis=0)
    mlp_terms = jnp.dot(activated, down_weight, preferred_element_type=wide).astype(jnp.bfloat16)

    grad_proj = contract_rows(heads_out, middle_low).astype(jnp.bfloat16)
    grad_heads = contract_cols(middle_low, proj_weight).astype(jnp.bfloat16)
    slot_grads = grad_heads.reshape(slot_len, heads_here, head_dim)
    query_part, key_part, value_part = attend_backward(
        slot_queries, key_rows, value_rows, length, block_rows, log_totals, slot_grads
    )
    grad_queries = query_part.reshape(slot_len, heads_here * head_dim)
    grad_kv_rows = jnp.concatenate([key_part, value_part], axis=1).astype(jnp.bfloat16)
    grad_qbias = jnp.sum(grad_queries.astype(wide), axis=0)
    grad_query = contract_rows(hidden1, grad_queries).astype(jnp.bfloat16)
    grad_keyval = contract_rows(hidden1, grad_kv_rows).astype(jnp.bfloat16)
    grad_vbias = jnp.sum(grad_kv_rows[:, head_dim:].astype(wide), axis=0)
    back1 = (
        contract_cols(grad_queries, query_weight) + contract_cols(grad_kv_rows, keyval_weight)
    ).astype(jnp.bfloat16)
    result, grad_tokens, kv_sum, sums1 = reduce_last(
        size,
        mlp_terms,
        back1,
        grad_keyval.reshape(-1, width),
        tokens,
        mid,
        dmid,
        row(down_bias),
        row(norm1_gain),
    )
    grad_query, grad_up = lax.optimization_barrier((grad_query, grad_up))
    grad_query, grad_proj, kv_sum = lax.psum((grad_query, grad_proj, kv_sum), "dp")
    shared = jnp.concatenate(
        [jnp.sum(sums1, axis=1).reshape(-1), jnp.sum(sums2, axis=1).reshape(-1), grad_vbias]
    )
    shared = lax.psum(shared, ("dp", "tensor"))
    split = lax.psum(jnp.concatenate([grad_qbias, grad_upbias]), "dp")
    grad_qbias, grad_upbias = split[: grad_qbias.shape[0]], split[grad_qbias.shape[0] :]
    grad_gain1, grad_shift1, grad_gain2, grad_shift2, grad_pbias, grad_dnbias = (
        shared[place * width : (place + 1) * width] for place in range(6)
    )
    grad_vbias = shared[6 * width :]
    return (
        result,
        grad_tokens,
        grad_gain1,
        grad_shift1,
        grad_query.astype(wide),
        grad_qbias,
        kv_sum.reshape(keyval_weight.shape).astype(wide),
        grad_vbias,
        grad_proj.astype(wide),
        grad_pbias,
        grad_gain2,
        grad_shift2,
        grad_up.astype(wide),
        grad_upbias,
        grad_down.astype(wide),
        grad_dnbias,
    )


def solution(mesh):
    in_specs = (
        P("dp", None),
        P("dp"),
        P(),
        P(),
        P(None, "tensor"),
        P("tensor"),
        P(),
        P(),
        P("tensor", None),
        P(),
        P(),
        P(),
        P(None, "tensor"),
        P("tensor"),
        P("tensor", None),
        P(),
        P("dp", None),
    )
    out_specs = (
        P("dp", None),
        P("dp", None),
        P(),
        P(),
        P(None, "tensor"),
        P("tensor"),
        P(),
        P(),
        P("tensor", None),
        P(),
        P(),
        P(),
        P(None, "tensor"),
        P("tensor"),
        P("tensor", None),
        P(),
    )
    return jax.shard_map(functools.partial(local, mesh.shape["tensor"]), mesh=mesh, in_specs=in_specs, out_specs=out_specs, check_vma=False)
```

time: 1100 us -> 666 us (0.61)
  waiting for transfers between devices: 738 us -> 42.2 us
  Pallas kernels: 0 us -> 308 us
  other arithmetic: 111 us -> 58.1 us
    psum x5 -> x3, waiting for transfers between devices: 738 us -> 42.2 us  [the longest x1 24.4 us: local(): lax.psum((grad_query, grad_proj, kv_sum), 'dp')]
    pallas_call x0 -> x3, Pallas kernels: none -> 308 us  [the longest x1 159 us: reduce_last(): pl.pallas_call(functools.partial(last_kernel, size, rows, width, kv_rows)...]
    reduce_sum x8 -> x3, other arithmetic: 34.9 us -> 0.34 us  [the longest x1 0.21 us: local(): grad_qbias = jnp.sum(grad_queries.astype(wide), axis=0)]
    convert_element_type x25 -> x12, other arithmetic: 54.2 us -> 37.2 us  [the longest x1 11.7 us: local(): grad_up.astype(wide)]
    dot_general x5, matrix products: 40.2 us -> 52.7 us  [contract_cols(): lax.dot_general(left, right, (((1,), (1,)), ((), ())), preferred_element_...]
  transfers between devices with their start and end apart: 5 -> 3, of which waited for: 5 -> 2; matrix products, arithmetic and copies ran while one was open for 12% -> 23% of each run, Pallas kernels for 0% -> 35%
where the time goes in v1:
time: 666 us; the launch traced here: 662 us
  Pallas kernels  308 us (46%)
  matrix products  153 us (23%)
  blocking collectives  66.5 us (10%)
  other arithmetic  58.1 us (9%)
  waiting for transfers between devices  42.2 us (6%)
  local copies, waits for them, and re-layouts  18.6 us (3%)
  between operations  15.5 us (2%)
    pallas_call x1, Pallas kernels, reduce_last(): pl.pallas_call(functools.partial(last_kernel, size, rows, width, kv_rows)...  159 us
    pallas_call x1, Pallas kernels, reduce_middle(): pl.pallas_call(functools.partial(middle_kernel, size, rows, width), out_s...  75.2 us
    pallas_call x1, Pallas kernels, reduce_back(): pl.pallas_call(functools.partial(back_kernel, size, rows, width), out_sha...  73.8 us
    dot_general x5, matrix products, contract_cols(): lax.dot_general(left, right, (((1,), (1,)), ((), ())), preferred_element_...  52.7 us
    psum x1, blocking collectives, local(): shared = lax.psum(shared, ('dp', 'tensor'))  38.4 us
    dot_general x5, matrix products, contract_rows(): lax.dot_general(left, right, (((0,), (0,)), ((), ())), preferred_element_...  37.4 us
    psum x1, blocking collectives, local(): split = lax.psum(jnp.concatenate([grad_qbias, grad_upbias]), 'dp')  28 us
    psum x1, waiting for transfers between devices, local(): lax.psum((grad_query, grad_proj, kv_sum), 'dp')  24.4 us
  transfers between devices with their start and end apart: 3, of which 2 were waited for; matrix products, arithmetic and copies ran while one was open for 23% of the time, Pallas kernels for 35%

profile of v1, /device:TPU:0, one launch (start us, length us, event | category | flops | bytes accessed | tf_op | source)
XLA Modules:
  0.0 662.0 jit_solution(3722511149110174904)
XLA Ops:
  10.0 3.0 convert_reduce_fusion
  13.0 3.4 fusion.2
  18.3 2.0 fusion.5
  20.4 2.4 add_convert_fusion.1
  25.3 2.4 broadcast_select_fusion.d_out
  27.7 1.6 fusion.66
  30.5 1.7 fusion.48
  32.8 1.6 fusion.67
  35.6 1.9 fusion.47
  38.8 4.4 convolution_convert_fusion.4.part
  43.2 75.2 %reduce_middle.1 = (bf16[1024,2048]{1,0:T(8,128)(2,1)}, f32[256,2048]{1,0:T(8,128)}) custom-call(bf16[1024,2048]{1,0:T(8,128)(2,1)} %convolution_convert_fusion.4.part, bf16[1024,2048]{1,0:T(8,128)(2,1)} %tokens.3, f32[1,2048]{1,0:T(1,128)} %bitcast.144, f32[1,2048]{1,0:T(1,128)} %bitcast.139, f32[1,2048]{1,0:T(1,128)} %bitcast.145), custom_call_target="tpu_custom_call" | custom-call | tf_op jit(solution)/shard_map/reduce_middle/pallas_call | solution.py:283
  118.4 12.6 %fusion.73 = f32[1024,2048]{1,0:T(8,128)S(1)} fusion(bf16[1024,2048]{1,0:T(8,128)(2,1)} %get-tuple-element.29, bf16[2048,2048]{1,0:T(8,128)(2,1)} %param.29), kind=kOutput, calls=%fused_computation.114 | convolution fusion | flops 8589934592 | bytes 20971520 | tf_op jit(solution)/shard_map/dot_general | solution.py:522
  131.1 3.4 copy-done.39
  134.4 12.7 %convolution_convert_fusion = bf16[2048,2048]{1,0:T(8,128)(2,1)} fusion(bf16[1024,2048]{1,0:T(8,128)(2,1)S(1)} %copy-done.5, f32[1024,2048]{1,0:T(8,128)S(1)} %fusion.73, f32[2048]{0:T(1024)S(1)} %convert_element_type.151), kind=kOutput, calls=%fused_computation.44 | convolution fusion | flops 8615100416 | bytes 20979712 | tf_op jit(solution)/shard_map/dot_general | solution.py:403
  147.2 20.3 %convert_reduce_fusion.1 = (f32[2048]{0:T(1024)S(1)}, bf16[1024,2048]{1,0:T(8,128)(2,1)S(1)}) fusion(bf16[1024,2048]{1,0:T(8,128)(2,1)} %broadcast_select_fusion.d_out, bf16[2048,2048]{1,0:T(8,128)(2,1)} %param.31, f32[1024,2048]{1,0:T(8,128)} %copy-done.39, f32[2048]{0:T(1024)S(1)} %convert_element_type.151), kind=kOutput, calls=%fused_computation.35 | convolution fusion | flops 8650749952 | bytes 25182208 | tf_op jit(solution)/shard_map/dot_general | solution.py:409
  167.5 14.4 %convolution_convert_fusion.2.part = bf16[1024,2048]{1,0:T(8,128)(2,1)} fusion(bf16[1024,2048]{1,0:T(8,128)(2,1)S(1)} %get-tuple-element.68, bf16[2048,2048]{1,0:T(8,128)(2,1)} %param.29), kind=kOutput, calls=%fused_computation.57 | convolution fusion | flops 8592031744 | bytes 16777216 | tf_op jit(solution)/shard_map/dot_general | solution.py:409
  181.9 73.8 %reduce_back.1 = (bf16[1024,2048]{1,0:T(8,128)(2,1)}, f32[256,2048]{1,0:T(8,128)}, f32[4,8,2048]{2,1,0:T(8,128)}) custom-call(bf16[1024,2048]{1,0:T(8,128)(2,1)} %convolution_convert_fusion.2.part, bf16[1024,2048]{1,0:T(8,128)(2,1)} %broadcast_select_fusion.d_out, f32[256,2048]{1,0:T(8,128)} %get-tuple-element.30.mid, f32[1,2048]{1,0:T(1,128)} %bitcast.140), custom_call_target="tpu_custom_call" | custom-call | tf_op jit(solution)/shard_map/reduce_back/pallas_call | solution.py:322
  255.7 4.8 convolution_convert_fusion.8
  260.6 5.3 fusion.15
  266.0 2.5 fusion.17
  268.5 3.3 convolution_bitcast_fusion
  271.8 1.5 fusion.39
  273.4 1.9 fusion.18
  275.3 2.6 fusion.20
  280.1 2.9 fusion.54
  283.0 5.8 fusion.74
  288.8 1.5 fusion.41
  290.4 1.6 convert_reduce_fusion.3
  293.9 11.4 %convolution_convert_fusion.1 = bf16[2048,2048]{1,0:T(8,128)(2,1)} fusion(bf16[1024,2048]{1,0:T(8,128)(2,1)S(1)} %copy-done.36, bf16[1024,2048]{1,0:T(8,128)(2,1)S(1)} %copy-done.41), kind=kOutput, calls=%fused_computation.45 | convolution fusion | flops 8594128896 | bytes 16777216 | tf_op jit(solution)/shard_map/dot_general | solution.py:403
  305.3 17.8 %all-reduce.5.cloned.1.call-done = bf16[2048,2048]{1,0:T(8,128)(2,1)} async-done(((bf16[2048,2048]{1,0:T(8,128)(2,1)}), bf16[2048,2048]{1,0:T(8,128)(2,1)}) %all-reduce.5.cloned.1.call-update) | async-done | bytes 8388624 | tf_op jit(solution)/shard_map/psum | solution.py:527
  323.2 3.5 convolution_convert_fusion.7
  327.3 1.7 reshape.198.kv
  329.0 7.5 %add_convert_fusion.part = bf16[1024,2048]{1,0:T(8,128)(2,1)} fusion(f32[1024,2048]{1,0:T(8,128)} %fusion.74, bf16[2048,256]{1,0:T(8,128)(2,1)S(1)} %copy-done.21, bf16[1024,128]{0,1:T(8,128)(2,1)S(1)} %get-tuple-element.66, bf16[1024,128]{0,1:T(8,128)(2,1)S(1)} %fusion.54), kind=kOutput, calls=%fused_computation.36 | convolution fusion | flops 1078984704 | bytes 14155776 | tf_op jit(solution)/shard_map/dot_general | solution.py:409
  336.5 16.1 %convolution_convert_fusion.3.mlp = bf16[1024,2048]{1,0:T(8,128)(2,1)} fusion(bf16[2048,2048]{1,0:T(8,128)(2,1)} %param.31, f32[1024,2048]{1,0:T(8,128)} %copy-done.39, f32[2048]{0:T(1024)S(1)} %convert_element_type.151), kind=kOutput, calls=%fused_computation.58 | convolution fusion | flops 8613003264 | bytes 20979712 | tf_op jit(solution)/shard_map/dot_general | solution.py:537
  352.6 159.2 %reduce_last.1 = (bf16[1024,2048]{1,0:T(8,128)(2,1)}, bf16[1024,2048]{1,0:T(8,128)(2,1)}, bf16[256,2048]{1,0:T(8,128)(2,1)}, f32[2,8,2048]{2,1,0:T(8,128)}) custom-call(bf16[1024,2048]{1,0:T(8,128)(2,1)} %convolution_convert_fusion.3.mlp, bf16[1024,2048]{1,0:T(8,128)(2,1)} %add_convert_fusion.part, bf16[256,2048]{1,0:T(8,128)(2,1)} %reshape.198.kv, ...), custom_call_target="tpu_custom_call" | custom-call | tf_op jit(solution)/shard_map/reduce_last/pallas_call | solution.py:370
  511.8 2.6 convert_element_type.176
  514.4 6.0 convolution_convert_fusion.5
  520.4 3.8 convolution_convert_fusion.6
  524.5 28.0 %psum.53 = f32[2560]{0:T(1024)S(1)} all-reduce(f32[2560]{0:T(1024)S(1)} %pad_maximum_fusion.6), channel_id=1, replica_groups=mesh['dp'=8,'tensor'=4] {'dp'}, use_global_device_ids=true, to_apply=%region_17.18 | all-reduce | flops 2560 | bytes 20480 | tf_op jit(solution)/shard_map/psum | solution.py:571
  553.9 38.4 %psum.49 = f32[12416]{0:T(1024)S(1)} all-reduce(f32[12416]{0:T(1024)S(1)} %pad_maximum_fusion.5), channel_id=1, replica_groups=mesh['dp'=8,'tensor'=4] {'dp','tensor'}, use_global_device_ids=true, to_apply=%region_11.12 | all-reduce | flops 12416 | bytes 99328 | tf_op jit(solution)/shard_map/psum | solution.py:570
  593.4 11.7 %convert_element_type.181 = f32[2048,2048]{1,0:T(8,128)} convert(bf16[2048,2048]{1,0:T(8,128)(2,1)} %all-reduce.5.cloned.1.call-done) | non-fusion elementwise | flops 4194304 | bytes 25165824 | tf_op jit(solution)/shard_map/convert_element_type | solution.py:592
  605.2 11.7 %convert_element_type.180 = f32[2048,2048]{1,0:T(8,128)} convert(bf16[2048,2048]{1,0:T(8,128)(2,1)} %all-reduce.7.cloned.1.call-done) | non-fusion elementwise | flops 4194304 | bytes 25165824 | tf_op jit(solution)/shard_map/convert_element_type | solution.py:590
  616.9 24.4 %all-reduce.9.cloned.1.call-done = (bf16[2048,512]{1,0:T(8,128)(2,1)}, bf16[2048,256]{1,0:T(8,128)(2,1)}, bf16[512,2048]{1,0:T(8,128)(2,1)}) async-done(((bf16[2048,512]{1,0:T(8,128)(2,1)}, bf16[2048,256]{1,0:T(8,128)(2,1)}, bf16[512,2048]{1,0:T(8,128)(2,1)}), (bf16[2048,512]{1,0:T(8,128)(2,1)}, bf16[2048,256]{1,0:T(8,128)(2,1)}, bf16[512,2048]{1,0:T(8,128)(2,1)})) %all-reduce.9.cloned.1.call-update) | async-done | bytes 5242896 | tf_op jit(solution)/shard_map/psum | solution.py:566
  641.3 4.3 convert_element_type.173
  645.7 2.9 convert_element_type.177
  648.5 2.5 convert_element_type.179
  651.1 2.1 copy.85
  653.2 2.0 copy.86
  (136 shorter events, 18.0 us)
Async XLA Ops:
  7.2 31.6 %copy-start = (bf16[512,2048]{1,0:T(8,128)(2,1)S(1)}, bf16[512,2048]{1,0:T(8,128)(2,1)}, u32[]{:S(2)}) copy-start(bf16[512,2048]{1,0:T(8,128)(2,1)} %param.25) | copy-start | bytes 6291460
  7.2 9.2 %copy-start.29 = (bf16[2048]{0:T(1024)(128)(2,1)S(1)}, bf16[2048]{0:T(1024)(128)(2,1)}, u32[]{:S(2)}) copy-start(bf16[2048]{0:T(1024)(128)(2,1)} %param.30) | copy-start | bytes 12292
  7.2 9.2 %copy-start.30 = (bf16[2048]{0:T(1024)(128)(2,1)S(1)}, bf16[2048]{0:T(1024)(128)(2,1)}, u32[]{:S(2)}) copy-start(bf16[2048]{0:T(1024)(128)(2,1)} %param.19) | copy-start | bytes 12292
  7.2 9.2 %copy-start.31 = (bf16[2048]{0:T(1024)(128)(2,1)S(1)}, bf16[2048]{0:T(1024)(128)(2,1)}, u32[]{:S(2)}) copy-start(bf16[2048]{0:T(1024)(128)(2,1)} %param.20) | copy-start | bytes 12292
  7.2 9.3 %copy-start.32 = (bf16[2048]{0:T(1024)(128)(2,1)S(1)}, bf16[2048]{0:T(1024)(128)(2,1)}, u32[]{:S(2)}) copy-start(bf16[2048]{0:T(1024)(128)(2,1)} %param.26) | copy-start | bytes 12292
  7.2 9.9 %copy-start.33 = (bf16[2048]{0:T(1024)(128)(2,1)S(1)}, bf16[2048]{0:T(1024)(128)(2,1)}, u32[]{:S(2)}) copy-start(bf16[2048]{0:T(1024)(128)(2,1)} %param.27) | copy-start | bytes 12292
  7.2 10.5 %copy-start.34 = (bf16[2048]{0:T(1024)(128)(2,1)S(1)}, bf16[2048]{0:T(1024)(128)(2,1)}, u32[]{:S(2)}) copy-start(bf16[2048]{0:T(1024)(128)(2,1)} %param.28) | copy-start | bytes 12292
  7.3 315.8 %all-reduce.5.cloned.1.call-start = ((), (), s32[]{:S(2)}) async-start(), calls=%async_computation | async-start | bytes 16777216 | tf_op jit(solution)/shard_map/psum | solution.py:527
  7.3 11.0 %copy-start.4 = (bf16[1024,2048]{1,0:T(8,128)(2,1)S(1)}, bf16[1024,2048]{1,0:T(8,128)(2,1)}, u32[]{:S(2)}) copy-start(bf16[1024,2048]{1,0:T(8,128)(2,1)} %tokens.3) | copy-start | bytes 12582916
  10.0 10.3 %copy-start.37 = (bf16[2048,512]{1,0:T(8,128)(2,1)S(1)}, bf16[2048,512]{1,0:T(8,128)(2,1)}, u32[]{:S(2)}) copy-start(bf16[2048,512]{1,0:T(8,128)(2,1)} %param.21) | copy-start | bytes 6291460
  16.5 1.8 copy-start.28
  20.4 2.5 copy-start.11
  20.4 2.5 copy-start.20
  22.8 2.5 copy-start.13
  22.9 4.8 copy-start.19
  24.2 8.6 %copy-start.6 = (f32[1024,256]{1,0:T(8,128)}, f32[1024,256]{1,0:T(8,128)S(1)}, u32[]{:S(2)}) copy-start(f32[1024,256]{1,0:T(8,128)S(1)} %fusion.72) | copy-start | bytes 3145732
  27.7 232.9 %copy-start.16 = (bf16[1024,128,1]{1,0,2:T(8,128)(2,1)}, bf16[1024,128,1]{1,0,2:T(8,128)(2,1)S(1)}, u32[]{:S(2)}) copy-start(bf16[1024,128,1]{1,0,2:T(8,128)(2,1)S(1)} %fusion.59) | copy-start | bytes 786436
  29.4 3.4 copy-start.2
  34.4 3.3 copy-start.3
  118.4 16.0 %copy-start.5 = (bf16[1024,2048]{1,0:T(8,128)(2,1)S(1)}, bf16[1024,2048]{1,0:T(8,128)(2,1)}, u32[]{:S(2)}) copy-start(bf16[1024,2048]{1,0:T(8,128)(2,1)} %broadcast_select_fusion.d_out) | copy-start | bytes 12582916
  131.0 3.4 copy-start.39
  147.1 377.1 %all-reduce.7.cloned.1.call-start = ((), (), s32[]{:S(2)}) async-start(), calls=%async_computation.1 | async-start | bytes 16777216 | tf_op jit(solution)/shard_map/psum | solution.py:535
  167.5 14.4 %copy-start.40 = (bf16[1024,2048]{1,0:T(8,128)(2,1)}, bf16[1024,2048]{1,0:T(8,128)(2,1)S(1)}, u32[]{:S(2)}) copy-start(bf16[1024,2048]{1,0:T(8,128)(2,1)S(1)} %get-tuple-element.68) | copy-start | bytes 12582916
  255.7 10.2 %slice-start = ((s8[8388608]{0:T(1024)(128)(4,1)}), s8[4194304]{0:T(1024)(128)(4,1)S(1)}, s32[]{:S(2)}) async-start(s8[8388608]{0:T(1024)(128)(4,1)} %bitcast.120), calls=%async_computation.3 | async-start | bytes 8388608
  260.5 5.4 slice-start.1
  260.6 12.7 %slice-start.2 = ((s8[8388608]{0:T(1024)(128)(4,1)}), s8[4194304]{0:T(1024)(128)(4,1)S(1)}, s32[]{:S(2)}) async-start(s8[8388608]{0:T(1024)(128)(4,1)} %bitcast.122), calls=%async_computation.5 | async-start | bytes 8388608
  266.0 5.9 copy-start.7
  266.0 7.4 %slice-start.3 = ((s8[8388608]{0:T(1024)(128)(4,1)}), s8[4194304]{0:T(1024)(128)(4,1)S(1)}, s32[]{:S(2)}) async-start(s8[8388608]{0:T(1024)(128)(4,1)} %bitcast.122), calls=%async_computation.6 | async-start | bytes 8388608
  268.5 4.9 copy-start.17
  278.0 5.0 copy-start.38
  278.7 10.1 %copy-start.9 = (bf16[512,4,128]{0,2,1:T(8,128)(2,1)}, bf16[512,4,128]{0,2,1:T(8,128)(2,1)S(1)}, u32[]{:S(2)}) copy-start(bf16[512,4,128]{0,2,1:T(8,128)(2,1)S(1)} %fusion.40) | copy-start | bytes 1572868
  280.1 8.7 %copy-start.24 = (bf16[1024,4,128]{0,2,1:T(8,128)(2,1)}, bf16[1024,4,128]{0,2,1:T(8,128)(2,1)S(1)}, u32[]{:S(2)}) copy-start(bf16[1024,4,128]{0,2,1:T(8,128)(2,1)S(1)} %pad_maximum_fusion.1) | copy-start | bytes 3145732
  290.4 2.2 copy-start.36
  290.4 3.5 copy-start.41
  305.3 21.4 %copy-start.35 = (bf16[2048]{0:T(1024)(128)(2,1)S(1)}, bf16[2048]{0:T(1024)(128)(2,1)}, u32[]{:S(2)}) copy-start(bf16[2048]{0:T(1024)(128)(2,1)} %param.32) | copy-start | bytes 12292
  305.3 23.7 %copy-start.21 = (bf16[2048,256]{1,0:T(8,128)(2,1)S(1)}, bf16[2048,256]{1,0:T(8,128)(2,1)}, u32[]{:S(2)}) copy-start(bf16[2048,256]{1,0:T(8,128)(2,1)} %param.23) | copy-start | bytes 3145732
  323.1 318.2 %all-reduce.9.cloned.1.call-start = ((), (), s32[]{:S(2)}) async-start(), calls=%async_computation.2 | async-start | bytes 10485760 | tf_op jit(solution)/shard_map/psum | solution.py:566
  352.6 161.8 %copy-start.23 = (bf16[1024,4,128]{0,2,1:T(8,128)(2,1)S(1)}, bf16[1024,4,128]{0,2,1:T(8,128)(2,1)}, u32[]{:S(2)}) copy-start(bf16[1024,4,128]{0,2,1:T(8,128)(2,1)} %copy-done.22) | copy-start | bytes 3145732
  511.8 8.6 %copy-start.25 = (bf16[1024,4,128]{0,2,1:T(8,128)(2,1)S(1)}, bf16[1024,4,128]{0,2,1:T(8,128)(2,1)}, u32[]{:S(2)}) copy-start(bf16[1024,4,128]{0,2,1:T(8,128)(2,1)} %copy-done.24) | copy-start | bytes 3145732
  514.4 6.0 copy-start.12
  520.4 3.9 copy-start.8
  520.4 3.9 copy-start.10
  520.4 33.3 %copy-start.26 = (f32[4,8,2048]{2,1,0:T(8,128)S(1)}, f32[4,8,2048]{2,1,0:T(8,128)}, u32[]{:S(2)}) copy-start(f32[4,8,2048]{2,1,0:T(8,128)} %get-tuple-element.36) | copy-start | bytes 786436
  520.4 33.4 %copy-start.27 = (f32[2,8,2048]{2,1,0:T(8,128)S(1)}, f32[2,8,2048]{2,1,0:T(8,128)}, u32[]{:S(2)}) copy-start(f32[2,8,2048]{2,1,0:T(8,128)} %get-tuple-element.35) | copy-start | bytes 393220
  641.3 7.2 %copy-start.18 = (bf16[512,2048]{1,0:T(8,128)(2,1)S(1)}, bf16[512,2048]{1,0:T(8,128)(2,1)}, u32[]{:S(2)}) copy-start(bf16[512,2048]{1,0:T(8,128)(2,1)} %get-tuple-element.44) | copy-start | bytes 6291460
  641.3 9.8 %copy-start.15 = (bf16[1024,2048]{1,0:T(8,128)(2,1)S(1)}, bf16[1024,2048]{1,0:T(8,128)(2,1)}, u32[]{:S(2)}) copy-start(bf16[1024,2048]{1,0:T(8,128)(2,1)} %get-tuple-element.85) | copy-start | bytes 12582916
  645.7 7.5 %copy-start.14 = (bf16[1024,2048]{1,0:T(8,128)(2,1)S(1)}, bf16[1024,2048]{1,0:T(8,128)(2,1)}, u32[]{:S(2)}) copy-start(bf16[1024,2048]{1,0:T(8,128)(2,1)} %get-tuple-element.86) | copy-start | bytes 12582916
  651.1 4.2 copy-start.1
  (1 other events, 1.0 us)
Sparse Core Ops, SparseCore 0:
  147.3 175.7 all-reduce.4
  325.4 175.6 all-reduce.6
  524.4 116.8 all-reduce.8

commit v2 on v1

--- a/solution.py
+++ b/solution.py
@@ -8,7 +8,6 @@
 from jax.sharding import PartitionSpec as P
 
 STRIP = 16
-SUBS = 2
 EPS = 1e-05
 
 
@@ -19,6 +18,10 @@
     for _ in range(count - 1):
         rest = [(bit,) + more for bit in (1, 0) for more in rest]
     return [(bit,) + more for bit in (1, 0) for more in rest]
+
+
+def pieces(unit):
+    return 2 if unit % (2 * STRIP) == 0 else 1
 
 
 def as_number(path):
@@ -66,11 +69,12 @@
     trees = [Tree(axis, size, number, rows) for number in (0, 1)]
     unit = trees[0].unit
     depth = trees[0].depth
-    sub_rows = unit // SUBS
+    subs = pieces(unit)
+    sub_rows = unit // subs
     sends = []
 
     def remote(tree, src, dst, kind, index, sub, level):
-        place = ((tree.number * 2 + kind) * (size - 1) + index) * SUBS + sub
+        place = ((tree.number * 2 + kind) * (size - 1) + index) * subs + sub
         copy = pltpu.make_async_remote_copy(
             src_ref=src,
             dst_ref=dst,
@@ -112,7 +116,7 @@
     for copy in copies:
         copy.start()
     for path in suffixes(depth - 1):
-        for sub in range(SUBS):
+        for sub in range(subs):
             for tree in trees:
                 copy = reduce_copy(tree, 0, path, sub)
                 copy.start()
@@ -128,7 +132,7 @@
             for load in loads:
                 load.wait()
         for path in suffixes(depth - 1 - level):
-            for sub in range(SUBS):
+            for sub in range(subs):
                 for tree in trees:
                     reduce_copy(tree, level, path, sub).wait_recv()
                     slot = tree.slot(level, path)
@@ -154,7 +158,7 @@
                         keep = pltpu.make_async_copy(
                             outbuf.at[tree.number, pl.ds(sub * sub_rows, sub_rows), :],
                             out.at[tree.rows(zero, sub, sub_rows), :],
-                            local_sem.at[2 + tree.number * SUBS + sub],
+                            local_sem.at[2 + tree.number * subs + sub],
                         )
                         keep.start()
                         stored.append(keep)
@@ -166,21 +170,19 @@
                         copy = reduce_copy(tree, level + 1, path[1:], sub)
                         copy.start()
                         sends.append(copy)
-            if not last:
                 yield
-        yield
     for level in reversed(range(depth)):
         for path in suffixes(depth - 1 - level):
             full = (0,) * level + (1,) + path
             sender = (0,) * (level + 1) + path
-            for sub in range(SUBS):
+            for sub in range(subs):
                 for tree in trees:
                     gather_copy(tree, level, sender, sub).wait_recv()
                     for back in reversed(range(level)):
                         copy = gather_copy(tree, back, full, sub)
                         copy.start()
                         sends.append(copy)
-        yield
+                yield
     for copy in sends:
         copy.wait_send()
     for copy in stored:
@@ -213,12 +215,13 @@
 def stream_scratch(size, rows, width):
     half = rows // 2
     unit = half // size
-    count = 2 * 2 * (size - 1) * SUBS
+    subs = pieces(unit)
+    count = 2 * 2 * (size - 1) * subs
     return [
         pltpu.VMEM((2, half // 2, width), jnp.bfloat16),
         pltpu.VMEM((2, size - 1, unit, width), jnp.bfloat16),
         pltpu.VMEM((2, unit, width), jnp.bfloat16),
-        pltpu.SemaphoreType.DMA((2 + 2 * SUBS,)),
+        pltpu.SemaphoreType.DMA((2 + 2 * subs,)),
         pltpu.SemaphoreType.DMA((count,)),
         pltpu.SemaphoreType.DMA((count,)),
     ]
@@ -335,11 +338,288 @@
     )(part, d_out, mid, gain)
 
 
-def last_kernel(size, rows, width, kv_rows, mlp, part, kv, tokens, mid, dmid, dbias, gain, result, grad, kv_out, sums, *scratch):
-    greet("tensor", size)
-    first, second, third = scratch[:6], scratch[6:12], scratch[12:18]
-    tok, load_sem = scratch[18:]
-    loads = load_rows("tensor", size, rows, tokens, tok, load_sem)
+def remote_copy(axis, target, src, dst, send_sem, recv_sem):
+    return pltpu.make_async_remote_copy(
+        src_ref=src,
+        dst_ref=dst,
+        send_sem=send_sem,
+        recv_sem=recv_sem,
+        device_id={axis: target},
+        device_id_type=pl.DeviceIdType.MESH,
+    )
+
+
+CHUNK = 64
+LAG = 3
+CORE_SEND, CORE_RECV, UP_SEND, LEFT_RECV, RIGHT_RECV, BACK_LEFT, BACK_RIGHT, BACK_RECV, TWIN_SEND, TWIN_RECV, KEEP, LOAD = range(12)
+
+
+def chain_scratch(shape):
+    half = shape[0] // 2
+    return [pltpu.VMEM((half, shape[1]), jnp.bfloat16)] * 4 + [pltpu.SemaphoreType.DMA((12, half // CHUNK))]
+
+
+def chain(devices, shape, array, out, own, twin, left, right, sems):
+    half = shape[0] // 2
+    count = half // CHUNK
+    length = devices // 2
+    me = lax.axis_index("dp")
+    core, place = me % 2, me // 2
+    other = me + 1 - 2 * core
+
+    def at(ref, chunk):
+        return ref.at[pl.ds(pl.multiple_of(chunk * CHUNK, CHUNK), CHUNK), :]
+
+    def part(ref, side, chunk):
+        return ref.at[pl.ds(pl.multiple_of(side * half + chunk * CHUNK, CHUNK), CHUNK), :]
+
+    def root(chunk):
+        return length // 2 - 1 + chunk % 2
+
+    def core_copy(chunk):
+        return remote_copy("dp", other, part(array, 1 - core, chunk), at(twin, chunk), sems.at[CORE_SEND, chunk], sems.at[CORE_RECV, chunk])
+
+    def load(chunk):
+        return pltpu.make_async_copy(part(array, core, chunk), at(own, chunk), sems.at[LOAD, chunk])
+
+    def to_right(chunk):
+        return remote_copy("dp", me + 2, at(own, chunk), at(left, chunk), sems.at[UP_SEND, chunk], sems.at[LEFT_RECV, chunk])
+
+    def to_left(chunk):
+        return remote_copy("dp", me - 2, at(own, chunk), at(right, chunk), sems.at[UP_SEND, chunk], sems.at[RIGHT_RECV, chunk])
+
+    def spread(chunk, src, step, send):
+        return remote_copy("dp", me + step, src, part(out, core, chunk), sems.at[send, chunk], sems.at[BACK_RECV, chunk])
+
+    def twin_copy(chunk, src):
+        return remote_copy("dp", other, src, part(out, core, chunk), sems.at[TWIN_SEND, chunk], sems.at[TWIN_RECV, chunk])
+
+    def twin_arrival(chunk):
+        there = part(out, 1 - core, chunk)
+        return remote_copy("dp", other, there, there, sems.at[TWIN_SEND, chunk], sems.at[TWIN_RECV, chunk])
+
+    def keep(chunk):
+        return pltpu.make_async_copy(at(own, chunk), part(out, core, chunk), sems.at[KEEP, chunk])
+
+    def add(chunk, terms):
+        def strip(step):
+            line = pl.ds(pl.multiple_of(chunk * CHUNK + step * STRIP, STRIP), STRIP)
+            total = own[line, :].astype(jnp.float32)
+            for term in terms:
+                total = total + term[line, :].astype(jnp.float32)
+            own[line, :] = total.astype(own.dtype)
+
+        pl.loop(0, CHUNK // STRIP)(strip)
+
+    def gather_up(chunk):
+        core_copy(chunk).wait_recv()
+        load(chunk).wait()
+        goal = root(chunk)
+        has_left = (place > 0) & (place <= goal)
+        has_right = (place < length - 1) & (place >= goal)
+
+        @pl.when(has_left)
+        def _():
+            to_right(chunk).wait_recv()
+
+        @pl.when(has_right)
+        def _():
+            to_left(chunk).wait_recv()
+
+        @pl.when(has_left & has_right)
+        def _():
+            add(chunk, [twin, left, right])
+
+        @pl.when(has_left & ~has_right)
+        def _():
+            add(chunk, [twin, left])
+
+        @pl.when(has_right & ~has_left)
+        def _():
+            add(chunk, [twin, right])
+
+        @pl.when(~has_right & ~has_left)
+        def _():
+            add(chunk, [twin])
+
+        @pl.when(place < goal)
+        def _():
+            to_right(chunk).start()
+
+        @pl.when(place > goal)
+        def _():
+            to_left(chunk).start()
+
+        @pl.when(place == goal)
+        def _():
+            @pl.when(place > 0)
+            def _():
+                spread(chunk, at(own, chunk), -2, BACK_LEFT).start()
+
+            @pl.when(place < length - 1)
+            def _():
+                spread(chunk, at(own, chunk), 2, BACK_RIGHT).start()
+
+            twin_copy(chunk, at(own, chunk)).start()
+            keep(chunk).start()
+
+    def hand_back(chunk):
+        goal = root(chunk)
+        here = part(out, core, chunk)
+
+        @pl.when(place < goal)
+        def _():
+            spread(chunk, here, 2, BACK_RIGHT).wait_recv()
+
+            @pl.when(place > 0)
+            def _():
+                spread(chunk, here, -2, BACK_LEFT).start()
+
+            twin_copy(chunk, here).start()
+
+        @pl.when(place > goal)
+        def _():
+            spread(chunk, here, -2, BACK_LEFT).wait_recv()
+
+            @pl.when(place < length - 1)
+            def _():
+                spread(chunk, here, 2, BACK_RIGHT).start()
+
+            twin_copy(chunk, here).start()
+
+    def finish(chunk):
+        goal = root(chunk)
+        here = part(out, core, chunk)
+        core_copy(chunk).wait_send()
+        twin_arrival(chunk).wait_recv()
+        twin_copy(chunk, here).wait_send()
+
+        @pl.when(place < goal)
+        def _():
+            to_right(chunk).wait_send()
+
+        @pl.when(place > goal)
+        def _():
+            to_left(chunk).wait_send()
+
+        @pl.when((place <= goal) & (place > 0))
+        def _():
+            spread(chunk, here, -2, BACK_LEFT).wait_send()
+
+        @pl.when((place >= goal) & (place < length - 1))
+        def _():
+            spread(chunk, here, 2, BACK_RIGHT).wait_send()
+
+        @pl.when(place == goal)
+        def _():
+            keep(chunk).wait()
+
+    @pl.loop(0, count)
+    def _(chunk):
+        core_copy(chunk).start()
+        load(chunk).start()
+
+    yield
+    groups = count // 2
+    for step in range(groups + LAG):
+        if step < groups:
+
+            @pl.loop(2 * step, 2 * step + 2)
+            def _(chunk):
+                gather_up(chunk)
+
+        if step >= LAG:
+
+            @pl.loop(2 * (step - LAG), 2 * (step - LAG) + 2)
+            def _(chunk):
+                hand_back(chunk)
+
+        yield
+
+    @pl.loop(0, count)
+    def _(chunk):
+        finish(chunk)
+
+
+def small_scratch(size, devices, width):
+    return [
+        pltpu.VMEM((size, 8, width), jnp.float32),
+        pltpu.VMEM((devices, 16, width), jnp.float32),
+        pltpu.SemaphoreType.DMA((2, size)),
+        pltpu.SemaphoreType.DMA((2, devices)),
+    ]
+
+
+def small_sum(size, devices, given, sums, out, near, far, near_sem, far_sem):
+    def exchange(axis, members, slots, sem):
+        me = lax.axis_index(axis)
+        copies = []
+        for step in range(1, members):
+            target = (me + step) % members
+            copy = remote_copy(axis, target, slots.at[me], slots.at[me], sem.at[0, target], sem.at[1, me])
+            copy.start()
+            copies.append(copy)
+        for step in range(1, members):
+            source = (me + step) % members
+            remote_copy(axis, source, slots.at[source], slots.at[source], sem.at[0, source], sem.at[1, source]).wait_recv()
+        for copy in copies:
+            copy.wait_send()
+
+    mine = given[0:8, :]
+    row = lax.broadcasted_iota(jnp.int32, mine.shape, 0)
+    mine = jnp.where(row == 0, jnp.sum(sums[0], axis=0, keepdims=True), mine)
+    mine = jnp.where(row == 1, jnp.sum(sums[1], axis=0, keepdims=True), mine)
+    near[lax.axis_index("tensor")] = mine
+    exchange("tensor", size, near, near_sem)
+    total = near[0]
+    for member in range(1, size):
+        total = total + near[member]
+    me = lax.axis_index("dp")
+    far[me, 0:8, :] = total
+    far[me, 8:16, :] = given[8:16, :]
+    exchange("dp", devices, far, far_sem)
+    total = far[0]
+    for member in range(1, devices):
+        total = total + far[member]
+    out[...] = total
+
+
+def one_after_another(*parts):
+    for part in parts:
+        yield from part
+
+
+def greet_all(sizes):
+    barrier = pltpu.get_barrier_semaphore()
+    total = 0
+    for axis, size in sizes:
+        me = lax.axis_index(axis)
+        for step in range(1, size):
+            pl.semaphore_signal(
+                barrier, inc=1, device_id={axis: (me + step) % size}, device_id_type=pl.DeviceIdType.MESH
+            )
+        total += size - 1
+    pl.semaphore_wait(barrier, total)
+
+
+def later(call):
+    call()
+    yield
+
+
+def last_kernel(size, devices, shapes, mlp, part, kv, tokens, mid, dmid, dbias, gain, small, *rest):
+    wide, kv_shape, summed = shapes[0], shapes[1], shapes[2:]
+    count = len(summed)
+    arrays, rest = rest[:count], rest[count:]
+    result, grad, kv_sum, small_out, rest = *rest[:4], rest[4:]
+    outs, rest = rest[:count], rest[count:]
+    kv_out, rest = rest[0], rest[1:]
+    first, second, third, rest = rest[:6], rest[6:12], rest[12:18], rest[18:]
+    tok, load_sem, sums, rest = *rest[:3], rest[3:]
+    near, rest = rest[:4], rest[4:]
+    chains = [rest[5 * place : 5 * place + 5] for place in range(count + 1)]
+    greet_all((("tensor", size), ("dp", devices)))
+    loads = load_rows("tensor", size, wide[0], tokens, tok, load_sem)
     sums[...] = jnp.zeros_like(sums)
 
     def finish_result(total, number, here, line):
@@ -354,35 +634,62 @@
     def finish_kv(total, number, here, line):
         return total.astype(jnp.bfloat16)
 
+    def small_part():
+        small_sum(size, devices, small, sums, small_out, *near)
+
     run_together(
         [
-            stream("tensor", size, (rows, width), mlp, result, *first, finish_result),
-            stream("tensor", size, (rows, width), part, grad, *second, finish_grad, loads),
-            stream("tensor", size, (kv_rows, width), kv, kv_out, *third, finish_kv),
+            one_after_another(
+                *(
+                    chain(devices, shape, array, out, *scratch)
+                    for shape, array, out, scratch in zip(summed, arrays, outs, chains)
+                )
+            ),
+            one_after_another(
+                stream("tensor", size, kv_shape, kv, kv_out, *third, finish_kv),
+                chain(devices, kv_shape, kv_out, kv_sum, *chains[-1]),
+            ),
+            one_after_another(
+                stream("tensor", size, wide, part, grad, *second, finish_grad, loads),
+                later(small_part),
+            ),
+            stream("tensor", size, wide, mlp, result, *first, finish_result),
         ]
     )
 
 
-def reduce_last(size, mlp, part, kv, tokens, mid, dmid, dbias, gain):
+def reduce_last(size, devices, mlp, part, kv, tokens, mid, dmid, dbias, gain, small, arrays):
     rows, width = part.shape
     unit = rows // 2 // size
-    kv_rows = kv.shape[0]
-    return pl.pallas_call(
-        functools.partial(last_kernel, size, rows, width, kv_rows),
+    shapes = (part.shape, kv.shape) + tuple(array.shape for array in arrays)
+    low = jnp.bfloat16
+    outs = pl.pallas_call(
+        functools.partial(last_kernel, size, devices, shapes),
         out_shape=(
-            jax.ShapeDtypeStruct((rows, width), jnp.bfloat16),
-            jax.ShapeDtypeStruct((rows, width), jnp.bfloat16),
-            jax.ShapeDtypeStruct((kv_rows, width), jnp.bfloat16),
-            jax.ShapeDtypeStruct((2, 8, width), jnp.float32),
+            jax.ShapeDtypeStruct((rows, width), low),
+            jax.ShapeDtypeStruct((rows, width), low),
+            jax.ShapeDtypeStruct(kv.shape, low),
+            jax.ShapeDtypeStruct(small.shape, jnp.float32),
+            *(jax.ShapeDtypeStruct(array.shape, low) for array in arrays),
+            jax.ShapeDtypeStruct(kv.shape, low),
         ),
-        in_specs=[HBM, HBM, HBM, HBM, VMEM, VMEM, VMEM, VMEM],
-        out_specs=(HBM, HBM, HBM, VMEM),
+        in_specs=[HBM] * 4 + [VMEM] * 5 + [HBM] * len(arrays),
+        out_specs=(HBM, HBM, HBM, VMEM) + (HBM,) * len(arrays) + (HBM,),
         scratch_shapes=stream_scratch(size, rows, width) * 2
-        + stream_scratch(size, kv_rows, width)
-        + [pltpu.VMEM((2, unit, width), jnp.bfloat16), pltpu.SemaphoreType.DMA((2,))],
-        compiler_params=pltpu.CompilerParams(collective_id=3, has_side_effects=True),
+        + stream_scratch(size, kv.shape[0], width)
+        + [
+            pltpu.VMEM((2, unit, width), low),
+            pltpu.SemaphoreType.DMA((2,)),
+            pltpu.VMEM((2, 8, width), jnp.float32),
+        ]
+        + small_scratch(size, devices, width)
+        + [one for shape in shapes[2:] + (kv.shape,) for one in chain_scratch(shape)],
+        compiler_params=pltpu.CompilerParams(
+            collective_id=3, has_side_effects=True, vmem_limit_bytes=60 * 1024 * 1024
+        ),
         name="reduce_last",
-    )(mlp, part, kv, tokens, mid, dmid, dbias, gain)
+    )(mlp, part, kv, tokens, mid, dmid, dbias, gain, small, *arrays)
+    return outs[:4], outs[4 : 4 + len(arrays)]
 
 
 def layer_norm(values, gain, shift):
@@ -478,6 +785,7 @@
 
 def local(
     size,
+    devices,
     tokens,
     lengths,
     norm1_gain,
@@ -531,8 +839,6 @@
     back2 = contract_cols(grad_pre, up_weight).astype(jnp.bfloat16)
     middle_low, dmid, sums2 = reduce_back(size, back2, d_out, mid, row(norm2_gain))
     grad_up = contract_rows(hidden2, grad_pre).astype(jnp.bfloat16)
-    grad_up, grad_down = lax.optimization_barrier((grad_up, grad_down))
-    grad_up = lax.psum(grad_up, "dp")
     grad_upbias = jnp.sum(grad_pre.astype(wide), axis=0)
     mlp_terms = jnp.dot(activated, down_weight, preferred_element_type=wide).astype(jnp.bfloat16)
 
@@ -545,43 +851,55 @@
     grad_queries = query_part.reshape(slot_len, heads_here * head_dim)
     grad_kv_rows = jnp.concatenate([key_part, value_part], axis=1).astype(jnp.bfloat16)
     grad_qbias = jnp.sum(grad_queries.astype(wide), axis=0)
-    grad_query = contract_rows(hidden1, grad_queries).astype(jnp.bfloat16)
-    grad_keyval = contract_rows(hidden1, grad_kv_rows).astype(jnp.bfloat16)
+    grad_query = contract_rows(grad_queries, hidden1).astype(jnp.bfloat16)
+    grad_keyval = contract_rows(grad_kv_rows, hidden1).astype(jnp.bfloat16)
     grad_vbias = jnp.sum(grad_kv_rows[:, head_dim:].astype(wide), axis=0)
     back1 = (
         contract_cols(grad_queries, query_weight) + contract_cols(grad_kv_rows, keyval_weight)
     ).astype(jnp.bfloat16)
-    result, grad_tokens, kv_sum, sums1 = reduce_last(
+
+    def padded(vector):
+        return jnp.pad(vector, (0, width - vector.shape[0])).reshape(1, width)
+
+    small = jnp.concatenate(
+        [
+            jnp.zeros((2, width), wide),
+            jnp.sum(sums2, axis=1),
+            padded(grad_vbias),
+            jnp.zeros((1, width), wide),
+            padded(grad_qbias),
+            padded(grad_upbias),
+            jnp.zeros((6, width), wide),
+        ]
+    )
+    (result, grad_tokens, kv_sum, small), (grad_up, grad_proj, grad_query) = reduce_last(
         size,
+        devices,
         mlp_terms,
         back1,
-        grad_keyval.reshape(-1, width),
+        grad_keyval,
         tokens,
         mid,
         dmid,
         row(down_bias),
         row(norm1_gain),
-    )
-    grad_query, grad_up = lax.optimization_barrier((grad_query, grad_up))
-    grad_query, grad_proj, kv_sum = lax.psum((grad_query, grad_proj, kv_sum), "dp")
-    shared = jnp.concatenate(
-        [jnp.sum(sums1, axis=1).reshape(-1), jnp.sum(sums2, axis=1).reshape(-1), grad_vbias]
-    )
-    shared = lax.psum(shared, ("dp", "tensor"))
-    split = lax.psum(jnp.concatenate([grad_qbias, grad_upbias]), "dp")
-    grad_qbias, grad_upbias = split[: grad_qbias.shape[0]], split[grad_qbias.shape[0] :]
+        small,
+        (grad_up, grad_proj, grad_query),
+    )
     grad_gain1, grad_shift1, grad_gain2, grad_shift2, grad_pbias, grad_dnbias = (
-        shared[place * width : (place + 1) * width] for place in range(6)
-    )
-    grad_vbias = shared[6 * width :]
+        small[place] for place in range(6)
+    )
+    grad_vbias = small[6, :head_dim]
+    grad_qbias = small[8, : query_bias.shape[0]]
+    grad_upbias = small[9, : up_bias.shape[0]]
     return (
         result,
         grad_tokens,
         grad_gain1,
         grad_shift1,
-        grad_query.astype(wide),
+        grad_query.T.astype(wide),
         grad_qbias,
-        kv_sum.reshape(keyval_weight.shape).astype(wide),
+        kv_sum.T.astype(wide),
         grad_vbias,
         grad_proj.astype(wide),
         grad_pbias,
@@ -632,4 +950,4 @@
         P("tensor", None),
         P(),
     )
-    return jax.shard_map(functools.partial(local, mesh.shape["tensor"]), mesh=mesh, in_specs=in_specs, out_specs=out_specs, check_vma=False)
+    return jax.shard_map(functools.partial(local, mesh.shape["tensor"], mesh.shape["dp"]), mesh=mesh, in_specs=in_specs, out_specs=out_specs, check_vma=False)

time: 666 us -> 839 us (1.26)
  Pallas kernels: 308 us -> 589 us
  blocking collectives: 66.5 us -> 0 us
  waiting for transfers between devices: 42.2 us -> 0.02 us
  matrix products: 153 us -> 141 us
    pallas_call x1, Pallas kernels: 159 us -> 440 us  [reduce_last(): pl.pallas_call(functools.partial(last_kernel, size, devices, shapes), out...]
    psum x2 -> x0, blocking collectives: 66.5 us -> none  [the longest x1 38.4 us: local(): shared = lax.psum(shared, ('dp', 'tensor'))]
    psum x2 -> x0, waiting for transfers between devices: 24.4 us -> none  [the longest x1 24.4 us: local(): lax.psum((grad_query, grad_proj, kv_sum), 'dp')]
    psum x1, waiting for transfers between devices: 17.8 us -> 0.01 us  [local(): grad_down = lax.psum(grad_down, 'dp')]
    dot_general x5, matrix products: 52.7 us -> 41.5 us  [contract_cols(): lax.dot_general(left, right, (((1,), (1,)), ((), ())), preferred_element_...]
    unnamed x96 -> x88, local copies, waits for them, and re-layouts: 11.9 us -> 19.3 us
  transfers between devices with their start and end apart: 3 -> 1, of which waited for: 2 -> 0; matrix products, arithmetic and copies ran while one was open for 23% -> 18% of each run, Pallas kernels for 35% -> 62%
where the time goes in v2:
time: 839 us; the launch traced here: 831 us
  Pallas kernels  589 us (70%)
  matrix products  141 us (17%)
  other arithmetic  59.5 us (7%)
  local copies, waits for them, and re-layouts  25.9 us (3%)
  between operations  15.8 us (2%)
    pallas_call x1, Pallas kernels, reduce_last(): pl.pallas_call(functools.partial(last_kernel, size, devices, shapes), out...  440 us
    pallas_call x1, Pallas kernels, reduce_middle(): pl.pallas_call(functools.partial(middle_kernel, size, rows, width), out_s...  75.3 us
    pallas_call x1, Pallas kernels, reduce_back(): pl.pallas_call(functools.partial(back_kernel, size, rows, width), out_sha...  73.8 us
    dot_general x5, matrix products, contract_cols(): lax.dot_general(left, right, (((1,), (1,)), ((), ())), preferred_element_...  41.5 us
    dot_general x5, matrix products, contract_rows(): lax.dot_general(left, right, (((0,), (0,)), ((), ())), preferred_element_...  38.4 us
    unnamed x88, local copies, waits for them, and re-layouts  19.3 us
  transfers between devices with their start and end apart: 1, of which 0 were waited for; matrix products, arithmetic and copies ran while one was open for 18% of the time, Pallas kernels for 62%

profile of v2, /device:TPU:0, one launch (start us, length us, event | category | flops | bytes accessed | tf_op | source)
XLA Modules:
  0.0 831.5 jit_solution(10378723964466816687)
XLA Ops:
  10.0 3.0 convert_reduce_fusion
  13.0 3.4 fusion.2
  18.3 2.0 fusion.5
  20.4 2.5 add_convert_fusion.1
  25.8 2.4 broadcast_select_fusion.d_out
  28.2 1.6 fusion.66
  31.0 1.7 fusion.48
  33.2 1.6 fusion.67
  36.0 1.9 fusion.47
  38.3 4.4 convolution_convert_fusion.4.part
  42.7 75.3 %reduce_middle.1 = (bf16[1024,2048]{1,0:T(8,128)(2,1)}, f32[256,2048]{1,0:T(8,128)}) custom-call(bf16[1024,2048]{1,0:T(8,128)(2,1)} %convolution_convert_fusion.4.part, bf16[1024,2048]{1,0:T(8,128)(2,1)} %tokens.3, f32[1,2048]{1,0:T(1,128)} %bitcast.152, f32[1,2048]{1,0:T(1,128)} %bitcast.150, f32[1,2048]{1,0:T(1,128)} %bitcast.154), custom_call_target="tpu_custom_call" | custom-call | tf_op jit(solution)/shard_map/reduce_middle/pallas_call | solution.py:286
  118.0 12.6 %fusion.73 = f32[1024,2048]{1,0:T(8,128)S(1)} fusion(bf16[1024,2048]{1,0:T(8,128)(2,1)} %get-tuple-element.28, bf16[2048,2048]{1,0:T(8,128)(2,1)} %param.29), kind=kOutput, calls=%fused_computation.115 | convolution fusion | flops 8589934592 | bytes 20971520 | tf_op jit(solution)/shard_map/dot_general | solution.py:830
  130.6 3.4 copy-done.37
  134.0 12.7 %convolution_convert_fusion = bf16[2048,2048]{1,0:T(8,128)(2,1)} fusion(bf16[1024,2048]{1,0:T(8,128)(2,1)S(1)} %copy-done.4, f32[1024,2048]{1,0:T(8,128)S(1)} %fusion.73, f32[2048]{0:T(1024)S(1)} %convert_element_type.158), kind=kOutput, calls=%fused_computation.44 | convolution fusion | flops 8615100416 | bytes 20979712 | tf_op jit(solution)/shard_map/dot_general | solution.py:710
  146.8 20.5 %convert_reduce_fusion.1 = (f32[2048]{0:T(1024)S(1)}, bf16[1024,2048]{1,0:T(8,128)(2,1)S(1)}) fusion(bf16[1024,2048]{1,0:T(8,128)(2,1)} %broadcast_select_fusion.d_out, bf16[2048,2048]{1,0:T(8,128)(2,1)} %param.31, f32[1024,2048]{1,0:T(8,128)} %copy-done.37, f32[2048]{0:T(1024)S(1)} %convert_element_type.158), kind=kOutput, calls=%fused_computation.35 | convolution fusion | flops 8650749952 | bytes 25182208 | tf_op jit(solution)/shard_map/dot_general | solution.py:716
  167.3 11.5 %convolution_convert_fusion.1.rest_0_ = bf16[2048,2048]{1,0:T(8,128)(2,1)} fusion(bf16[1024,2048]{1,0:T(8,128)(2,1)S(1)} %copy-done.33, bf16[1024,2048]{1,0:T(8,128)(2,1)S(1)} %get-tuple-element.80), kind=kOutput, calls=%fused_computation.45 | convolution fusion | flops 8594128896 | bytes 16777216 | tf_op jit(solution)/shard_map/dot_general | solution.py:710
  178.8 12.9 %convolution_convert_fusion.2.part = bf16[1024,2048]{1,0:T(8,128)(2,1)} fusion(bf16[1024,2048]{1,0:T(8,128)(2,1)S(1)} %get-tuple-element.80, bf16[2048,2048]{1,0:T(8,128)(2,1)} %param.29), kind=kOutput, calls=%fused_computation.58 | convolution fusion | flops 8592031744 | bytes 16777216 | tf_op jit(solution)/shard_map/dot_general | solution.py:716
  191.7 73.8 %reduce_back.1 = (bf16[1024,2048]{1,0:T(8,128)(2,1)}, f32[256,2048]{1,0:T(8,128)}, f32[4,8,2048]{2,1,0:T(8,128)}) custom-call(bf16[1024,2048]{1,0:T(8,128)(2,1)} %convolution_convert_fusion.2.part, bf16[1024,2048]{1,0:T(8,128)(2,1)} %broadcast_select_fusion.d_out, f32[256,2048]{1,0:T(8,128)} %get-tuple-element.29.mid, f32[1,2048]{1,0:T(1,128)} %bitcast.151), custom_call_target="tpu_custom_call" | custom-call | tf_op jit(solution)/shard_map/reduce_back/pallas_call | solution.py:325
  265.6 6.0 convolution_convert_fusion.6.rest_1_
  271.6 2.4 convolution_convert_fusion.8
  274.9 1.9 fusion.15
  276.8 2.7 fusion.17
  279.5 3.4 convolution_bitcast_fusion
  282.9 2.6 fusion.39
  285.5 2.3 fusion.41
  287.8 1.9 fusion.18
  289.8 2.4 fusion.20
  292.2 1.8 fusion.40
  294.0 1.4 pad_maximum_fusion.1
  295.4 5.9 convolution_convert_fusion.5.rest_2_
  301.3 2.4 fusion.74
  303.8 1.6 convert_reduce_fusion.3
  305.4 1.5 fusion.54
  307.0 3.4 add_convert_fusion.part
  310.3 2.3 convolution_convert_fusion.7.kv
  314.9 16.3 %convolution_convert_fusion.3.mlp = bf16[1024,2048]{1,0:T(8,128)(2,1)} fusion(bf16[2048,2048]{1,0:T(8,128)(2,1)} %param.31, f32[1024,2048]{1,0:T(8,128)} %copy-done.37, f32[2048]{0:T(1024)S(1)} %convert_element_type.158), kind=kOutput, calls=%fused_computation.59 | convolution fusion | flops 8613003264 | bytes 20979712 | tf_op jit(solution)/shard_map/dot_general | solution.py:843
  331.2 440.4 %reduce_last.1 = (bf16[1024,2048]{1,0:T(8,128)(2,1)}, bf16[1024,2048]{1,0:T(8,128)(2,1)}, bf16[256,2048]{1,0:T(8,128)(2,1)}, f32[16,2048]{1,0:T(8,128)}, bf16[20...) custom-call(bf16[1024,2048]{1,0:T(8,128)(2,1)} %convolution_convert_fusi, ...), custom_call_target="tpu_custom_call" | custom-call | tf_op jit(solution)/shard_map/reduce_last/pallas_call | solution.py:666
  772.9 2.8 convert_bitcast_fusion.1
  775.7 2.9 copy.52
  778.6 4.1 convert_bitcast_fusion
  782.7 5.5 copy.51
  788.2 4.1 convert_element_type.186
  792.3 11.7 %convert_element_type.187 = f32[2048,2048]{1,0:T(8,128)} convert(bf16[2048,2048]{1,0:T(8,128)(2,1)} %get-tuple-element.39) | non-fusion elementwise | flops 4194304 | bytes 25165824 | tf_op jit(solution)/shard_map/convert_element_type | solution.py:908
  805.2 1.7 fusion.65
  806.9 11.8 %convert_element_type.189 = f32[2048,2048]{1,0:T(8,128)} convert(bf16[2048,2048]{1,0:T(8,128)(2,1)} %all-reduce.4.cloned.1.call-done) | non-fusion elementwise | flops 4194304 | bytes 25165824 | tf_op jit(solution)/shard_map/convert_element_type | solution.py:910
  818.8 2.1 copy.81
  820.9 1.6 copy-done.15
  822.5 2.0 copy.82
  (120 shorter events, 15.7 us)
Async XLA Ops:
  7.2 31.1 %copy-start = (bf16[512,2048]{1,0:T(8,128)(2,1)S(1)}, bf16[512,2048]{1,0:T(8,128)(2,1)}, u32[]{:S(2)}) copy-start(bf16[512,2048]{1,0:T(8,128)(2,1)} %param.25) | copy-start | bytes 6291460
  7.2 9.2 %copy-start.26 = (bf16[2048]{0:T(1024)(128)(2,1)S(1)}, bf16[2048]{0:T(1024)(128)(2,1)}, u32[]{:S(2)}) copy-start(bf16[2048]{0:T(1024)(128)(2,1)} %param.30) | copy-start | bytes 12292
  7.2 9.2 %copy-start.27 = (bf16[2048]{0:T(1024)(128)(2,1)S(1)}, bf16[2048]{0:T(1024)(128)(2,1)}, u32[]{:S(2)}) copy-start(bf16[2048]{0:T(1024)(128)(2,1)} %param.19) | copy-start | bytes 12292
  7.2 9.2 %copy-start.28 = (bf16[2048]{0:T(1024)(128)(2,1)S(1)}, bf16[2048]{0:T(1024)(128)(2,1)}, u32[]{:S(2)}) copy-start(bf16[2048]{0:T(1024)(128)(2,1)} %param.20) | copy-start | bytes 12292
  7.2 9.3 %copy-start.29 = (bf16[2048]{0:T(1024)(128)(2,1)S(1)}, bf16[2048]{0:T(1024)(128)(2,1)}, u32[]{:S(2)}) copy-start(bf16[2048]{0:T(1024)(128)(2,1)} %param.26) | copy-start | bytes 12292
  7.2 9.9 %copy-start.30 = (bf16[2048]{0:T(1024)(128)(2,1)S(1)}, bf16[2048]{0:T(1024)(128)(2,1)}, u32[]{:S(2)}) copy-start(bf16[2048]{0:T(1024)(128)(2,1)} %param.27) | copy-start | bytes 12292
  7.2 10.5 %copy-start.31 = (bf16[2048]{0:T(1024)(128)(2,1)S(1)}, bf16[2048]{0:T(1024)(128)(2,1)}, u32[]{:S(2)}) copy-start(bf16[2048]{0:T(1024)(128)(2,1)} %param.28) | copy-start | bytes 12292
  7.3 799.7 %all-reduce.4.cloned.1.call-start = ((), (), s32[]{:S(2)}) async-start(), calls=%async_computation | async-start | bytes 16777216 | tf_op jit(solution)/shard_map/psum | solution.py:835
  7.3 11.0 %copy-start.3 = (bf16[1024,2048]{1,0:T(8,128)(2,1)S(1)}, bf16[1024,2048]{1,0:T(8,128)(2,1)}, u32[]{:S(2)}) copy-start(bf16[1024,2048]{1,0:T(8,128)(2,1)} %tokens.3) | copy-start | bytes 12582916
  10.0 10.3 %copy-start.35 = (bf16[2048,512]{1,0:T(8,128)(2,1)S(1)}, bf16[2048,512]{1,0:T(8,128)(2,1)}, u32[]{:S(2)}) copy-start(bf16[2048,512]{1,0:T(8,128)(2,1)} %param.21) | copy-start | bytes 6291460
  16.5 1.8 copy-start.25
  20.4 2.6 copy-start.12
  20.4 2.6 copy-start.21
  22.8 2.9 copy-start.14
  23.0 5.3 copy-start.20
  23.0 10.3 %copy-start.6 = (bf16[512,512]{0,1:T(8,128)(2,1)}, bf16[512,512]{0,1:T(8,128)(2,1)S(1)}, u32[]{:S(2)}) copy-start(bf16[512,512]{0,1:T(8,128)(2,1)S(1)} %get-tuple-element.58) | copy-start | bytes 1572868
  24.2 9.0 %copy-start.5 = (f32[1024,256]{1,0:T(8,128)}, f32[1024,256]{1,0:T(8,128)S(1)}, u32[]{:S(2)}) copy-start(f32[1024,256]{1,0:T(8,128)S(1)} %fusion.72) | copy-start | bytes 3145732
  28.2 246.7 %copy-start.18 = (bf16[1024,128,1]{1,0,2:T(8,128)(2,1)}, bf16[1024,128,1]{1,0,2:T(8,128)(2,1)S(1)}, u32[]{:S(2)}) copy-start(bf16[1024,128,1]{1,0,2:T(8,128)(2,1)S(1)} %fusion.59) | copy-start | bytes 786436
  29.8 3.4 copy-start.1
  34.9 3.3 copy-start.2
  118.0 16.0 %copy-start.4 = (bf16[1024,2048]{1,0:T(8,128)(2,1)S(1)}, bf16[1024,2048]{1,0:T(8,128)(2,1)}, u32[]{:S(2)}) copy-start(bf16[1024,2048]{1,0:T(8,128)(2,1)} %broadcast_select_fusion.d_out) | copy-start | bytes 12582916
  130.6 3.4 copy-start.37
  146.7 20.5 %copy-start.33 = (bf16[1024,2048]{1,0:T(8,128)(2,1)S(1)}, bf16[1024,2048]{1,0:T(8,128)(2,1)}, u32[]{:S(2)}) copy-start(bf16[1024,2048]{1,0:T(8,128)(2,1)} %get-tuple-element.28) | copy-start | bytes 12582916
  265.5 6.1 copy-start.34
  265.5 9.3 %slice-start = ((s8[8388608]{0:T(1024)(128)(4,1)}), s8[4194304]{0:T(1024)(128)(4,1)S(1)}, s32[]{:S(2)}) async-start(s8[8388608]{0:T(1024)(128)(4,1)} %bitcast.133), calls=%async_computation.1 | async-start | bytes 8388608
  271.6 3.3 slice-start.1
  274.9 10.6 %slice-start.2 = ((s8[8388608]{0:T(1024)(128)(4,1)}), s8[4194304]{0:T(1024)(128)(4,1)S(1)}, s32[]{:S(2)}) async-start(s8[8388608]{0:T(1024)(128)(4,1)} %bitcast.135), calls=%async_computation.3 | async-start | bytes 8388608
  276.8 8.6 %slice-start.3 = ((s8[8388608]{0:T(1024)(128)(4,1)}), s8[4194304]{0:T(1024)(128)(4,1)S(1)}, s32[]{:S(2)}) async-start(s8[8388608]{0:T(1024)(128)(4,1)} %bitcast.135), calls=%async_computation.4 | async-start | bytes 8388608
  279.5 6.0 copy-start.8
  285.5 2.4 copy-start.19
  294.0 1.4 copy-start.10
  294.0 7.3 copy-start.36
  301.3 2.4 copy-start.17
  303.7 1.7 copy-start.7
  303.7 1.7 copy-start.23
  303.7 3.2 copy-start.22
  306.9 3.4 copy-start.13
  306.9 5.7 copy-start.32
  306.9 6.2 copy-start.24
  306.9 6.3 copy-start.9
  306.9 6.3 copy-start.11
  806.9 11.8 %copy-start.16 = (bf16[1024,2048]{1,0:T(8,128)(2,1)S(1)}, bf16[1024,2048]{1,0:T(8,128)(2,1)}, u32[]{:S(2)}) copy-start(bf16[1024,2048]{1,0:T(8,128)(2,1)} %get-tuple-element.97) | copy-start | bytes 12582916
  818.7 3.7 copy-start.15
Sparse Core Ops, SparseCore 0:
  146.8 175.7 all-reduce.3

commit v3 on v2

--- a/solution.py
+++ b/solution.py
@@ -123,7 +123,7 @@
                 sends.append(copy)
     for copy in copies:
         copy.wait()
-    yield
+    yield True
     zero = (0,) * depth
     stored = []
     for level in range(depth):
@@ -131,7 +131,8 @@
         if last:
             for load in loads:
                 load.wait()
-        for path in suffixes(depth - 1 - level):
+        paths = suffixes(depth - 1 - level)
+        for path in paths:
             for sub in range(subs):
                 for tree in trees:
                     reduce_copy(tree, level, path, sub).wait_recv()
@@ -170,9 +171,10 @@
                         copy = reduce_copy(tree, level + 1, path[1:], sub)
                         copy.start()
                         sends.append(copy)
-                yield
+                yield path == paths[-1] and sub == subs - 1
     for level in reversed(range(depth)):
-        for path in suffixes(depth - 1 - level):
+        paths = suffixes(depth - 1 - level)
+        for path in paths:
             full = (0,) * level + (1,) + path
             sender = (0,) * (level + 1) + path
             for sub in range(subs):
@@ -182,7 +184,7 @@
                         copy = gather_copy(tree, back, full, sub)
                         copy.start()
                         sends.append(copy)
-                yield
+                yield path == paths[-1] and sub == subs - 1
     for copy in sends:
         copy.wait_send()
     for copy in stored:
@@ -349,38 +351,34 @@
     )
 
 
-CHUNK = 64
-LAG = 3
+CHUNK = 32
+SKEW = 1
 CORE_SEND, CORE_RECV, UP_SEND, LEFT_RECV, RIGHT_RECV, BACK_LEFT, BACK_RIGHT, BACK_RECV, TWIN_SEND, TWIN_RECV, KEEP, LOAD = range(12)
 
 
-def chain_scratch(shape):
-    half = shape[0] // 2
-    return [pltpu.VMEM((half, shape[1]), jnp.bfloat16)] * 4 + [pltpu.SemaphoreType.DMA((12, half // CHUNK))]
-
-
-def chain(devices, shape, array, out, own, twin, left, right, sems):
-    half = shape[0] // 2
-    count = half // CHUNK
+def chain_scratch(rows, width):
+    half = rows // 2
+    return [pltpu.VMEM((half, width), jnp.bfloat16)] * 4 + [pltpu.SemaphoreType.DMA((12, half // CHUNK))]
+
+
+def chain(devices, sources, out, own, twin, left, right, sems):
     length = devices // 2
     me = lax.axis_index("dp")
     core, place = me % 2, me // 2
     other = me + 1 - 2 * core
+    deepest = length // 2
 
     def at(ref, chunk):
         return ref.at[pl.ds(pl.multiple_of(chunk * CHUNK, CHUNK), CHUNK), :]
 
     def part(ref, side, chunk):
-        return ref.at[pl.ds(pl.multiple_of(side * half + chunk * CHUNK, CHUNK), CHUNK), :]
-
-    def root(chunk):
-        return length // 2 - 1 + chunk % 2
-
-    def core_copy(chunk):
-        return remote_copy("dp", other, part(array, 1 - core, chunk), at(twin, chunk), sems.at[CORE_SEND, chunk], sems.at[CORE_RECV, chunk])
-
-    def load(chunk):
-        return pltpu.make_async_copy(part(array, core, chunk), at(own, chunk), sems.at[LOAD, chunk])
+        return ref.at[pl.ds(pl.multiple_of((2 * chunk + side) * CHUNK, CHUNK), CHUNK), :]
+
+    def core_copy(source, chunk, first):
+        return remote_copy("dp", other, part(source, 1 - core, chunk - first), at(twin, chunk), sems.at[CORE_SEND, chunk], sems.at[CORE_RECV, chunk])
+
+    def load(source, chunk, first):
+        return pltpu.make_async_copy(part(source, core, chunk - first), at(own, chunk), sems.at[LOAD, chunk])
 
     def to_right(chunk):
         return remote_copy("dp", me + 2, at(own, chunk), at(left, chunk), sems.at[UP_SEND, chunk], sems.at[LEFT_RECV, chunk])
@@ -411,36 +409,31 @@
 
         pl.loop(0, CHUNK // STRIP)(strip)
 
-    def gather_up(chunk):
-        core_copy(chunk).wait_recv()
-        load(chunk).wait()
-        goal = root(chunk)
+    def gather_up(chunk, goal):
+        core_copy(out, chunk, 0).wait_recv()
+        load(out, chunk, 0).wait()
         has_left = (place > 0) & (place <= goal)
         has_right = (place < length - 1) & (place >= goal)
 
-        @pl.when(has_left)
+        @pl.when(~has_right & ~has_left)
+        def _():
+            add(chunk, [twin])
+
+        @pl.when(has_left & ~has_right)
         def _():
             to_right(chunk).wait_recv()
-
-        @pl.when(has_right)
+            add(chunk, [twin, left])
+
+        @pl.when(has_right & ~has_left)
         def _():
             to_left(chunk).wait_recv()
+            add(chunk, [twin, right])
 
         @pl.when(has_left & has_right)
         def _():
+            to_right(chunk).wait_recv()
+            to_left(chunk).wait_recv()
             add(chunk, [twin, left, right])
-
-        @pl.when(has_left & ~has_right)
-        def _():
-            add(chunk, [twin, left])
-
-        @pl.when(has_right & ~has_left)
-        def _():
-            add(chunk, [twin, right])
-
-        @pl.when(~has_right & ~has_left)
-        def _():
-            add(chunk, [twin])
 
         @pl.when(place < goal)
         def _():
@@ -463,8 +456,7 @@
             twin_copy(chunk, at(own, chunk)).start()
             keep(chunk).start()
 
-    def hand_back(chunk):
-        goal = root(chunk)
+    def hand_back(chunk, goal):
         here = part(out, core, chunk)
 
         @pl.when(place < goal)
@@ -487,10 +479,9 @@
 
             twin_copy(chunk, here).start()
 
-    def finish(chunk):
-        goal = root(chunk)
+    def finish(chunk, goal):
         here = part(out, core, chunk)
-        core_copy(chunk).wait_send()
+        core_copy(out, chunk, 0).wait_send()
         twin_arrival(chunk).wait_recv()
         twin_copy(chunk, here).wait_send()
 
@@ -514,31 +505,53 @@
         def _():
             keep(chunk).wait()
 
-    @pl.loop(0, count)
-    def _(chunk):
-        core_copy(chunk).start()
-        load(chunk).start()
-
+    def open_source(source, first, count):
+        @pl.loop(first, first + count)
+        def _(chunk):
+            core_copy(source, chunk, first).start()
+            load(source, chunk, first).start()
+
+    late = []
+    first = 0
+    for source, rows, before in sources:
+        count = rows // 2 // CHUNK
+        if before is None:
+            open_source(source, first, count)
+        else:
+            late.append((source, first, count, before))
+        first += count
+    pairs = first // 2
     yield
-    groups = count // 2
-    for step in range(groups + LAG):
-        if step < groups:
-
-            @pl.loop(2 * step, 2 * step + 2)
-            def _(chunk):
-                gather_up(chunk)
-
-        if step >= LAG:
-
-            @pl.loop(2 * (step - LAG), 2 * (step - LAG) + 2)
-            def _(chunk):
-                hand_back(chunk)
+    for step in range(pairs + SKEW * 2 * deepest):
+        for source, begin, count, before in late:
+            if step == max(0, begin // 2 - 2):
+                for _ in before:
+                    pass
+                open_source(source, begin, count)
+        for parity in (0, 1):
+            goal = deepest - 1 + parity
+            below = (place < goal).astype(jnp.int32)
+            above = (place > goal).astype(jnp.int32)
+            level = below * place + above * (length - 1 - place) + (1 - below - above) * deepest
+            pair = step - SKEW * level
+
+            @pl.when((pair >= 0) & (pair < pairs))
+            def _(parity=parity, goal=goal, pair=pair):
+                gather_up(2 * pair + parity, goal)
+
+            away = below * (goal - place) + above * (place - goal)
+            pair_back = step - SKEW * (deepest + away)
+
+            @pl.when((away > 0) & (pair_back >= 0) & (pair_back < pairs))
+            def _(parity=parity, goal=goal, pair_back=pair_back):
+                hand_back(2 * pair_back + parity, goal)
 
         yield
 
-    @pl.loop(0, count)
-    def _(chunk):
-        finish(chunk)
+    @pl.loop(0, pairs)
+    def _(pair):
+        finish(2 * pair, deepest - 1)
+        finish(2 * pair + 1, deepest)
 
 
 def small_scratch(size, devices, width):
@@ -550,8 +563,8 @@
     ]
 
 
-def small_sum(size, devices, given, sums, out, near, far, near_sem, far_sem):
-    def exchange(axis, members, slots, sem):
+def small_sum(size, devices, turns, given, sums, out, near, far, near_sem, far_sem):
+    def send(axis, members, slots, sem):
         me = lax.axis_index(axis)
         copies = []
         for step in range(1, members):
@@ -559,34 +572,57 @@
             copy = remote_copy(axis, target, slots.at[me], slots.at[me], sem.at[0, target], sem.at[1, me])
             copy.start()
             copies.append(copy)
+        return copies
+
+    def receive(axis, members, slots, sem, copies):
+        me = lax.axis_index(axis)
         for step in range(1, members):
             source = (me + step) % members
             remote_copy(axis, source, slots.at[source], slots.at[source], sem.at[0, source], sem.at[1, source]).wait_recv()
         for copy in copies:
             copy.wait_send()
 
+    for _ in range(turns):
+        yield True
     mine = given[0:8, :]
     row = lax.broadcasted_iota(jnp.int32, mine.shape, 0)
     mine = jnp.where(row == 0, jnp.sum(sums[0], axis=0, keepdims=True), mine)
     mine = jnp.where(row == 1, jnp.sum(sums[1], axis=0, keepdims=True), mine)
     near[lax.axis_index("tensor")] = mine
-    exchange("tensor", size, near, near_sem)
+    copies = send("tensor", size, near, near_sem)
+    yield True
+    receive("tensor", size, near, near_sem, copies)
     total = near[0]
     for member in range(1, size):
         total = total + near[member]
     me = lax.axis_index("dp")
     far[me, 0:8, :] = total
     far[me, 8:16, :] = given[8:16, :]
-    exchange("dp", devices, far, far_sem)
+    copies = send("dp", devices, far, far_sem)
+    yield False
+    yield False
+    receive("dp", devices, far, far_sem, copies)
     total = far[0]
     for member in range(1, devices):
         total = total + far[member]
     out[...] = total
 
 
-def one_after_another(*parts):
-    for part in parts:
-        yield from part
+def in_turns(*parts):
+    waiting = list(parts)
+    while waiting:
+        left = []
+        for one, quiet in waiting:
+            ended = False
+            try:
+                while not ended:
+                    ended = next(one)
+                    if not quiet:
+                        yield
+                left.append((one, quiet))
+            except StopIteration:
+                pass
+        waiting = left
 
 
 def greet_all(sizes):
@@ -602,22 +638,12 @@
     pl.semaphore_wait(barrier, total)
 
 
-def later(call):
-    call()
-    yield
-
-
 def last_kernel(size, devices, shapes, mlp, part, kv, tokens, mid, dmid, dbias, gain, small, *rest):
     wide, kv_shape, summed = shapes[0], shapes[1], shapes[2:]
-    count = len(summed)
-    arrays, rest = rest[:count], rest[count:]
-    result, grad, kv_sum, small_out, rest = *rest[:4], rest[4:]
-    outs, rest = rest[:count], rest[count:]
-    kv_out, rest = rest[0], rest[1:]
+    arrays, rest = rest[: len(summed)], rest[len(summed) :]
+    result, grad, total, small_out, kv_out, rest = *rest[:5], rest[5:]
     first, second, third, rest = rest[:6], rest[6:12], rest[12:18], rest[18:]
     tok, load_sem, sums, rest = *rest[:3], rest[3:]
-    near, rest = rest[:4], rest[4:]
-    chains = [rest[5 * place : 5 * place + 5] for place in range(count + 1)]
     greet_all((("tensor", size), ("dp", devices)))
     loads = load_rows("tensor", size, wide[0], tokens, tok, load_sem)
     sums[...] = jnp.zeros_like(sums)
@@ -634,26 +660,18 @@
     def finish_kv(total, number, here, line):
         return total.astype(jnp.bfloat16)
 
-    def small_part():
-        small_sum(size, devices, small, sums, small_out, *near)
-
+    kv_stream = stream("tensor", size, kv_shape, kv, kv_out, *third, finish_kv)
+    sources = [(array, shape[0], None) for array, shape in zip(arrays, summed)]
+    sources.append((kv_out, kv_shape[0], kv_stream))
     run_together(
         [
-            one_after_another(
-                *(
-                    chain(devices, shape, array, out, *scratch)
-                    for shape, array, out, scratch in zip(summed, arrays, outs, chains)
-                )
+            in_turns(
+                (kv_stream, True),
+                (stream("tensor", size, wide, part, grad, *second, finish_grad, loads), False),
+                (stream("tensor", size, wide, mlp, result, *first, finish_result), False),
+                (small_sum(size, devices, size.bit_length() - 1, small, sums, small_out, *rest[:4]), False),
             ),
-            one_after_another(
-                stream("tensor", size, kv_shape, kv, kv_out, *third, finish_kv),
-                chain(devices, kv_shape, kv_out, kv_sum, *chains[-1]),
-            ),
-            one_after_another(
-                stream("tensor", size, wide, part, grad, *second, finish_grad, loads),
-                later(small_part),
-            ),
-            stream("tensor", size, wide, mlp, result, *first, finish_result),
+            chain(devices, sources, total, *rest[4:]),
         ]
     )
 
@@ -662,19 +680,19 @@
     rows, width = part.shape
     unit = rows // 2 // size
     shapes = (part.shape, kv.shape) + tuple(array.shape for array in arrays)
+    lines = sum(shape[0] for shape in shapes[1:])
     low = jnp.bfloat16
-    outs = pl.pallas_call(
+    return pl.pallas_call(
         functools.partial(last_kernel, size, devices, shapes),
         out_shape=(
             jax.ShapeDtypeStruct((rows, width), low),
             jax.ShapeDtypeStruct((rows, width), low),
-            jax.ShapeDtypeStruct(kv.shape, low),
+            jax.ShapeDtypeStruct((lines, width), low),
             jax.ShapeDtypeStruct(small.shape, jnp.float32),
-            *(jax.ShapeDtypeStruct(array.shape, low) for array in arrays),
             jax.ShapeDtypeStruct(kv.shape, low),
         ),
         in_specs=[HBM] * 4 + [VMEM] * 5 + [HBM] * len(arrays),
-        out_specs=(HBM, HBM, HBM, VMEM) + (HBM,) * len(arrays) + (HBM,),
+        out_specs=(HBM, HBM, HBM, VMEM, HBM),
         scratch_shapes=stream_scratch(size, rows, width) * 2
         + stream_scratch(size, kv.shape[0], width)
         + [
@@ -683,13 +701,12 @@
             pltpu.VMEM((2, 8, width), jnp.float32),
         ]
         + small_scratch(size, devices, width)
-        + [one for shape in shapes[2:] + (kv.shape,) for one in chain_scratch(shape)],
+        + chain_scratch(lines, width),
         compiler_params=pltpu.CompilerParams(
             collective_id=3, has_side_effects=True, vmem_limit_bytes=60 * 1024 * 1024
         ),
         name="reduce_last",
-    )(mlp, part, kv, tokens, mid, dmid, dbias, gain, small, *arrays)
-    return outs[:4], outs[4 : 4 + len(arrays)]
+    )(mlp, part, kv, tokens, mid, dmid, dbias, gain, small, *arrays)[:4]
 
 
 def layer_norm(values, gain, shift):
@@ -838,7 +855,10 @@
     grad_pre = gelu_pull(grad_act.astype(wide))[0].astype(jnp.bfloat16)
     back2 = contract_cols(grad_pre, up_weight).astype(jnp.bfloat16)
     middle_low, dmid, sums2 = reduce_back(size, back2, d_out, mid, row(norm2_gain))
-    grad_up = contract_rows(hidden2, grad_pre).astype(jnp.bfloat16)
+    if up_weight.shape[1] == width:
+        grad_up = contract_rows(hidden2, grad_pre).astype(jnp.bfloat16)
+    else:
+        grad_up = contract_rows(grad_pre, hidden2).astype(jnp.bfloat16)
     grad_upbias = jnp.sum(grad_pre.astype(wide), axis=0)
     mlp_terms = jnp.dot(activated, down_weight, preferred_element_type=wide).astype(jnp.bfloat16)
 
@@ -872,7 +892,8 @@
             jnp.zeros((6, width), wide),
         ]
     )
-    (result, grad_tokens, kv_sum, small), (grad_up, grad_proj, grad_query) = reduce_last(
+    arrays = (grad_up, grad_proj, grad_query, grad_keyval)
+    result, grad_tokens, total, small = reduce_last(
         size,
         devices,
         mlp_terms,
@@ -884,8 +905,14 @@
         row(down_bias),
         row(norm1_gain),
         small,
-        (grad_up, grad_proj, grad_query),
-    )
+        arrays[:3],
+    )
+    ends = [0]
+    for array in arrays:
+        ends.append(ends[-1] + array.shape[0])
+    grad_up, grad_proj, grad_query, kv_sum = (total[low:high] for low, high in zip(ends, ends[1:]))
+    if up_weight.shape[1] != width:
+        grad_up = grad_up.T
     grad_gain1, grad_shift1, grad_gain2, grad_shift2, grad_pbias, grad_dnbias = (
         small[place] for place in range(6)
     )

time: 839 us -> 613 us (0.73)
  Pallas kernels: 589 us -> 371 us
    pallas_call x1, Pallas kernels: 440 us -> 222 us  [reduce_last(): pl.pallas_call(functools.partial(last_kernel, size, devices, shapes), out...]
    unnamed x88 -> x92, local copies, waits for them, and re-layouts: 19.3 us -> 19.2 us
  transfers between devices with their start and end apart: 1 -> 1, of which waited for: 0 -> 0; matrix products, arithmetic and copies ran while one was open for 18% -> 23% of each run, Pallas kernels for 62% -> 48%
where the time goes in v3:
time: 613 us; the launch traced here: 609 us
  Pallas kernels  371 us (61%)
  matrix products  140 us (23%)
  other arithmetic  57 us (9%)
  local copies, waits for them, and re-layouts  25.8 us (4%)
  between operations  15.8 us (3%)
    pallas_call x1, Pallas kernels, reduce_last(): pl.pallas_call(functools.partial(last_kernel, size, devices, shapes), out...  222 us
    pallas_call x1, Pallas kernels, reduce_middle(): pl.pallas_call(functools.partial(middle_kernel, size, rows, width), out_s...  75.2 us
    pallas_call x1, Pallas kernels, reduce_back(): pl.pallas_call(functools.partial(back_kernel, size, rows, width), out_sha...  73.8 us
    dot_general x5, matrix products, contract_rows(): lax.dot_general(left, right, (((0,), (0,)), ((), ())), preferred_element_...  42 us
    dot_general x5, matrix products, contract_cols(): lax.dot_general(left, right, (((1,), (1,)), ((), ())), preferred_element_...  39 us
    unnamed x92, local copies, waits for them, and re-layouts  19.2 us
    dot_general x1, matrix products, local(): jnp.dot(activated, down_weight, preferred_element_type=wide)  16.3 us
    dot_general x1, matrix products, local(): jnp.dot(hidden2, up_weight, preferred_element_type=wide)  12.6 us
  transfers between devices with their start and end apart: 1, of which 0 were waited for; matrix products, arithmetic and copies ran while one was open for 23% of the time, Pallas kernels for 48%

profile of v3, /device:TPU:0, one launch (start us, length us, event | category | flops | bytes accessed | tf_op | source)
XLA Modules:
  0.0 609.3 jit_solution(8437546005257206385)
XLA Ops:
  10.0 3.0 convert_reduce_fusion
  13.0 3.4 fusion.2
  18.3 2.4 fusion.5
  20.7 2.5 add_convert_fusion.1
  23.3 1.3 fusion.72
  26.1 2.4 broadcast_select_fusion.d_out
  28.6 1.6 fusion.66
  31.4 1.7 fusion.48
  33.6 1.6 fusion.67
  36.4 1.9 fusion.47
  38.7 4.4 convolution_convert_fusion.4.part
  43.1 75.2 %reduce_middle.1 = (bf16[1024,2048]{1,0:T(8,128)(2,1)}, f32[256,2048]{1,0:T(8,128)}) custom-call(bf16[1024,2048]{1,0:T(8,128)(2,1)} %convolution_convert_fusion.4.part, bf16[1024,2048]{1,0:T(8,128)(2,1)} %tokens.3, f32[1,2048]{1,0:T(1,128)} %bitcast.152, f32[1,2048]{1,0:T(1,128)} %bitcast.150, f32[1,2048]{1,0:T(1,128)} %bitcast.153), custom_call_target="tpu_custom_call" | custom-call | tf_op jit(solution)/shard_map/reduce_middle/pallas_call | solution.py:288
  118.3 12.6 %fusion.73 = f32[1024,2048]{1,0:T(8,128)S(1)} fusion(bf16[1024,2048]{1,0:T(8,128)(2,1)} %get-tuple-element.25, bf16[2048,2048]{1,0:T(8,128)(2,1)} %param.29), kind=kOutput, calls=%fused_computation.117 | convolution fusion | flops 8589934592 | bytes 20971520 | tf_op jit(solution)/shard_map/dot_general | solution.py:847
  130.9 3.4 copy-done.36
  134.3 12.8 %convolution_convert_fusion = bf16[2048,2048]{1,0:T(8,128)(2,1)} fusion(bf16[1024,2048]{1,0:T(8,128)(2,1)S(1)} %copy-done.4, f32[1024,2048]{1,0:T(8,128)S(1)} %fusion.73, f32[2048]{0:T(1024)S(1)} %convert_element_type.158), kind=kOutput, calls=%fused_computation.45 | convolution fusion | flops 8615100416 | bytes 20979712 | tf_op jit(solution)/shard_map/dot_general | solution.py:727
  147.2 16.3 %convolution_convert_fusion.3.mlp = bf16[1024,2048]{1,0:T(8,128)(2,1)} fusion(bf16[2048,2048]{1,0:T(8,128)(2,1)} %param.31, f32[1024,2048]{1,0:T(8,128)} %copy-done.36, f32[2048]{0:T(1024)S(1)} %convert_element_type.158), kind=kOutput, calls=%fused_computation.60 | convolution fusion | flops 8613003264 | bytes 20979712 | tf_op jit(solution)/shard_map/dot_general | solution.py:863
  163.5 20.4 %convert_reduce_fusion.1 = (f32[2048]{0:T(1024)S(1)}, bf16[1024,2048]{1,0:T(8,128)(2,1)}) fusion(bf16[1024,2048]{1,0:T(8,128)(2,1)S(1)} %copy-done.5, bf16[2048,2048]{1,0:T(8,128)(2,1)} %param.31, f32[1024,2048]{1,0:T(8,128)} %copy-done.36, f32[2048]{0:T(1024)S(1)} %convert_element_type.158), kind=kOutput, calls=%fused_computation.36 | convolution fusion | flops 8650749952 | bytes 25182208 | tf_op jit(solution)/shard_map/dot_general | solution.py:733
  183.9 14.7 %convolution_convert_fusion.1.rest_0_ = bf16[2048,2048]{1,0:T(8,128)(2,1)} fusion(bf16[1024,2048]{1,0:T(8,128)(2,1)} %get-tuple-element.25, bf16[1024,2048]{1,0:T(8,128)(2,1)} %get-tuple-element.76), kind=kOutput, calls=%fused_computation.46 | convolution fusion | flops 8594128896 | bytes 16777216 | tf_op jit(solution)/shard_map/dot_general | solution.py:727
  198.6 10.4 %convolution_convert_fusion.2.part = bf16[1024,2048]{1,0:T(8,128)(2,1)} fusion(bf16[1024,2048]{1,0:T(8,128)(2,1)S(1)} %copy-done.37, bf16[2048,2048]{1,0:T(8,128)(2,1)S(1)} %bitcast.168), kind=kOutput, calls=%fused_computation.59 | convolution fusion | flops 8592031744 | bytes 16777216 | tf_op jit(solution)/shard_map/dot_general | solution.py:733
  209.0 73.8 %reduce_back.1 = (bf16[1024,2048]{1,0:T(8,128)(2,1)}, f32[256,2048]{1,0:T(8,128)}, f32[4,8,2048]{2,1,0:T(8,128)}) custom-call(bf16[1024,2048]{1,0:T(8,128)(2,1)} %convolution_convert_fusion.2.part, bf16[1024,2048]{1,0:T(8,128)(2,1)} %broadcast_select_fusion.d_out, f32[256,2048]{1,0:T(8,128)} %get-tuple-element.26.mid, f32[1,2048]{1,0:T(1,128)} %bitcast.151), custom_call_target="tpu_custom_call" | custom-call | tf_op jit(solution)/shard_map/reduce_back/pallas_call | solution.py:327
  282.8 6.0 convolution_convert_fusion.6.rest_1_
  288.8 2.4 convolution_convert_fusion.8
  292.1 1.9 fusion.15
  294.1 2.5 fusion.17
  296.6 3.4 convolution_bitcast_fusion
  299.9 2.6 fusion.39
  302.5 1.5 fusion.41
  304.1 1.9 fusion.18
  306.0 1.6 convert_reduce_fusion.3
  307.7 2.7 fusion.20
  311.2 1.5 fusion.54
  312.9 2.4 fusion.74
  315.3 3.4 add_convert_fusion.part
  318.7 2.3 convolution_convert_fusion.7.kv
  321.9 1.3 concatenate.17.small
  323.2 6.2 %convolution_convert_fusion.5.rest_2_ = bf16[512,2048]{1,0:T(8,128)(2,1)} fusion(bf16[1024,512]{0,1:T(8,128)(2,1)} %bitcast.148, bf16[1024,2048]{1,0:T(8,128)(2,1)} %copy-done.12), kind=kOutput, calls=%fused_computation.62 | convolution fusion | flops 2148532224 | bytes 7340032 | tf_op jit(solution)/shard_map/dot_general | solution.py:727
  329.4 221.7 %reduce_last.1 = (bf16[1024,2048]{1,0:T(8,128)(2,1)}, bf16[1024,2048]{1,0:T(8,128)(2,1)}, bf16[3328,2048]{1,0:T(8,128)(2,1)}, f32[16,2048]{1,0:T(8,128)}, bf16[256,2048]{1,0:T(8,128)(2,1)}) custom-call(bf16[1024,2048]{1,0:T(8,128)(2,1)} %convolution_convert_fusion.3.mlp, bf16[1024,2048]{1,0:T(8,128)(2,1)} %add_convert_fusion.part, ...), custom_call_target="tpu_custom_call" | custom-call | tf_op jit(solution)/shard_map/reduce_last/pallas_call | solution.py:685
  551.1 1.3 slice.89
  552.4 2.8 convert_bitcast_fusion.1
  555.2 2.9 copy.52
  558.1 6.7 %slice_convert_fusion.1 = (f32[512,2048]{1,0:T(8,128)}, f32[2048,512]{0,1:T(8,128)}) fusion(bf16[3328,2048]{1,0:T(8,128)(2,1)} %get-tuple-element.33), kind=kLoop, calls=%fused_computation.66 | loop fusion | flops 2097152 | bytes 12582912 | tf_op jit(solution)/shard_map/convert_element_type | solution.py:931
  564.8 5.3 copy.51
  571.3 1.8 fusion.65
  573.1 11.7 %slice_convert_fusion = f32[2048,2048]{1,0:T(8,128)} fusion(bf16[3328,2048]{1,0:T(8,128)(2,1)} %get-tuple-element.33), kind=kLoop, calls=%fused_computation.35 | loop fusion | flops 4194304 | bytes 25165824 | tf_op jit(solution)/shard_map/convert_element_type | solution.py:935
  584.7 11.8 %convert_element_type.189 = f32[2048,2048]{1,0:T(8,128)} convert(bf16[2048,2048]{1,0:T(8,128)(2,1)} %all-reduce.4.cloned.1.call-done) | non-fusion elementwise | flops 4194304 | bytes 25165824 | tf_op jit(solution)/shard_map/convert_element_type | solution.py:937
  596.6 2.1 copy.81
  598.7 1.6 copy-done.15
  600.3 2.0 copy.82
  (124 shorter events, 12.7 us)
Async XLA Ops:
  7.2 31.5 %copy-start = (bf16[512,2048]{1,0:T(8,128)(2,1)S(1)}, bf16[512,2048]{1,0:T(8,128)(2,1)}, u32[]{:S(2)}) copy-start(bf16[512,2048]{1,0:T(8,128)(2,1)} %param.25) | copy-start | bytes 6291460
  7.2 9.2 %copy-start.26 = (bf16[2048]{0:T(1024)(128)(2,1)S(1)}, bf16[2048]{0:T(1024)(128)(2,1)}, u32[]{:S(2)}) copy-start(bf16[2048]{0:T(1024)(128)(2,1)} %param.30) | copy-start | bytes 12292
  7.2 9.2 %copy-start.27 = (bf16[2048]{0:T(1024)(128)(2,1)S(1)}, bf16[2048]{0:T(1024)(128)(2,1)}, u32[]{:S(2)}) copy-start(bf16[2048]{0:T(1024)(128)(2,1)} %param.19) | copy-start | bytes 12292
  7.2 9.2 %copy-start.28 = (bf16[2048]{0:T(1024)(128)(2,1)S(1)}, bf16[2048]{0:T(1024)(128)(2,1)}, u32[]{:S(2)}) copy-start(bf16[2048]{0:T(1024)(128)(2,1)} %param.20) | copy-start | bytes 12292
  7.2 9.3 %copy-start.29 = (bf16[2048]{0:T(1024)(128)(2,1)S(1)}, bf16[2048]{0:T(1024)(128)(2,1)}, u32[]{:S(2)}) copy-start(bf16[2048]{0:T(1024)(128)(2,1)} %param.26) | copy-start | bytes 12292
  7.2 9.9 %copy-start.30 = (bf16[2048]{0:T(1024)(128)(2,1)S(1)}, bf16[2048]{0:T(1024)(128)(2,1)}, u32[]{:S(2)}) copy-start(bf16[2048]{0:T(1024)(128)(2,1)} %param.27) | copy-start | bytes 12292
  7.2 10.5 %copy-start.31 = (bf16[2048]{0:T(1024)(128)(2,1)S(1)}, bf16[2048]{0:T(1024)(128)(2,1)}, u32[]{:S(2)}) copy-start(bf16[2048]{0:T(1024)(128)(2,1)} %param.28) | copy-start | bytes 12292
  7.3 577.5 %all-reduce.4.cloned.1.call-start = ((), (), s32[]{:S(2)}) async-start(), calls=%async_computation | async-start | bytes 16777216 | tf_op jit(solution)/shard_map/psum | solution.py:852
  7.3 11.0 %copy-start.3 = (bf16[1024,2048]{1,0:T(8,128)(2,1)S(1)}, bf16[1024,2048]{1,0:T(8,128)(2,1)}, u32[]{:S(2)}) copy-start(bf16[1024,2048]{1,0:T(8,128)(2,1)} %tokens.3) | copy-start | bytes 12582916
  10.0 10.7 %copy-start.34 = (bf16[2048,512]{1,0:T(8,128)(2,1)S(1)}, bf16[2048,512]{1,0:T(8,128)(2,1)}, u32[]{:S(2)}) copy-start(bf16[2048,512]{1,0:T(8,128)(2,1)} %param.21) | copy-start | bytes 6291460
  16.5 1.8 copy-start.25
  20.7 2.6 copy-start.12
  20.7 2.6 copy-start.20
  23.2 2.9 copy-start.14
  23.3 5.3 copy-start.19
  23.3 10.3 %copy-start.8 = (bf16[512,512]{0,1:T(8,128)(2,1)}, bf16[512,512]{0,1:T(8,128)(2,1)S(1)}, u32[]{:S(2)}) copy-start(bf16[512,512]{0,1:T(8,128)(2,1)S(1)} %get-tuple-element.54) | copy-start | bytes 1572868
  24.6 9.0 %copy-start.6 = (f32[1024,256]{1,0:T(8,128)}, f32[1024,256]{1,0:T(8,128)S(1)}, u32[]{:S(2)}) copy-start(f32[1024,256]{1,0:T(8,128)S(1)} %fusion.72) | copy-start | bytes 3145732
  28.6 263.6 %copy-start.17 = (bf16[1024,128,1]{1,0,2:T(8,128)(2,1)}, bf16[1024,128,1]{1,0,2:T(8,128)(2,1)S(1)}, u32[]{:S(2)}) copy-start(bf16[1024,128,1]{1,0,2:T(8,128)(2,1)S(1)} %fusion.59) | copy-start | bytes 786436
  30.2 3.4 copy-start.1
  35.2 3.3 copy-start.2
  118.3 16.0 %copy-start.4 = (bf16[1024,2048]{1,0:T(8,128)(2,1)S(1)}, bf16[1024,2048]{1,0:T(8,128)(2,1)}, u32[]{:S(2)}) copy-start(bf16[1024,2048]{1,0:T(8,128)(2,1)} %broadcast_select_fusion.d_out) | copy-start | bytes 12582916
  130.9 3.4 copy-start.36
  147.2 16.3 %copy-start.5 = (bf16[1024,2048]{1,0:T(8,128)(2,1)S(1)}, bf16[1024,2048]{1,0:T(8,128)(2,1)}, u32[]{:S(2)}) copy-start(bf16[1024,2048]{1,0:T(8,128)(2,1)} %broadcast_select_fusion.d_out) | copy-start | bytes 12582916
  147.2 51.3 %slice-start.4 = ((s8[8388608]{0:T(1024)(128)(4,1)}), s8[4194304]{0:T(1024)(128)(4,1)S(1)}, s32[]{:S(2)}) async-start(s8[8388608]{0:T(1024)(128)(4,1)} %bitcast.167), calls=%async_computation.5 | async-start | bytes 8388608
  163.5 35.0 %slice-start.5 = ((s8[8388608]{0:T(1024)(128)(4,1)}), s8[4194304]{0:T(1024)(128)(4,1)S(1)}, s32[]{:S(2)}) async-start(s8[8388608]{0:T(1024)(128)(4,1)} %bitcast.167), calls=%async_computation.6 | async-start | bytes 8388608
  183.9 14.7 %copy-start.37 = (bf16[1024,2048]{1,0:T(8,128)(2,1)S(1)}, bf16[1024,2048]{1,0:T(8,128)(2,1)}, u32[]{:S(2)}) copy-start(bf16[1024,2048]{1,0:T(8,128)(2,1)} %get-tuple-element.76) | copy-start | bytes 12582916
  282.8 6.0 copy-start.33
  282.8 9.3 %slice-start = ((s8[8388608]{0:T(1024)(128)(4,1)}), s8[4194304]{0:T(1024)(128)(4,1)S(1)}, s32[]{:S(2)}) async-start(s8[8388608]{0:T(1024)(128)(4,1)} %bitcast.133), calls=%async_computation.1 | async-start | bytes 8388608
  288.8 3.3 slice-start.1
  292.1 10.4 %slice-start.2 = ((s8[8388608]{0:T(1024)(128)(4,1)}), s8[4194304]{0:T(1024)(128)(4,1)S(1)}, s32[]{:S(2)}) async-start(s8[8388608]{0:T(1024)(128)(4,1)} %bitcast.135), calls=%async_computation.3 | async-start | bytes 8388608
  294.1 8.4 %slice-start.3 = ((s8[8388608]{0:T(1024)(128)(4,1)}), s8[4194304]{0:T(1024)(128)(4,1)S(1)}, s32[]{:S(2)}) async-start(s8[8388608]{0:T(1024)(128)(4,1)} %bitcast.135), calls=%async_computation.4 | async-start | bytes 8388608
  296.6 6.0 copy-start.10
  302.5 1.6 copy-start.18
  307.7 2.7 copy-start.7
  307.7 3.5 copy-start.9
  307.7 3.5 copy-start.23
  310.4 2.3 copy-start.11
  310.4 2.4 copy-start.35
  312.7 2.6 copy-start.21
  312.8 5.9 copy-start.22
  315.2 3.5 copy-start.13
  315.3 5.7 copy-start.32
  315.3 6.3 %copy-start.24 = (f32[4,8,2048]{2,1,0:T(8,128)S(1)}, f32[4,8,2048]{2,1,0:T(8,128)}, u32[]{:S(2)}) copy-start(f32[4,8,2048]{2,1,0:T(8,128)} %get-tuple-element.29) | copy-start | bytes 786436
  584.7 11.8 %copy-start.16 = (bf16[1024,2048]{1,0:T(8,128)(2,1)S(1)}, bf16[1024,2048]{1,0:T(8,128)(2,1)}, u32[]{:S(2)}) copy-start(bf16[1024,2048]{1,0:T(8,128)(2,1)} %get-tuple-element.93) | copy-start | bytes 12582916
  596.5 3.7 copy-start.15
Sparse Core Ops, SparseCore 0:
  147.3 175.7 all-reduce.3

commit v4 on v3

--- a/solution.py
+++ b/solution.py
@@ -263,11 +263,86 @@
     return values[:8] + values[8:]
 
 
+BLOCK = 256
+
+
+def block_of(index):
+    return pl.ds(pl.multiple_of(index * BLOCK, BLOCK), BLOCK)
+
+
+def plain_task(left, right, out, index):
+    @pl.loop(0, left.shape[0] // BLOCK)
+    def _(step):
+        rows = block_of(step)
+        out[rows, block_of(index)] = jnp.dot(
+            left[rows, :], right[:, block_of(index)], preferred_element_type=jnp.float32
+        ).astype(out.dtype)
+
+
+def flipped_task(left, right, out, index):
+    @pl.loop(0, left.shape[0] // BLOCK)
+    def _(step):
+        rows = block_of(step)
+        out[rows, block_of(index)] = contract_cols(left[rows, :], right[block_of(index), :]).astype(out.dtype)
+
+
+def rows_task(left, right, out, turned, index):
+    turned[...] = left[:, block_of(index)].T
+
+    @pl.loop(0, right.shape[1] // BLOCK)
+    def _(step):
+        columns = block_of(step)
+        out[block_of(index), columns] = jnp.dot(
+            turned[...], right[:, columns], preferred_element_type=jnp.float32
+        ).astype(out.dtype)
+
+
+def widen(array, start, rows):
+    width = array.shape[1]
+
+    def body(source, target):
+        target[...] = source[...].astype(jnp.float32)
+
+    return pl.pallas_call(
+        body,
+        grid=(rows // BLOCK,),
+        out_shape=jax.ShapeDtypeStruct((rows, width), jnp.float32),
+        in_specs=[pl.BlockSpec((BLOCK, width), lambda step: (step + start // BLOCK, 0))],
+        out_specs=pl.BlockSpec((BLOCK, width), lambda step: (step, 0)),
+        name="widen",
+    )(array)
+
+
+def products(sources, targets, load_sems, store_sems, jobs, early=()):
+    loads = [pltpu.make_async_copy(src, dst, load_sems.at[place]) for place, (src, dst) in enumerate(zip(sources, targets))]
+    for load in loads:
+        load.start()
+    yield
+    waited = set()
+    stores = []
+    for needs, task, out, where, index in jobs:
+        for place in needs:
+            if place not in waited:
+                waited.add(place)
+                loads[place].wait()
+        task(index)
+        held = out[0].at[block_of(index), :] if where == 0 else out[0].at[:, block_of(index)]
+        there = out[1].at[block_of(index), :] if where == 0 else out[1].at[:, block_of(index)]
+        store = pltpu.make_async_copy(held, there, store_sems.at[len(stores)])
+        store.start()
+        stores.append(store)
+        if len(stores) not in early:
+            yield
+    for store in stores:
+        store.wait()
+
+
 HBM = pl.BlockSpec(memory_space=pl.ANY)
 VMEM = pl.BlockSpec(memory_space=pltpu.VMEM)
 
 
-def middle_kernel(size, rows, width, part, tokens, pbias, gain, shift, hidden, mid, own, slots, outbuf, local_sem, send_sem, recv_sem, tok, load_sem):
+def middle_kernel(size, rows, width, part, tokens, pbias, gain, shift, d_out, down, hidden, mid, act, own, slots, outbuf, local_sem, send_sem, recv_sem, tok, load_sem, *work):
+    dout_here, down_here, act_here, in_sem, out_sem = work
     greet("tensor", size)
     loads = load_rows("tensor", size, rows, tokens, tok, load_sem)
 
@@ -277,30 +352,49 @@
         scaled, _ = moments(value)
         return (scaled * gain[...] + shift[...]).astype(jnp.bfloat16)
 
+    jobs = [
+        ((0, 1), functools.partial(flipped_task, dout_here, down_here, act_here), (act_here, act), 1, index)
+        for index in range(down.shape[0] // BLOCK)
+    ]
     run_together(
-        [stream("tensor", size, (rows, width), part, hidden, own, slots, outbuf, local_sem, send_sem, recv_sem, finish, loads)]
-    )
-
-
-def reduce_middle(size, part, tokens, pbias, gain, shift):
+        [
+            stream("tensor", size, (rows, width), part, hidden, own, slots, outbuf, local_sem, send_sem, recv_sem, finish, loads),
+            products((d_out, down), (dout_here, down_here), in_sem, out_sem, jobs),
+        ]
+    )
+
+
+def reduce_middle(size, part, tokens, pbias, gain, shift, d_out, down):
     rows, width = part.shape
+    units = down.shape[0]
     unit = rows // 2 // size
     return pl.pallas_call(
         functools.partial(middle_kernel, size, rows, width),
         out_shape=(
             jax.ShapeDtypeStruct((rows, width), jnp.bfloat16),
             jax.ShapeDtypeStruct((2 * unit, width), jnp.float32),
+            jax.ShapeDtypeStruct((rows, units), jnp.bfloat16),
         ),
-        in_specs=[HBM, HBM, VMEM, VMEM, VMEM],
-        out_specs=(HBM, VMEM),
+        in_specs=[HBM, HBM, VMEM, VMEM, VMEM, HBM, HBM],
+        out_specs=(HBM, VMEM, HBM),
         scratch_shapes=stream_scratch(size, rows, width)
-        + [pltpu.VMEM((2, unit, width), jnp.bfloat16), pltpu.SemaphoreType.DMA((2,))],
-        compiler_params=pltpu.CompilerParams(collective_id=1, has_side_effects=True),
+        + [pltpu.VMEM((2, unit, width), jnp.bfloat16), pltpu.SemaphoreType.DMA((2,))]
+        + [
+            pltpu.VMEM((rows, width), jnp.bfloat16),
+            pltpu.VMEM((units, width), jnp.bfloat16),
+            pltpu.VMEM((rows, units), jnp.bfloat16),
+            pltpu.SemaphoreType.DMA((2,)),
+            pltpu.SemaphoreType.DMA((units // BLOCK,)),
+        ],
+        compiler_params=pltpu.CompilerParams(
+            collective_id=1, has_side_effects=True, vmem_limit_bytes=60 * 1024 * 1024
+        ),
         name="reduce_middle",
-    )(part, tokens, pbias, gain, shift)
-
-
-def back_kernel(size, rows, width, part, d_out, mid, gain, low, dmid, sums, own, slots, outbuf, local_sem, send_sem, recv_sem, dout, load_sem):
+    )(part, tokens, pbias, gain, shift, d_out, down)
+
+
+def back_kernel(size, rows, width, part, d_out, mid, gain, act, down, hidden, pre, low, dmid, sums, mlp, grad_up, own, slots, outbuf, local_sem, send_sem, recv_sem, dout, load_sem, *work):
+    act_here, down_here, hidden_here, pre_here, mlp_here, up_here, turned, in_sem, out_sem = work
     greet("tensor", size)
     loads = load_rows("tensor", size, rows, d_out, dout, load_sem)
     sums[...] = jnp.zeros_like(sums)
@@ -316,13 +410,26 @@
         sums[3] += fold(direct)
         return value.astype(jnp.bfloat16)
 
+    jobs = [
+        ((0, 1), functools.partial(plain_task, act_here, down_here, mlp_here), (mlp_here, mlp), 1, index)
+        for index in range(width // BLOCK)
+    ] + [
+        ((2, 3), functools.partial(rows_task, hidden_here, pre_here, up_here, turned), (up_here, grad_up), 0, index)
+        for index in range(width // BLOCK)
+    ]
     run_together(
-        [stream("tensor", size, (rows, width), part, low, own, slots, outbuf, local_sem, send_sem, recv_sem, finish, loads)]
-    )
-
-
-def reduce_back(size, part, d_out, mid, gain):
+        [
+            stream("tensor", size, (rows, width), part, low, own, slots, outbuf, local_sem, send_sem, recv_sem, finish, loads),
+            products(
+                (act, down, hidden, pre), (act_here, down_here, hidden_here, pre_here), in_sem, out_sem, jobs, (1, 2, 4, 5, 7, 8)
+            ),
+        ]
+    )
+
+
+def reduce_back(size, part, d_out, mid, gain, act, down, hidden, pre):
     rows, width = part.shape
+    units = down.shape[0]
     unit = rows // 2 // size
     return pl.pallas_call(
         functools.partial(back_kernel, size, rows, width),
@@ -330,14 +437,29 @@
             jax.ShapeDtypeStruct((rows, width), jnp.bfloat16),
             jax.ShapeDtypeStruct((2 * unit, width), jnp.float32),
             jax.ShapeDtypeStruct((4, 8, width), jnp.float32),
+            jax.ShapeDtypeStruct((rows, width), jnp.bfloat16),
+            jax.ShapeDtypeStruct((width, units), jnp.bfloat16),
         ),
-        in_specs=[HBM, HBM, VMEM, VMEM],
-        out_specs=(HBM, VMEM, VMEM),
+        in_specs=[HBM, HBM, VMEM, VMEM, HBM, HBM, HBM, HBM],
+        out_specs=(HBM, VMEM, VMEM, HBM, HBM),
         scratch_shapes=stream_scratch(size, rows, width)
-        + [pltpu.VMEM((2, unit, width), jnp.bfloat16), pltpu.SemaphoreType.DMA((2,))],
-        compiler_params=pltpu.CompilerParams(collective_id=2, has_side_effects=True),
+        + [pltpu.VMEM((2, unit, width), jnp.bfloat16), pltpu.SemaphoreType.DMA((2,))]
+        + [
+            pltpu.VMEM((rows, units), jnp.bfloat16),
+            pltpu.VMEM((units, width), jnp.bfloat16),
+            pltpu.VMEM((rows, width), jnp.bfloat16),
+            pltpu.VMEM((rows, units), jnp.bfloat16),
+            pltpu.VMEM((rows, width), jnp.bfloat16),
+            pltpu.VMEM((width, units), jnp.bfloat16),
+            pltpu.VMEM((BLOCK, rows), jnp.bfloat16),
+            pltpu.SemaphoreType.DMA((4,)),
+            pltpu.SemaphoreType.DMA((2 * (width // BLOCK),)),
+        ],
+        compiler_params=pltpu.CompilerParams(
+            collective_id=2, has_side_effects=True, vmem_limit_bytes=60 * 1024 * 1024
+        ),
         name="reduce_back",
-    )(part, d_out, mid, gain)
+    )(part, d_out, mid, gain, act, down, hidden, pre)
 
 
 def remote_copy(axis, target, src, dst, send_sem, recv_sem):
@@ -842,25 +964,25 @@
     attended, log_totals = attend_forward(slot_queries, key_rows, value_rows, length, block_rows)
     heads_out = attended.reshape(slot_len, heads_here * head_dim).astype(jnp.bfloat16)
     attn_terms = jnp.dot(heads_out, proj_weight, preferred_element_type=wide).astype(jnp.bfloat16)
-    hidden2, mid = reduce_middle(size, attn_terms, tokens, row(proj_bias), row(norm2_gain), row(norm2_shift))
+    valid = (jnp.arange(slot_len, dtype=jnp.int32) < length)[:, None]
+    d_out = jnp.where(valid, cotangent, jnp.zeros_like(cotangent))
+    hidden2, mid, grad_act = reduce_middle(
+        size, attn_terms, tokens, row(proj_bias), row(norm2_gain), row(norm2_shift), d_out, down_weight
+    )
 
     pre_act = jnp.dot(hidden2, up_weight, preferred_element_type=wide) + up_bias.astype(wide)
     activated = gelu_tanh(pre_act).astype(jnp.bfloat16)
-    valid = (jnp.arange(slot_len, dtype=jnp.int32) < length)[:, None]
-    d_out = jnp.where(valid, cotangent, jnp.zeros_like(cotangent))
     grad_down = contract_rows(activated, d_out).astype(jnp.bfloat16)
     grad_down = lax.psum(grad_down, "dp")
-    grad_act = contract_cols(d_out, down_weight).astype(jnp.bfloat16)
     gelu_pull = jax.vjp(gelu_tanh, pre_act)[1]
     grad_pre = gelu_pull(grad_act.astype(wide))[0].astype(jnp.bfloat16)
     back2 = contract_cols(grad_pre, up_weight).astype(jnp.bfloat16)
-    middle_low, dmid, sums2 = reduce_back(size, back2, d_out, mid, row(norm2_gain))
-    if up_weight.shape[1] == width:
-        grad_up = contract_rows(hidden2, grad_pre).astype(jnp.bfloat16)
-    else:
-        grad_up = contract_rows(grad_pre, hidden2).astype(jnp.bfloat16)
+    middle_low, dmid, sums2, mlp_terms, grad_up = reduce_back(
+        size, back2, d_out, mid, row(norm2_gain), activated, down_weight, hidden2, grad_pre
+    )
+    if up_weight.shape[1] != width:
+        grad_up = grad_up.T
     grad_upbias = jnp.sum(grad_pre.astype(wide), axis=0)
-    mlp_terms = jnp.dot(activated, down_weight, preferred_element_type=wide).astype(jnp.bfloat16)
 
     grad_proj = contract_rows(heads_out, middle_low).astype(jnp.bfloat16)
     grad_heads = contract_cols(middle_low, proj_weight).astype(jnp.bfloat16)
@@ -911,6 +1033,7 @@
     for array in arrays:
         ends.append(ends[-1] + array.shape[0])
     grad_up, grad_proj, grad_query, kv_sum = (total[low:high] for low, high in zip(ends, ends[1:]))
+    grad_up = widen(total, 0, ends[1])
     if up_weight.shape[1] != width:
         grad_up = grad_up.T
     grad_gain1, grad_shift1, grad_gain2, grad_shift2, grad_pbias, grad_dnbias = (
@@ -932,9 +1055,9 @@
         grad_pbias,
         grad_gain2,
         grad_shift2,
-        grad_up.astype(wide),
+        grad_up,
         grad_upbias,
-        grad_down.astype(wide),
+        widen(grad_down, 0, grad_down.shape[0]),
         grad_dnbias,
     )
 

time: 613 us -> 591 us (0.964)
  Pallas kernels: 371 us -> 400 us
  other arithmetic: 57 us -> 33.3 us
  matrix products: 140 us -> 120 us
    convert_element_type x2 -> x0, other arithmetic: 23.5 us -> none  [the longest x1 11.8 us: local(): grad_down.astype(wide)]
    pallas_call x0 -> x2, Pallas kernels: none -> 20.5 us  [widen(): pl.pallas_call(body, grid=(rows // BLOCK,), out_shape=jax.ShapeDtypeStruc...]
    dot_general x5 -> x4, matrix products: 42 us -> 23.1 us  [contract_rows(): lax.dot_general(left, right, (((0,), (0,)), ((), ())), preferred_element_...]
    dot_general x1 -> x0, matrix products: 16.3 us -> none  [local(): jnp.dot(activated, down_weight, preferred_element_type=wide)]
    dot_general x2, matrix products: 3.57 us -> 15.9 us  [attend_forward(): jnp.einsum('hqk,kd->qhd', probability, value_rows, preferred_element_type...]
    dot_general x5 -> x4, matrix products: 39 us -> 27 us  [contract_cols(): lax.dot_general(left, right, (((1,), (1,)), ((), ())), preferred_element_...]
    dot_general x1, matrix products: 12.6 us -> 21.9 us  [local(): jnp.dot(hidden2, up_weight, preferred_element_type=wide)]
    unnamed x92 -> x84, local copies, waits for them, and re-layouts: 19.2 us -> 18.4 us
  transfers between devices with their start and end apart: 1 -> 1, of which waited for: 0 -> 0; matrix products, arithmetic and copies ran while one was open for 23% -> 15% of each run, Pallas kernels for 48% -> 53%
where the time goes in v4:
time: 591 us; the launch traced here: 593 us
  Pallas kernels  400 us (68%)
  matrix products  120 us (20%)
  other arithmetic  33.3 us (6%)
  local copies, waits for them, and re-layouts  24.1 us (4%)
  between operations  15.7 us (3%)
    pallas_call x1, Pallas kernels, reduce_last(): pl.pallas_call(functools.partial(last_kernel, size, devices, shapes), out...  226 us
    pallas_call x1, Pallas kernels, reduce_back(): pl.pallas_call(functools.partial(back_kernel, size, rows, width), out_sha...  77.9 us
    pallas_call x1, Pallas kernels, reduce_middle(): pl.pallas_call(functools.partial(middle_kernel, size, rows, width), out_s...  75.3 us
    dot_general x4, matrix products, contract_cols(): lax.dot_general(left, right, (((1,), (1,)), ((), ())), preferred_element_...  27 us
    dot_general x4, matrix products, contract_rows(): lax.dot_general(left, right, (((0,), (0,)), ((), ())), preferred_element_...  23.1 us
    dot_general x1, matrix products, local(): jnp.dot(hidden2, up_weight, preferred_element_type=wide)  21.9 us
    pallas_call x2, Pallas kernels, widen(): pl.pallas_call(body, grid=(rows // BLOCK,), out_shape=jax.ShapeDtypeStruc...  20.5 us
    unnamed x84, local copies, waits for them, and re-layouts  18.4 us
  transfers between devices with their start and end apart: 1, of which 0 were waited for; matrix products, arithmetic and copies ran while one was open for 15% of the time, Pallas kernels for 53%

profile of v4, /device:TPU:0, one launch (start us, length us, event | category | flops | bytes accessed | tf_op | source)
XLA Modules:
  0.0 592.5 jit_solution(15510769850127090055)
XLA Ops:
  8.1 1.2 convert_element_type.135
  10.0 3.0 convert_reduce_fusion
  13.0 3.4 fusion.2
  18.3 2.3 fusion.5
  20.6 2.4 add_convert_fusion.1
  23.1 1.3 fusion.73
  25.5 2.4 broadcast_select_fusion.d_out
  28.0 1.6 fusion.67
  29.6 1.2 fusion.22
  30.8 1.7 fusion.48
  33.0 1.6 fusion.68
  35.8 14.2 %fusion.47 = bf16[512,4,128]{0,2,1:T(8,128)(2,1)S(1)} fusion(bf16[1024,128,1]{1,0,2:T(8,128)(2,1)S(1)} %fusion.59, f32[4,512,1024]{1,2,0:T(8,128)S(1)} %get-tuple-element.77, f32[4,512]{1,0:T(4,128)S(1)} %fusion.21, f32[4,512]{1,0:T(4,128)S(1)} %get-tuple-element.76), kind=kOutput, calls=%fused_computation.83 | convolution fusion | flops 543424512 | bytes 9191424 | tf_op jit(solution)/shard_map/hqk,kd->qhd/dot_general | solution.py:883
  51.2 4.4 convolution_convert_fusion.2.part
  55.6 75.3 %reduce_middle.1 = (bf16[1024,2048]{1,0:T(8,128)(2,1)}, f32[256,2048]{1,0:T(8,128)}, bf16[1024,2048]{1,0:T(8,128)(2,1)}) custom-call(bf16[1024,2048]{1,0:T(8,128)(2,1)} %convolution_convert_fusion.2.part, bf16[1024,2048]{1,0:T(8,128)(2,1)} %tokens.3, f32[1,2048]{1,0:T(1,128)} %bitcast.149, f32[1,2048]{1,0:T(1,128)} %bitcast.146, f32[1,2048]{1,0:T(1,128)} %bitcast.150, ...), custom_call_target="tpu_custom_call" | custom-call | tf_op jit(solution)/shard_map/reduce_middle/pallas_call | solution.py:371
  130.9 21.9 %convert_reduce_fusion.1 = (f32[2048]{0:T(1024)S(1)}, bf16[1024,2048]{1,0:T(8,128)(2,1)}, bf16[1024,2048]{1,0:T(8,128)(2,1)S(1)}) fusion(bf16[1024,2048]{1,0:T(8,128)(2,1)} %get-tuple-element.29, f32[2048]{0:T(1024)S(1)} %convert_element_type.143, bf16[1024,2048]{1,0:T(8,128)(2,1)} %get-tuple-element.28.hidden, bf16[2048,2048]{1,0:T(8,128)(2,1)} %param.29), kind=kOutput, calls=%fused_computation.35 | convolution fusion | flops 8652847104 | bytes 25182208 | tf_op jit(solution)/shard_map/dot_general | solution.py:973
  152.8 2.0 copy-done.10
  154.8 11.2 %convolution_convert_fusion = bf16[2048,2048]{1,0:T(8,128)(2,1)} fusion(bf16[1024,2048]{1,0:T(8,128)(2,1)S(1)} %get-tuple-element.60.act, bf16[1024,2048]{1,0:T(8,128)(2,1)S(1)} %copy-done.6), kind=kOutput, calls=%fused_computation.44 | convolution fusion | flops 8594128896 | bytes 16777216 | tf_op jit(solution)/shard_map/dot_general | solution.py:849
  166.1 14.3 %convolution_convert_fusion.1.part = bf16[1024,2048]{1,0:T(8,128)(2,1)} fusion(bf16[1024,2048]{1,0:T(8,128)(2,1)} %get-tuple-element.57.pre, bf16[2048,2048]{1,0:T(8,128)(2,1)} %param.29), kind=kOutput, calls=%fused_computation.57 | convolution fusion | flops 8592031744 | bytes 16777216 | tf_op jit(solution)/shard_map/dot_general | solution.py:855
  180.3 77.9 %reduce_back.1 = (bf16[1024,2048]{1,0:T(8,128)(2,1)}, f32[256,2048]{1,0:T(8,128)}, f32[4,8,2048]{2,1,0:T(8,128)}, bf16[1024,2048]{1,0:T(8,128)(2,1)}, bf16[2048,2048]{1,0:T(8,128)(2,1)}) custom-call(bf16[1024,2048]{1,0:T(8,128)(2,1)} %convolution_convert_fusion.1.part, bf16[1024,2048]{1,0:T(8,128)(2,1)} %broadcast_select_fusion.d_out, ...), custom_call_target="tpu_custom_call" | custom-call | tf_op jit(solution)/shard_map/reduce_back/pallas_call | solution.py:434
  258.2 4.9 convolution_convert_fusion.6
  263.3 5.3 fusion.15
  268.6 2.5 fusion.17
  271.1 3.3 convolution_bitcast_fusion
  274.4 1.5 fusion.39
  275.9 2.3 fusion.41
  278.3 1.9 fusion.18
  280.2 2.6 fusion.20
  283.9 1.3 pad_maximum_fusion.1
  285.8 1.6 convert_reduce_fusion.3
  287.6 3.7 fusion.54
  291.3 4.6 convolution_convert_fusion.5.kv
  295.9 1.3 concatenate.17.small
  297.2 4.4 fusion.74
  301.6 3.4 add_convert_fusion.part
  305.1 3.7 convolution_convert_fusion.4.rest_1_
  308.7 3.7 convolution_convert_fusion.3.rest_2_
  312.4 226.0 %reduce_last.1 = (bf16[1024,2048]{1,0:T(8,128)(2,1)}, bf16[1024,2048]{1,0:T(8,128)(2,1)}, bf16[3328,2048]{1,0:T(8,128)(2,1)}, f32[16,2048]{1,0:T(8,128)}, bf16[256,2048]{1,0:T(8,128)(2,1)}) custom-call(bf16[1024,2048]{1,0:T(8,128)(2,1)} %get-tuple-element.31.mlp, bf16[1024,2048]{1,0:T(8,128)(2,1)} %add_convert_fusion.part, ...), custom_call_target="tpu_custom_call" | custom-call | tf_op jit(solution)/shard_map/reduce_last/pallas_call | solution.py:807
  538.4 1.3 slice.86
  539.7 10.3 %widen.2 = f32[2048,2048]{1,0:T(8,128)} custom-call(bf16[3328,2048]{1,0:T(8,128)(2,1)} %get-tuple-element.39.source), custom_call_target="tpu_custom_call" | custom-call | tf_op jit(solution)/shard_map/widen/pallas_call | solution.py:306
  550.0 1.5 convert_bitcast_fusion.1
  551.5 1.8 copy.52
  553.3 6.7 %slice_convert_fusion = (f32[512,2048]{1,0:T(8,128)}, f32[2048,512]{0,1:T(8,128)}) fusion(bf16[3328,2048]{1,0:T(8,128)(2,1)} %get-tuple-element.39.source), kind=kLoop, calls=%fused_computation.63 | loop fusion | flops 2097152 | bytes 12582912 | tf_op jit(solution)/shard_map/convert_element_type | solution.py:1054
  560.0 5.3 copy.51
  565.3 1.2 slice_bitcast_fusion
  566.5 1.8 fusion.66
  568.3 10.3 %widen.3 = f32[2048,2048]{1,0:T(8,128)} custom-call(bf16[2048,2048]{1,0:T(8,128)(2,1)} %all-reduce.4.cloned.1.call-done.source), custom_call_target="tpu_custom_call" | custom-call | tf_op jit(solution)/shard_map/widen/pallas_call | solution.py:306
  578.5 4.9 copy.81
  583.5 2.0 copy.82
  (112 shorter events, 8.6 us)
Async XLA Ops:
  7.2 44.0 %copy-start = (bf16[512,2048]{1,0:T(8,128)(2,1)S(1)}, bf16[512,2048]{1,0:T(8,128)(2,1)}, u32[]{:S(2)}) copy-start(bf16[512,2048]{1,0:T(8,128)(2,1)} %param.25) | copy-start | bytes 6291460
  7.2 9.2 %copy-start.27 = (bf16[2048]{0:T(1024)(128)(2,1)S(1)}, bf16[2048]{0:T(1024)(128)(2,1)}, u32[]{:S(2)}) copy-start(bf16[2048]{0:T(1024)(128)(2,1)} %param.19) | copy-start | bytes 12292
  7.2 9.2 %copy-start.28 = (bf16[2048]{0:T(1024)(128)(2,1)S(1)}, bf16[2048]{0:T(1024)(128)(2,1)}, u32[]{:S(2)}) copy-start(bf16[2048]{0:T(1024)(128)(2,1)} %param.20) | copy-start | bytes 12292
  7.2 9.3 %copy-start.29 = (bf16[2048]{0:T(1024)(128)(2,1)S(1)}, bf16[2048]{0:T(1024)(128)(2,1)}, u32[]{:S(2)}) copy-start(bf16[2048]{0:T(1024)(128)(2,1)} %param.26) | copy-start | bytes 12292
  7.2 9.9 %copy-start.30 = (bf16[2048]{0:T(1024)(128)(2,1)S(1)}, bf16[2048]{0:T(1024)(128)(2,1)}, u32[]{:S(2)}) copy-start(bf16[2048]{0:T(1024)(128)(2,1)} %param.27) | copy-start | bytes 12292
  7.2 10.4 %copy-start.31 = (bf16[2048]{0:T(1024)(128)(2,1)S(1)}, bf16[2048]{0:T(1024)(128)(2,1)}, u32[]{:S(2)}) copy-start(bf16[2048]{0:T(1024)(128)(2,1)} %param.28) | copy-start | bytes 12292
  7.2 11.0 %copy-start.32 = (bf16[2048]{0:T(1024)(128)(2,1)S(1)}, bf16[2048]{0:T(1024)(128)(2,1)}, u32[]{:S(2)}) copy-start(bf16[2048]{0:T(1024)(128)(2,1)} %param.30) | copy-start | bytes 12292
  7.3 561.0 %all-reduce.4.cloned.1.call-start = ((), (), s32[]{:S(2)}) async-start(), calls=%async_computation | async-start | bytes 16777216 | tf_op jit(solution)/shard_map/psum | solution.py:976
  7.3 11.0 %copy-start.4 = (bf16[1024,2048]{1,0:T(8,128)(2,1)S(1)}, bf16[1024,2048]{1,0:T(8,128)(2,1)}, u32[]{:S(2)}) copy-start(bf16[1024,2048]{1,0:T(8,128)(2,1)} %tokens.3) | copy-start | bytes 12582916
  10.0 10.5 %copy-start.35 = (bf16[2048,512]{1,0:T(8,128)(2,1)S(1)}, bf16[2048,512]{1,0:T(8,128)(2,1)}, u32[]{:S(2)}) copy-start(bf16[2048,512]{1,0:T(8,128)(2,1)} %param.21) | copy-start | bytes 6291460
  16.4 1.9 copy-start.26
  20.6 2.5 copy-start.11
  20.6 2.5 copy-start.19
  23.0 2.5 copy-start.13
  23.1 4.8 copy-start.18
  24.4 8.6 %copy-start.7 = (f32[1024,256]{1,0:T(8,128)}, f32[1024,256]{1,0:T(8,128)S(1)}, u32[]{:S(2)}) copy-start(f32[1024,256]{1,0:T(8,128)S(1)} %fusion.73) | copy-start | bytes 3145732
  27.9 235.4 %copy-start.16 = (bf16[1024,128,1]{1,0,2:T(8,128)(2,1)}, bf16[1024,128,1]{1,0,2:T(8,128)(2,1)S(1)}, u32[]{:S(2)}) copy-start(bf16[1024,128,1]{1,0,2:T(8,128)(2,1)S(1)} %fusion.59) | copy-start | bytes 786436
  29.6 3.4 copy-start.2
  34.6 15.4 %copy-start.3 = (f32[4,512,1024]{1,2,0:T(8,128)}, f32[4,512,1024]{1,2,0:T(8,128)S(1)}, u32[]{:S(2)}) copy-start(f32[4,512,1024]{1,2,0:T(8,128)S(1)} %get-tuple-element.77) | copy-start | bytes 25165828
  50.1 1.0 copy-start.21
  130.9 23.9 %copy-start.6 = (bf16[1024,2048]{1,0:T(8,128)(2,1)S(1)}, bf16[1024,2048]{1,0:T(8,128)(2,1)}, u32[]{:S(2)}) copy-start(bf16[1024,2048]{1,0:T(8,128)(2,1)} %broadcast_select_fusion.d_out) | copy-start | bytes 12582916
  152.8 2.0 copy-start.10
  258.2 10.3 %slice-start = ((s8[8388608]{0:T(1024)(128)(4,1)}), s8[4194304]{0:T(1024)(128)(4,1)S(1)}, s32[]{:S(2)}) async-start(s8[8388608]{0:T(1024)(128)(4,1)} %bitcast.129), calls=%async_computation.1 | async-start | bytes 8388608
  263.2 5.4 slice-start.1
  263.3 12.6 %slice-start.2 = ((s8[8388608]{0:T(1024)(128)(4,1)}), s8[4194304]{0:T(1024)(128)(4,1)S(1)}, s32[]{:S(2)}) async-start(s8[8388608]{0:T(1024)(128)(4,1)} %bitcast.131), calls=%async_computation.3 | async-start | bytes 8388608
  268.6 5.8 copy-start.8
  268.6 7.3 %slice-start.3 = ((s8[8388608]{0:T(1024)(128)(4,1)}), s8[4194304]{0:T(1024)(128)(4,1)S(1)}, s32[]{:S(2)}) async-start(s8[8388608]{0:T(1024)(128)(4,1)} %bitcast.131), calls=%async_computation.4 | async-start | bytes 8388608
  275.9 2.4 copy-start.17
  280.2 3.4 copy-start.9
  282.9 4.6 copy-start.5
  282.9 2.3 copy-start.33
  282.9 2.9 copy-start.15
  285.2 2.3 copy-start.25
  285.8 1.8 copy-start.24
  291.3 10.3 %copy-start.20 = (bf16[2048,256]{1,0:T(8,128)(2,1)S(1)}, bf16[2048,256]{1,0:T(8,128)(2,1)}, u32[]{:S(2)}) copy-start(bf16[2048,256]{1,0:T(8,128)(2,1)} %param.23) | copy-start | bytes 3145732
  301.6 3.4 copy-start.22
  301.6 3.4 copy-start.34
  305.0 3.7 copy-start.12
  305.0 3.7 copy-start.23
  578.5 4.9 copy-start.14
  578.5 7.0 %copy-start.1 = (bf16[512,2048]{1,0:T(8,128)(2,1)S(1)}, bf16[512,2048]{1,0:T(8,128)(2,1)}, u32[]{:S(2)}) copy-start(bf16[512,2048]{1,0:T(8,128)(2,1)} %param.25) | copy-start | bytes 6291460
Sparse Core Ops, SparseCore 0:
  166.1 187.0 all-reduce.3

commit v5 on v4

--- a/solution.py
+++ b/solution.py
@@ -172,9 +172,11 @@
                         copy.start()
                         sends.append(copy)
                 yield path == paths[-1] and sub == subs - 1
-    for level in reversed(range(depth)):
-        paths = suffixes(depth - 1 - level)
-        for path in paths:
+    order = [(level, path) for level in reversed(range(depth)) for path in suffixes(depth - 1 - level)]
+    direct = [(level, path) for level, path in order if not any(path)]
+    passed = [(level, path) for level, path in order if any(path)]
+    for group in (direct, passed):
+        for level, path in group:
             full = (0,) * level + (1,) + path
             sender = (0,) * (level + 1) + path
             for sub in range(subs):
@@ -184,7 +186,7 @@
                         copy = gather_copy(tree, back, full, sub)
                         copy.start()
                         sends.append(copy)
-                yield path == paths[-1] and sub == subs - 1
+                yield (level, path) == group[-1] and sub == subs - 1
     for copy in sends:
         copy.wait_send()
     for copy in stored:
@@ -474,7 +476,7 @@
 
 
 CHUNK = 32
-SKEW = 1
+SKEW = 2
 CORE_SEND, CORE_RECV, UP_SEND, LEFT_RECV, RIGHT_RECV, BACK_LEFT, BACK_RIGHT, BACK_RECV, TWIN_SEND, TWIN_RECV, KEEP, LOAD = range(12)
 
 

time: 591 us -> 582 us (0.985)
  matrix products: 120 us -> 108 us
    dot_general x2, matrix products: 15.9 us -> 3.79 us  [attend_forward(): jnp.einsum('hqk,kd->qhd', probability, value_rows, preferred_element_type...]
  transfers between devices with their start and end apart: 1 -> 1, of which waited for: 0 -> 0; matrix products, arithmetic and copies ran while one was open for 15% -> 15% of each run, Pallas kernels for 53% -> 54%
where the time goes in v5:
time: 582 us; the launch traced here: 578 us
  Pallas kernels  397 us (68%)
  matrix products  108 us (19%)
  other arithmetic  33.3 us (6%)
  local copies, waits for them, and re-layouts  24.3 us (4%)
  between operations  15.7 us (3%)
    pallas_call x1, Pallas kernels, reduce_last(): pl.pallas_call(functools.partial(last_kernel, size, devices, shapes), out...  227 us
    pallas_call x1, Pallas kernels, reduce_middle(): pl.pallas_call(functools.partial(middle_kernel, size, rows, width), out_s...  75.3 us
    pallas_call x1, Pallas kernels, reduce_back(): pl.pallas_call(functools.partial(back_kernel, size, rows, width), out_sha...  74.2 us
    dot_general x4, matrix products, contract_cols(): lax.dot_general(left, right, (((1,), (1,)), ((), ())), preferred_element_...  26.5 us
    dot_general x4, matrix products, contract_rows(): lax.dot_general(left, right, (((0,), (0,)), ((), ())), preferred_element_...  23.1 us
    dot_general x1, matrix products, local(): jnp.dot(hidden2, up_weight, preferred_element_type=wide)  21.9 us
    pallas_call x2, Pallas kernels, widen(): pl.pallas_call(body, grid=(rows // BLOCK,), out_shape=jax.ShapeDtypeStruc...  20.5 us
    unnamed x84, local copies, waits for them, and re-layouts  18.5 us
  transfers between devices with their start and end apart: 1, of which 0 were waited for; matrix products, arithmetic and copies ran while one was open for 15% of the time, Pallas kernels for 54%

profile of v5, /device:TPU:0, one launch (start us, length us, event | category | flops | bytes accessed | tf_op | source)
XLA Modules:
  0.0 577.8 jit_solution(2120213804825050228)
XLA Ops:
  8.1 1.2 convert_element_type.135
  10.0 3.0 convert_reduce_fusion
  13.0 3.4 fusion.2
  18.3 2.1 fusion.5
  20.4 2.4 add_convert_fusion.1
  22.9 1.3 fusion.73
  25.3 2.4 broadcast_select_fusion.d_out
  27.8 1.6 fusion.67
  29.4 1.2 fusion.22
  30.6 1.7 fusion.48
  32.8 1.6 fusion.68
  35.6 2.1 fusion.47
  39.0 4.4 convolution_convert_fusion.2.part
  43.4 75.3 %reduce_middle.1 = (bf16[1024,2048]{1,0:T(8,128)(2,1)}, f32[256,2048]{1,0:T(8,128)}, bf16[1024,2048]{1,0:T(8,128)(2,1)}) custom-call(bf16[1024,2048]{1,0:T(8,128)(2,1)} %convolution_convert_fusion.2.part, bf16[1024,2048]{1,0:T(8,128)(2,1)} %tokens.3, f32[1,2048]{1,0:T(1,128)} %bitcast.149, f32[1,2048]{1,0:T(1,128)} %bitcast.146, f32[1,2048]{1,0:T(1,128)} %bitcast.150, ...), custom_call_target="tpu_custom_call" | custom-call | tf_op jit(solution)/shard_map/reduce_middle/pallas_call | solution.py:373
  118.7 21.9 %convert_reduce_fusion.1 = (f32[2048]{0:T(1024)S(1)}, bf16[1024,2048]{1,0:T(8,128)(2,1)}, bf16[1024,2048]{1,0:T(8,128)(2,1)S(1)}) fusion(bf16[1024,2048]{1,0:T(8,128)(2,1)} %get-tuple-element.29, f32[2048]{0:T(1024)S(1)} %convert_element_type.143, bf16[1024,2048]{1,0:T(8,128)(2,1)} %get-tuple-element.28.hidden, bf16[2048,2048]{1,0:T(8,128)(2,1)} %param.29), kind=kOutput, calls=%fused_computation.35 | convolution fusion | flops 8652847104 | bytes 25182208 | tf_op jit(solution)/shard_map/dot_general | solution.py:975
  140.6 2.0 copy-done.10
  142.6 11.2 %convolution_convert_fusion = bf16[2048,2048]{1,0:T(8,128)(2,1)} fusion(bf16[1024,2048]{1,0:T(8,128)(2,1)S(1)} %get-tuple-element.60.act, bf16[1024,2048]{1,0:T(8,128)(2,1)S(1)} %copy-done.6), kind=kOutput, calls=%fused_computation.44 | convolution fusion | flops 8594128896 | bytes 16777216 | tf_op jit(solution)/shard_map/dot_general | solution.py:851
  153.8 14.0 %convolution_convert_fusion.1.part = bf16[1024,2048]{1,0:T(8,128)(2,1)} fusion(bf16[1024,2048]{1,0:T(8,128)(2,1)} %get-tuple-element.57.pre, bf16[2048,2048]{1,0:T(8,128)(2,1)} %param.29), kind=kOutput, calls=%fused_computation.57 | convolution fusion | flops 8592031744 | bytes 16777216 | tf_op jit(solution)/shard_map/dot_general | solution.py:857
  167.9 74.2 %reduce_back.1 = (bf16[1024,2048]{1,0:T(8,128)(2,1)}, f32[256,2048]{1,0:T(8,128)}, f32[4,8,2048]{2,1,0:T(8,128)}, bf16[1024,2048]{1,0:T(8,128)(2,1)}, bf16[2048,2048]{1,0:T(8,128)(2,1)}) custom-call(bf16[1024,2048]{1,0:T(8,128)(2,1)} %convolution_convert_fusion.1.part, bf16[1024,2048]{1,0:T(8,128)(2,1)} %broadcast_select_fusion.d_out, ...), custom_call_target="tpu_custom_call" | custom-call | tf_op jit(solution)/shard_map/reduce_back/pallas_call | solution.py:436
  242.1 4.7 convolution_convert_fusion.6
  246.9 6.0 %fusion.15 = (f32[4,512]{1,0:T(4,128)S(1)}, f32[1024,512,4]{1,0,2:T(8,128)S(1)}) fusion(f32[4,512,1024]{1,2,0:T(8,128)} %copy-done.2, f32[4,512]{1,0:T(4,128)S(1)} %log_add_fusion, bf16[1024,128,1]{1,0,2:T(8,128)(2,1)S(1)} %fusion.59, bf16[512,4,128]{0,2,1:T(8,128)(2,1)S(1)} %bitcast.135), kind=kOutput, calls=%fused_computation.25 | convolution fusion | flops 543160320 | bytes 17580032 | tf_op jit(solution)/shard_map/qhd,kd->hqk/dot_general | solution.py:900
  253.0 2.5 fusion.17
  255.5 3.3 convolution_bitcast_fusion
  258.8 1.5 fusion.39
  260.3 2.3 fusion.41
  262.7 1.9 fusion.18
  264.6 2.8 fusion.20
  268.5 1.3 pad_maximum_fusion.1
  270.4 1.6 convert_reduce_fusion.3
  272.2 3.7 fusion.54
  275.9 4.6 convolution_convert_fusion.5.kv
  280.5 1.3 concatenate.17.small
  281.8 4.4 fusion.74
  286.2 3.4 add_convert_fusion.part
  289.6 3.7 convolution_convert_fusion.4.rest_1_
  293.3 3.7 convolution_convert_fusion.3.rest_2_
  297.0 226.7 %reduce_last.1 = (bf16[1024,2048]{1,0:T(8,128)(2,1)}, bf16[1024,2048]{1,0:T(8,128)(2,1)}, bf16[3328,2048]{1,0:T(8,128)(2,1)}, f32[16,2048]{1,0:T(8,128)}, bf16[256,2048]{1,0:T(8,128)(2,1)}) custom-call(bf16[1024,2048]{1,0:T(8,128)(2,1)} %get-tuple-element.31.mlp, bf16[1024,2048]{1,0:T(8,128)(2,1)} %add_convert_fusion.part, ...), custom_call_target="tpu_custom_call" | custom-call | tf_op jit(solution)/shard_map/reduce_last/pallas_call | solution.py:809
  523.7 1.3 slice.86
  525.0 10.3 %widen.2 = f32[2048,2048]{1,0:T(8,128)} custom-call(bf16[3328,2048]{1,0:T(8,128)(2,1)} %get-tuple-element.39.source), custom_call_target="tpu_custom_call" | custom-call | tf_op jit(solution)/shard_map/widen/pallas_call | solution.py:308
  535.3 1.5 convert_bitcast_fusion.1
  536.7 1.8 copy.52
  538.5 6.7 %slice_convert_fusion = (f32[512,2048]{1,0:T(8,128)}, f32[2048,512]{0,1:T(8,128)}) fusion(bf16[3328,2048]{1,0:T(8,128)(2,1)} %get-tuple-element.39.source), kind=kLoop, calls=%fused_computation.63 | loop fusion | flops 2097152 | bytes 12582912 | tf_op jit(solution)/shard_map/convert_element_type | solution.py:1056
  545.2 5.3 copy.51
  550.6 1.2 slice_bitcast_fusion
  551.7 1.8 fusion.66
  553.5 10.3 %widen.3 = f32[2048,2048]{1,0:T(8,128)} custom-call(bf16[2048,2048]{1,0:T(8,128)(2,1)} %all-reduce.4.cloned.1.call-done.source), custom_call_target="tpu_custom_call" | custom-call | tf_op jit(solution)/shard_map/widen/pallas_call | solution.py:308
  563.8 4.9 copy.81
  568.7 2.0 copy.82
  (112 shorter events, 8.7 us)
Async XLA Ops:
  7.2 31.8 %copy-start = (bf16[512,2048]{1,0:T(8,128)(2,1)S(1)}, bf16[512,2048]{1,0:T(8,128)(2,1)}, u32[]{:S(2)}) copy-start(bf16[512,2048]{1,0:T(8,128)(2,1)} %param.25) | copy-start | bytes 6291460
  7.2 9.2 %copy-start.27 = (bf16[2048]{0:T(1024)(128)(2,1)S(1)}, bf16[2048]{0:T(1024)(128)(2,1)}, u32[]{:S(2)}) copy-start(bf16[2048]{0:T(1024)(128)(2,1)} %param.19) | copy-start | bytes 12292
  7.2 9.2 %copy-start.28 = (bf16[2048]{0:T(1024)(128)(2,1)S(1)}, bf16[2048]{0:T(1024)(128)(2,1)}, u32[]{:S(2)}) copy-start(bf16[2048]{0:T(1024)(128)(2,1)} %param.20) | copy-start | bytes 12292
  7.2 9.3 %copy-start.29 = (bf16[2048]{0:T(1024)(128)(2,1)S(1)}, bf16[2048]{0:T(1024)(128)(2,1)}, u32[]{:S(2)}) copy-start(bf16[2048]{0:T(1024)(128)(2,1)} %param.26) | copy-start | bytes 12292
  7.2 9.9 %copy-start.30 = (bf16[2048]{0:T(1024)(128)(2,1)S(1)}, bf16[2048]{0:T(1024)(128)(2,1)}, u32[]{:S(2)}) copy-start(bf16[2048]{0:T(1024)(128)(2,1)} %param.27) | copy-start | bytes 12292
  7.2 10.4 %copy-start.31 = (bf16[2048]{0:T(1024)(128)(2,1)S(1)}, bf16[2048]{0:T(1024)(128)(2,1)}, u32[]{:S(2)}) copy-start(bf16[2048]{0:T(1024)(128)(2,1)} %param.28) | copy-start | bytes 12292
  7.2 11.0 %copy-start.32 = (bf16[2048]{0:T(1024)(128)(2,1)S(1)}, bf16[2048]{0:T(1024)(128)(2,1)}, u32[]{:S(2)}) copy-start(bf16[2048]{0:T(1024)(128)(2,1)} %param.30) | copy-start | bytes 12292
  7.3 546.2 %all-reduce.4.cloned.1.call-start = ((), (), s32[]{:S(2)}) async-start(), calls=%async_computation | async-start | bytes 16777216 | tf_op jit(solution)/shard_map/psum | solution.py:978
  7.3 11.0 %copy-start.4 = (bf16[1024,2048]{1,0:T(8,128)(2,1)S(1)}, bf16[1024,2048]{1,0:T(8,128)(2,1)}, u32[]{:S(2)}) copy-start(bf16[1024,2048]{1,0:T(8,128)(2,1)} %tokens.3) | copy-start | bytes 12582916
  10.0 10.3 %copy-start.35 = (bf16[2048,512]{1,0:T(8,128)(2,1)S(1)}, bf16[2048,512]{1,0:T(8,128)(2,1)}, u32[]{:S(2)}) copy-start(bf16[2048,512]{1,0:T(8,128)(2,1)} %param.21) | copy-start | bytes 6291460
  16.4 1.9 copy-start.26
  20.4 2.5 copy-start.11
  20.4 2.5 copy-start.19
  22.8 2.5 copy-start.13
  22.9 4.8 copy-start.18
  24.2 8.6 %copy-start.7 = (f32[1024,256]{1,0:T(8,128)}, f32[1024,256]{1,0:T(8,128)S(1)}, u32[]{:S(2)}) copy-start(f32[1024,256]{1,0:T(8,128)S(1)} %fusion.73) | copy-start | bytes 3145732
  27.7 219.2 %copy-start.16 = (bf16[1024,128,1]{1,0,2:T(8,128)(2,1)}, bf16[1024,128,1]{1,0,2:T(8,128)(2,1)S(1)}, u32[]{:S(2)}) copy-start(bf16[1024,128,1]{1,0,2:T(8,128)(2,1)S(1)} %fusion.59) | copy-start | bytes 786436
  29.4 3.4 copy-start.2
  34.4 3.4 copy-start.3
  37.9 1.0 copy-start.21
  118.7 23.9 %copy-start.6 = (bf16[1024,2048]{1,0:T(8,128)(2,1)S(1)}, bf16[1024,2048]{1,0:T(8,128)(2,1)}, u32[]{:S(2)}) copy-start(bf16[1024,2048]{1,0:T(8,128)(2,1)} %broadcast_select_fusion.d_out) | copy-start | bytes 12582916
  140.6 2.0 copy-start.10
  242.1 10.9 %slice-start = ((s8[8388608]{0:T(1024)(128)(4,1)}), s8[4194304]{0:T(1024)(128)(4,1)S(1)}, s32[]{:S(2)}) async-start(s8[8388608]{0:T(1024)(128)(4,1)} %bitcast.129), calls=%async_computation.1 | async-start | bytes 8388608
  246.8 6.2 %slice-start.1 = ((s8[8388608]{0:T(1024)(128)(4,1)}), s8[4194304]{0:T(1024)(128)(4,1)S(1)}, s32[]{:S(2)}) async-start(s8[8388608]{0:T(1024)(128)(4,1)} %bitcast.129), calls=%async_computation.2 | async-start | bytes 8388608
  246.9 13.4 %slice-start.2 = ((s8[8388608]{0:T(1024)(128)(4,1)}), s8[4194304]{0:T(1024)(128)(4,1)S(1)}, s32[]{:S(2)}) async-start(s8[8388608]{0:T(1024)(128)(4,1)} %bitcast.131), calls=%async_computation.3 | async-start | bytes 8388608
  253.0 5.8 %copy-start.8 = (f32[1024,256]{1,0:T(8,128)S(1)}, f32[1024,256]{1,0:T(8,128)}, u32[]{:S(2)}) copy-start(f32[1024,256]{1,0:T(8,128)} %copy-done.7) | copy-start | bytes 3145732
  253.0 7.3 %slice-start.3 = ((s8[8388608]{0:T(1024)(128)(4,1)}), s8[4194304]{0:T(1024)(128)(4,1)S(1)}, s32[]{:S(2)}) async-start(s8[8388608]{0:T(1024)(128)(4,1)} %bitcast.131), calls=%async_computation.4 | async-start | bytes 8388608
  260.3 2.4 copy-start.17
  264.6 3.6 copy-start.9
  267.5 4.6 copy-start.5
  267.5 2.3 copy-start.33
  267.5 2.9 copy-start.15
  269.8 2.3 copy-start.25
  270.4 1.8 copy-start.24
  275.9 10.3 %copy-start.20 = (bf16[2048,256]{1,0:T(8,128)(2,1)S(1)}, bf16[2048,256]{1,0:T(8,128)(2,1)}, u32[]{:S(2)}) copy-start(bf16[2048,256]{1,0:T(8,128)(2,1)} %param.23) | copy-start | bytes 3145732
  286.2 3.4 copy-start.22
  286.2 3.4 copy-start.34
  289.6 3.7 copy-start.12
  289.6 3.7 copy-start.23
  563.8 4.9 copy-start.14
  563.8 7.0 %copy-start.1 = (bf16[512,2048]{1,0:T(8,128)(2,1)S(1)}, bf16[512,2048]{1,0:T(8,128)(2,1)}, u32[]{:S(2)}) copy-start(bf16[512,2048]{1,0:T(8,128)(2,1)} %param.25) | copy-start | bytes 6291460
Sparse Core Ops, SparseCore 0:
  153.9 190.3 all-reduce.3
